TPU v7x, 512 devices: a whole 4x8x8 slice. The times are simulated.
512 devices in a mesh: tile: 32 (over z, y_hi), col: 16 (over x, y_lo, core).
Axes of the slice: x: 4, y: 8 (y_hi: 4, y_lo: 2; y = y_hi * 2 + y_lo), z: 8, core: 2. Of those that a mesh axis runs over, the one named last changes fastest.
Arguments:
- latent: bfloat16 [32, 17, 4, 64, 256], P('tile', None, None, 'col'), may hold values from -20 to 20
- intersections: int32 [32], P('tile'), may hold values from 0 to 4, as said below
- norm_gain_one: float32 [256], replicated, may hold values from 0.5 to 1.5
- norm_shift_one: float32 [256], replicated, may hold values from -3 to 3
- weight_one: bfloat16 [3, 3, 3, 256, 256], P(None, None, None, 'col'), may hold values from -0.078125 to 0.078125
- norm_gain_two: float32 [256], replicated, may hold values from 0.5 to 1.5
- norm_shift_two: float32 [256], replicated, may hold values from -3 to 3
- weight_two: bfloat16 [3, 3, 3, 256, 256], P(None, None, None, 'col'), may hold values from -0.078125 to 0.078125
- conv_bias: float32 [256], replicated, may hold values from -1.8 to 1.8
Outputs:
- blended: bfloat16 [32, 17, 4, 64, 256], P('tile', None, None, 'col')
Inputs may be any that keep to these rules, and one draw needn't show every extreme that they name: intersections[0] is 0 and every other entry is 1 to 4; some entry equals 4.
All inputs are finite; a program needn't handle non-finite values.
Results may differ from a plain program's by a relative error of at most 0.0055.
Values may be sent and summed in bfloat16 or wider, within the bound.
No kernel may reach another device: no remote copies, remote signals or barrier semaphores. Data moves between devices by JAX's collectives and lax.ppermute only.
A program may use at most 64 MiB of HBM per device.

v0:
```python
import jax
import jax.numpy as jnp
from jax import lax
from jax.sharding import PartitionSpec as P

GROUPS = 32
OVMAX = 4


epsilon = 1e-06


def copy_for_each(array, axis):
    copies = jnp.broadcast_to(array, (lax.axis_size(axis), *array.shape))
    return lax.all_to_all(copies, axis, split_axis=0, concat_axis=0, tiled=True)


def over_copies(array, axis):
    return copy_for_each(array, axis).sum(axis=0)


def together(arrays, axis):
    flat, at, gathered = (jnp.concatenate([a.reshape(-1) for a in arrays]), 0, [])
    so_far = over_copies(flat, axis)
    for a in arrays:
        gathered.append(so_far[at : at + a.size].reshape(a.shape))
        at += a.size
    return tuple(gathered)


def extended_2(array, sides, width):
    for axis, dim in sides:
        size, length = (lax.axis_size(axis), array.shape[dim])
        up = [(i, (i + 1) % size) for i in range(size - 1)]
        down = [(j, i) for i, j in up]
        last = lax.slice_in_dim(array, length - width, length, axis=dim)
        first = lax.slice_in_dim(array, 0, width, axis=dim)
        before = lax.ppermute(last, axis, up)
        after = lax.ppermute(first, axis, down)
        array = jnp.concatenate([before, array, after], axis=dim)
    return array


def shifted(block, axis, distance):
    devices = range(lax.axis_size(axis))
    route = [(i - distance, i) for i in devices if i - distance in devices]
    return lax.ppermute(block, axis, route)


def conv_taps(padded, kernel):
    frames = padded.shape[0]
    height = padded.shape[1]
    out_width = padded.shape[2] - 2
    channels = padded.shape[3]
    outputs = kernel.shape[4]
    padded = jnp.pad(padded, ((2, 0), (1, 1), (0, 0), (0, 0)))
    running = jnp.zeros((frames * height * out_width, outputs), jnp.float32)
    for tap_t in range(3):
        for tap_h in range(3):
            for tap_w in range(3):
                window = padded[
                    tap_t : tap_t + frames, tap_h : tap_h + height, tap_w : tap_w + out_width
                ]
                running = running + jnp.dot(
                    window.reshape(-1, channels),
                    kernel[tap_t, tap_h, tap_w],
                    preferred_element_type=jnp.float32,
                )
    return running.reshape(frames, height, out_width, outputs)


def group_total(values, per_group):
    return jnp.sum(values, axis=(0, 1, 2)).reshape(GROUPS, per_group).sum(axis=1)


def norm_silu(values, inner, gain, shift):
    channels = values.shape[3]
    per_group = channels // GROUPS
    members = inner.shape[0] * inner.shape[1] * inner.shape[2] * lax.axis_size("col") * per_group
    chan_sums = group_total(inner, per_group)
    chan_squares = group_total(inner * inner, per_group)
    totals, squares = together((chan_sums, chan_squares), "col")
    group_mean = totals / members
    spread = jnp.maximum(squares / members - group_mean * group_mean, 0.0)
    inv_std = lax.rsqrt(spread + epsilon)
    normed = (values - jnp.repeat(group_mean, per_group)) * jnp.repeat(
        inv_std, per_group
    ) * gain + shift
    return jax.nn.silu(normed).astype(jnp.bfloat16)


def shards(
    latent,
    intersections,
    norm_gain_one,
    norm_shift_one,
    weight_one,
    norm_gain_two,
    norm_shift_two,
    weight_two,
    conv_bias,
):
    source = latent[0]
    latent_full = source.astype(jnp.float32)
    act_one = norm_silu(latent_full, latent_full, norm_gain_one, norm_shift_one)
    kernel_one, kernel_two = (
        lax.all_gather(weight_one, "col", axis=3, tiled=True),
        lax.all_gather(weight_two, "col", axis=3, tiled=True),
    )
    margin = extended_2(act_one, (("col", 2),), 2)
    hidden = conv_taps(margin, kernel=kernel_one).astype(jnp.bfloat16)
    hidden_full = hidden.astype(jnp.float32)
    act_two = norm_silu(hidden_full, hidden_full[:, :, 1:-1], norm_gain_two, norm_shift_two)
    own_width = source.shape[2]
    position = lax.axis_index("col") * own_width - 1 + jnp.arange(own_width + 2, dtype=jnp.int32)
    inside = (position >= 0) & (position < own_width * lax.axis_size("col"))
    act_two = jnp.where(inside[None, None, :, None], act_two, jnp.zeros_like(act_two))
    branch = conv_taps(act_two, kernel=kernel_two)
    decoded = (latent_full + (branch + conv_bias)).astype(jnp.bfloat16)
    frames = decoded.shape[0]
    received = shifted(decoded[frames - OVMAX :], "tile", 1)
    shared = intersections[0]
    extended = jnp.concatenate([received, jnp.zeros_like(received)], axis=0)
    aligned = lax.dynamic_slice_in_dim(extended, OVMAX - shared, OVMAX, 0)
    position_t = jnp.arange(OVMAX, dtype=jnp.int32)
    own_share = ((position_t + 1).astype(jnp.float32) / (shared + 1).astype(jnp.float32))[
        :, None, None, None
    ]
    head = decoded[:OVMAX].astype(jnp.float32)
    active = (position_t < shared)[:, None, None, None]
    mixed = jnp.where(
        active, own_share * head + (1.0 - own_share) * aligned.astype(jnp.float32), head
    )
    blended = jnp.concatenate([mixed.astype(jnp.bfloat16), decoded[OVMAX:]], axis=0)
    return blended[None]


def solution(mesh):
    in_specs = (
        P("tile", None, None, "col", None),
        P("tile"),
        P(),
        P(),
        P(None, None, None, "col", None),
        P(),
        P(),
        P(None, None, None, "col", None),
        P(),
    )
    out_specs = P("tile", None, None, "col", None)
    return jax.shard_map(shards, mesh=mesh, in_specs=in_specs, out_specs=out_specs, check_vma=False)
```

profile of v0, /device:TPU:64, one launch (start us, length us, event | category | flops | bytes accessed | tf_op | source)
XLA Modules:
  0.0 126.9 jit_solution(7533719370882032942)
XLA Ops:
  10.4 5.4 %all-to-all-start = ((f32[16,1,64]{2,1,0:T(1,128)}), f32[16,1,64]{2,1,0:T(1,128)S(1)}, u32[]{:S(2)}, u32[]{:S(2)}) async-start(f32[16,1,64]{2,1,0:T(1,128)} %broadcast_in_dim.51), calls=%async_computation | async-start | bytes 16384 | tf_op jit(solution)/shard_map/all_to_all | solution.py:15
  17.2 4.6 %all-to-all-done = f32[16,1,64]{2,1,0:T(1,128)S(1)} async-done(((f32[16,1,64]{2,1,0:T(1,128)}), f32[16,1,64]{2,1,0:T(1,128)S(1)}, u32[]{:S(2)}, u32[]{:S(2)}) %all-to-all-start) | async-done | bytes 4128 | tf_op jit(solution)/shard_map/all_to_all | solution.py:15
  23.5 1.8 %collective-permute-start = (bf16[17,4,2,256]{3,2,1,0:T(2,128)(2,1)S(1)}, bf16[17,4,2,256]{3,2,1,0:T(2,128)(2,1)S(1)}, u32[]{:S(2)}, u32[]{:S(2)}) collective-permute-start(bf16[17,4,2,256]{3,2,1,0:T(2,128)(2,1)S(1)} %get-tuple-element.61), channel_id=1, source_target_pairs={{0,1},{1,2},{2,3},{3,4},{4,5},{5,6},{6,7},{7,8},{8,9},{9,10},{10,1... | collective-permute-start | bytes 208904 | tf_op jit(solution)/shard_map/ppermute | solution.py:38
  27.1 1.7 %collective-permute-done.1 = bf16[17,4,2,256]{3,2,1,0:T(2,128)(2,1)S(1)} collective-permute-done((bf16[17,4,2,256]{3,2,1,0:T(2,128)(2,1)S(1)}, bf16[17,4,2,256]{3,2,1,0:T(2,128)(2,1)S(1)}, u32[]{:S(2)}, u32[]{:S(2)}) %collective-permute-start.1) | collective-permute-done | bytes 69664 | tf_op jit(solution)/shard_map/ppermute | solution.py:39
  29.4 2.0 %pad_slice_fusion.24 = (bf16[17,4,6,256]{3,2,1,0:T(8,128)(2,1)S(1)}, bf16[17,4,6,256]{3,2,1,0:T(8,128)(2,1)}, bf16[17,4,6,256]{3,2,1,0:T(8,128)(2,1)}, bf16[17,4...) fusion(bf16[17,4,8,256]{3,2,1,0:T(8,128)(2,1)S(1)} %pad_maximum, ...), kind=kLoop, calls=%fused_computation.24 | loop fusion | bytes 4247552 | tf_op jit(solution)/shard_map/slice | solution.py:61
  31.7 1.7 %reshape.223 = bf16[408,256]{1,0:T(8,128)(2,1)} reshape(bf16[17,4,6,256]{3,2,1,0:T(8,128)(2,1)} %get-tuple-element.35) | data formatting | bytes 417792 | tf_op jit(solution)/shard_map/reshape | solution.py:65
  34.2 1.7 %reshape.224 = bf16[408,256]{1,0:T(8,128)(2,1)} reshape(bf16[17,4,6,256]{3,2,1,0:T(8,128)(2,1)} %get-tuple-element.36) | data formatting | bytes 417792 | tf_op jit(solution)/shard_map/reshape | solution.py:65
  36.0 1.7 %reshape.225 = bf16[408,256]{1,0:T(8,128)(2,1)} reshape(bf16[17,4,6,256]{3,2,1,0:T(8,128)(2,1)} %get-tuple-element.37) | data formatting | bytes 417792 | tf_op jit(solution)/shard_map/reshape | solution.py:65
  37.7 1.7 %reshape.226 = bf16[408,256]{1,0:T(8,128)(2,1)} reshape(bf16[17,4,6,256]{3,2,1,0:T(8,128)(2,1)} %get-tuple-element.38) | data formatting | bytes 417792 | tf_op jit(solution)/shard_map/reshape | solution.py:65
  39.4 1.7 %reshape.227 = bf16[408,256]{1,0:T(8,128)(2,1)} reshape(bf16[17,4,6,256]{3,2,1,0:T(8,128)(2,1)} %get-tuple-element.39) | data formatting | bytes 417792 | tf_op jit(solution)/shard_map/reshape | solution.py:65
  41.1 1.7 %reshape.228 = bf16[408,256]{1,0:T(8,128)(2,1)} reshape(bf16[17,4,6,256]{3,2,1,0:T(8,128)(2,1)} %get-tuple-element.40) | data formatting | bytes 417792 | tf_op jit(solution)/shard_map/reshape | solution.py:65
  42.8 1.7 %reshape.229 = bf16[408,256]{1,0:T(8,128)(2,1)} reshape(bf16[17,4,6,256]{3,2,1,0:T(8,128)(2,1)} %get-tuple-element.41) | data formatting | bytes 417792 | tf_op jit(solution)/shard_map/reshape | solution.py:65
  44.6 1.7 %reshape.230 = bf16[408,256]{1,0:T(8,128)(2,1)} reshape(bf16[17,4,6,256]{3,2,1,0:T(8,128)(2,1)} %get-tuple-element.42) | data formatting | bytes 417792 | tf_op jit(solution)/shard_map/reshape | solution.py:65
  46.3 1.7 %reshape.231 = bf16[408,256]{1,0:T(8,128)(2,1)} reshape(bf16[17,4,6,256]{3,2,1,0:T(8,128)(2,1)} %get-tuple-element.43) | data formatting | bytes 417792 | tf_op jit(solution)/shard_map/reshape | solution.py:65
  48.0 1.7 %reshape.232 = bf16[408,256]{1,0:T(8,128)(2,1)} reshape(bf16[17,4,6,256]{3,2,1,0:T(8,128)(2,1)} %get-tuple-element.44) | data formatting | bytes 417792 | tf_op jit(solution)/shard_map/reshape | solution.py:65
  49.7 1.7 %reshape.233 = bf16[408,256]{1,0:T(8,128)(2,1)} reshape(bf16[17,4,6,256]{3,2,1,0:T(8,128)(2,1)} %get-tuple-element.45) | data formatting | bytes 417792 | tf_op jit(solution)/shard_map/reshape | solution.py:65
  51.5 1.7 %reshape.234 = bf16[408,256]{1,0:T(8,128)(2,1)} reshape(bf16[17,4,6,256]{3,2,1,0:T(8,128)(2,1)} %get-tuple-element.46) | data formatting | bytes 417792 | tf_op jit(solution)/shard_map/reshape | solution.py:65
  57.3 1.4 %fusion.17 = f32[408,256]{1,0:T(8,128)S(1)} fusion(bf16[408,256]{1,0:T(8,128)(2,1)} %reshape.223, bf16[3,3,3,256,256]{4,3,2,1,0:T(8,128)(2,1)} %all-gather.3.cloned.1.call-done), kind=kOutput, calls=%fused_computation.178 | convolution fusion | flops 53477376 | bytes 757760 | tf_op jit(solution)/shard_map/dot_general | solution.py:64
  70.3 8.9 %all-to-all-start.1 = ((f32[16,1,64]{2,1,0:T(1,128)}), f32[16,1,64]{2,1,0:T(1,128)S(1)}, u32[]{:S(2)}, u32[]{:S(2)}) async-start(f32[16,1,64]{2,1,0:T(1,128)} %broadcast_in_dim.54), calls=%async_computation.1 | async-start | bytes 16384 | tf_op jit(solution)/shard_map/all_to_all | solution.py:15
  79.2 6.0 %all-to-all-done.1 = f32[16,1,64]{2,1,0:T(1,128)S(1)} async-done(((f32[16,1,64]{2,1,0:T(1,128)}), f32[16,1,64]{2,1,0:T(1,128)S(1)}, u32[]{:S(2)}, u32[]{:S(2)}) %all-to-all-start.1) | async-done | bytes 4128 | tf_op jit(solution)/shard_map/all_to_all | solution.py:15
  93.7 5.8 %all-gather.5.cloned.1.call-done = bf16[3,3,3,256,256]{4,3,2,1,0:T(8,128)(2,1)} async-done(((bf16[3,3,3,16,256]{4,3,2,1,0:T(8,128)(2,1)}), bf16[3,3,3,256,256]{4,3,2,1,0:T(8,128)(2,1)}) %all-gather.5.cloned.1.call-update) | async-done | bytes 3538960 | tf_op jit(solution)/shard_map/all_gather | solution.py:108
  99.5 1.3 %fusion.14 = f32[272,256]{1,0:T(8,128)S(1)} fusion(bf16[272,256]{1,0:T(8,128)(2,1)} %reshape.251, bf16[3,3,3,256,256]{4,3,2,1,0:T(8,128)(2,1)} %all-gather.5.cloned.1.call-done), kind=kOutput, calls=%fused_computation.149 | convolution fusion | flops 35651584 | bytes 548864 | tf_op jit(solution)/shard_map/dot_general | solution.py:64
  110.0 4.3 %collective-permute-start.2 = (bf16[4,4,4,256]{3,2,1,0:T(4,128)(2,1)S(1)}, bf16[4,4,4,256]{3,2,1,0:T(4,128)(2,1)S(1)}, u32[]{:S(2)}, u32[]{:S(2)}) collective-permute-start(bf16[4,4,4,256]{3,2,1,0:T(4,128)(2,1)S(1)} %slice.536), channel_id=1, source_target_pairs={{0,16},{16,32},{32,48},{48,64},{64,80},{80,96},{96,112},{112,128},... | collective-permute-start | bytes 98312 | tf_op jit(solution)/shard_map/ppermute | solution.py:47
  114.4 4.8 %collective-permute-done.2 = bf16[4,4,4,256]{3,2,1,0:T(4,128)(2,1)S(1)} collective-permute-done((bf16[4,4,4,256]{3,2,1,0:T(4,128)(2,1)S(1)}, bf16[4,4,4,256]{3,2,1,0:T(4,128)(2,1)S(1)}, u32[]{:S(2)}, u32[]{:S(2)}) %collective-permute-start.2) | collective-permute-done | bytes 32800 | tf_op jit(solution)/shard_map/ppermute | solution.py:47
  (194 shorter events, 43.3 us)
Async XLA Ops:
  6.5 50.8 %all-gather.3.cloned.1.call-start = ((), (), s32[]{:S(2)}) async-start(), calls=%async_computation.2 | async-start | bytes 3760128 | tf_op jit(solution)/shard_map/all_gather | solution.py:107
  10.4 11.4 %all-to-all-start = ((f32[16,1,64]{2,1,0:T(1,128)}), f32[16,1,64]{2,1,0:T(1,128)S(1)}, u32[]{:S(2)}, u32[]{:S(2)}) async-start(f32[16,1,64]{2,1,0:T(1,128)} %broadcast_in_dim.51), calls=%async_computation | async-start | bytes 16384 | tf_op jit(solution)/shard_map/all_to_all | solution.py:15
  15.8 83.7 %all-gather.5.cloned.1.call-start = ((), (), s32[]{:S(2)}) async-start(), calls=%async_computation.3 | async-start | bytes 3760128 | tf_op jit(solution)/shard_map/all_gather | solution.py:108
  23.5 3.6 %collective-permute-start = (bf16[17,4,2,256]{3,2,1,0:T(2,128)(2,1)S(1)}, bf16[17,4,2,256]{3,2,1,0:T(2,128)(2,1)S(1)}, u32[]{:S(2)}, u32[]{:S(2)}) collective-permute-start(bf16[17,4,2,256]{3,2,1,0:T(2,128)(2,1)S(1)} %get-tuple-element.61), channel_id=1, source_target_pairs={{0,1},{1,2},{2,3},{3,4},{4,5},{5,6},{6,7},{7,8},{8,9},{9,10},{10,1... | collective-permute-start | bytes 208904 | tf_op jit(solution)/shard_map/ppermute | solution.py:38
  25.3 3.5 %collective-permute-start.1 = (bf16[17,4,2,256]{3,2,1,0:T(2,128)(2,1)S(1)}, bf16[17,4,2,256]{3,2,1,0:T(2,128)(2,1)S(1)}, u32[]{:S(2)}, u32[]{:S(2)}) collective-permute-start(bf16[17,4,2,256]{3,2,1,0:T(2,128)(2,1)S(1)} %get-tuple-element.62), channel_id=1, source_target_pairs={{1,0},{2,1},{3,2},{4,3},{5,4},{6,5},{7,6},{8,7},{9,8},{10,9},{11,1... | collective-permute-start | bytes 208904 | tf_op jit(solution)/shard_map/ppermute | solution.py:39
  34.2 18.9 %copy-start.3 = (bf16[17,4,6,256]{3,2,1,0:T(8,128)(2,1)S(1)}, bf16[17,4,6,256]{3,2,1,0:T(8,128)(2,1)}, u32[]{:S(2)}) copy-start(bf16[17,4,6,256]{3,2,1,0:T(8,128)(2,1)} %get-tuple-element.47) | copy-start | bytes 626692
  57.1 6.9 %copy-start.14 = (bf16[408,256]{1,0:T(8,128)(2,1)S(1)}, bf16[408,256]{1,0:T(8,128)(2,1)}, u32[]{:S(2)}) copy-start(bf16[408,256]{1,0:T(8,128)(2,1)} %reshape.226) | copy-start | bytes 626692
  57.3 6.9 %copy-start.13 = (bf16[408,256]{1,0:T(8,128)(2,1)S(1)}, bf16[408,256]{1,0:T(8,128)(2,1)}, u32[]{:S(2)}) copy-start(bf16[408,256]{1,0:T(8,128)(2,1)} %reshape.227) | copy-start | bytes 626692
  57.3 5.2 %copy-start.1 = (bf16[3,3,3,256,256]{4,3,2,1,0:T(8,128)(2,1)S(1)}, bf16[3,3,3,256,256]{4,3,2,1,0:T(8,128)(2,1)}, u32[]{:S(2)}) copy-start(bf16[3,3,3,256,256]{4,3,2,1,0:T(8,128)(2,1)} %all-gather.3.cloned.1.call-done) | copy-start | bytes 10616836
  57.3 6.4 %copy-start.15 = (bf16[408,256]{1,0:T(8,128)(2,1)S(1)}, bf16[408,256]{1,0:T(8,128)(2,1)}, u32[]{:S(2)}) copy-start(bf16[408,256]{1,0:T(8,128)(2,1)} %reshape.246) | copy-start | bytes 626692
  58.7 5.7 %copy-start.12 = (bf16[408,256]{1,0:T(8,128)(2,1)S(1)}, bf16[408,256]{1,0:T(8,128)(2,1)}, u32[]{:S(2)}) copy-start(bf16[408,256]{1,0:T(8,128)(2,1)} %reshape.228) | copy-start | bytes 626692
  61.2 3.5 %copy-start.11 = (bf16[408,256]{1,0:T(8,128)(2,1)S(1)}, bf16[408,256]{1,0:T(8,128)(2,1)}, u32[]{:S(2)}) copy-start(bf16[408,256]{1,0:T(8,128)(2,1)} %reshape.229) | copy-start | bytes 626692
  62.5 2.4 %copy-start.10 = (bf16[408,256]{1,0:T(8,128)(2,1)S(1)}, bf16[408,256]{1,0:T(8,128)(2,1)}, u32[]{:S(2)}) copy-start(bf16[408,256]{1,0:T(8,128)(2,1)} %reshape.230) | copy-start | bytes 626692
  64.0 1.5 %copy-start.8 = (bf16[408,256]{1,0:T(8,128)(2,1)S(1)}, bf16[408,256]{1,0:T(8,128)(2,1)}, u32[]{:S(2)}) copy-start(bf16[408,256]{1,0:T(8,128)(2,1)} %reshape.232) | copy-start | bytes 626692
  68.0 17.6 %copy-start.20 = (f32[256]{0:T(256)S(1)}, f32[256]{0:T(256)}, u32[]{:S(2)}) copy-start(f32[256]{0:T(256)} %param.15) | copy-start | bytes 3076
  68.0 17.6 %copy-start.21 = (f32[256]{0:T(256)S(1)}, f32[256]{0:T(256)}, u32[]{:S(2)}) copy-start(f32[256]{0:T(256)} %param.14) | copy-start | bytes 3076
  70.3 14.9 %all-to-all-start.1 = ((f32[16,1,64]{2,1,0:T(1,128)}), f32[16,1,64]{2,1,0:T(1,128)S(1)}, u32[]{:S(2)}, u32[]{:S(2)}) async-start(f32[16,1,64]{2,1,0:T(1,128)} %broadcast_in_dim.54), calls=%async_computation.1 | async-start | bytes 16384 | tf_op jit(solution)/shard_map/all_to_all | solution.py:15
  87.9 4.6 %copy-start.17 = (bf16[17,4,4,256]{3,2,1,0:T(4,128)(2,1)S(1)}, bf16[17,4,4,256]{3,2,1,0:T(4,128)(2,1)}, u32[]{:S(2)}) copy-start(bf16[17,4,4,256]{3,2,1,0:T(4,128)(2,1)} %get-tuple-element.32) | copy-start | bytes 417796
  87.9 4.7 %copy-start.16 = (bf16[17,4,4,256]{3,2,1,0:T(4,128)(2,1)S(1)}, bf16[17,4,4,256]{3,2,1,0:T(4,128)(2,1)}, u32[]{:S(2)}) copy-start(bf16[17,4,4,256]{3,2,1,0:T(4,128)(2,1)} %get-tuple-element.31) | copy-start | bytes 417796
  99.5 5.9 %copy-start = (bf16[3,3,3,256,256]{4,3,2,1,0:T(8,128)(2,1)S(1)}, bf16[3,3,3,256,256]{4,3,2,1,0:T(8,128)(2,1)}, u32[]{:S(2)}) copy-start(bf16[3,3,3,256,256]{4,3,2,1,0:T(8,128)(2,1)} %all-gather.5.cloned.1.call-done) | copy-start | bytes 10616836
  108.2 1.7 %copy-start.2 = (bf16[1,17,4,4,256]{4,3,2,1,0:T(4,128)(2,1)S(1)}, bf16[1,17,4,4,256]{4,3,2,1,0:T(4,128)(2,1)}, u32[]{:S(2)}) copy-start(bf16[1,17,4,4,256]{4,3,2,1,0:T(4,128)(2,1)} %param.9) | copy-start | bytes 417796
  108.2 1.7 %copy-start.22 = (f32[256]{0:T(256)S(1)}, f32[256]{0:T(256)}, u32[]{:S(2)}) copy-start(f32[256]{0:T(256)} %param.17) | copy-start | bytes 3076
  108.4 10.8 %copy-start.23 = (f32[4]{0:T(128)S(1)}, f32[4]{0:T(128)}, u32[]{:S(2)}) copy-start(f32[4]{0:T(128)} %get-tuple-element.68) | copy-start | bytes 52
  110.0 9.2 %collective-permute-start.2 = (bf16[4,4,4,256]{3,2,1,0:T(4,128)(2,1)S(1)}, bf16[4,4,4,256]{3,2,1,0:T(4,128)(2,1)S(1)}, u32[]{:S(2)}, u32[]{:S(2)}) collective-permute-start(bf16[4,4,4,256]{3,2,1,0:T(4,128)(2,1)S(1)} %slice.536), channel_id=1, source_target_pairs={{0,16},{16,32},{32,48},{48,64},{64,80},{80,96},{96,112},{112,128},... | collective-permute-start | bytes 98312 | tf_op jit(solution)/shard_map/ppermute | solution.py:47
  (7 other events, 9.1 us)
Sparse Core Ops, SparseCore 0:
  9.4 46.1 all-gather.2
  57.7 41.7 all-gather.4
where the time goes:
time: 128 us; the launch traced here: 127 us
  local copies, waits for them, and re-layouts  38.3 us (30%)
  waiting for transfers between devices  24.2 us (19%)
  starting transfers between devices  21.7 us (17%)
  matrix products  21.3 us (17%)
  between operations  15.1 us (12%)
  other arithmetic  6.35 us (5%)
    reshape x54, local copies, waits for them, and re-layouts, conv_taps(): window.reshape(-1, channels)  31 us
    dot_general x54, matrix products, conv_taps(): jnp.dot(window.reshape(-1, channels), kernel[tap_t, tap_h, tap_w], prefer...  21.3 us
    all_to_all x2, starting transfers between devices, copy_for_each(): return lax.all_to_all(copies, axis, split_axis=0, concat_axis=0, tiled=True)  14.3 us
    all_to_all x2, waiting for transfers between devices, copy_for_each(): return lax.all_to_all(copies, axis, split_axis=0, concat_axis=0, tiled=True)  10.6 us
    all_gather x1, waiting for transfers between devices, shards(): lax.all_gather(weight_two, 'col', axis=3, tiled=True)  5.76 us
    ppermute x1, waiting for transfers between devices, shifted(): return lax.ppermute(block, axis, route)  4.79 us
    slice x4, local copies, waits for them, and re-layouts, conv_taps(): padded[tap_t:tap_t + frames, tap_h:tap_h + height, tap_w:tap_w + out_width]  4.33 us
    ppermute x1, starting transfers between devices, shifted(): return lax.ppermute(block, axis, route)  4.3 us
  transfers between devices with their start and end apart: 7, of which 5 were waited for; matrix products, arithmetic and copies ran while one was open for 43% of the time, Pallas kernels for 0%

commit v1 on v0

v1 whole, which is shorter than its diff:
```python
import jax
import jax.numpy as jnp
from jax import lax
from jax.experimental import pallas as pl
from jax.experimental.pallas import tpu as pltpu
from jax.sharding import Mesh
from jax.sharding import PartitionSpec as P

GROUPS = 32
OVMAX = 4
epsilon = 1e-06
F32, BF16 = jnp.float32, jnp.bfloat16

COL = ("x", "yl", "core")
JAX_ = ("yl", "core")
TILE = ("z", "yh")
T, H, W, C = 17, 4, 64, 256
ROW = 24
PARAMS = pltpu.CompilerParams(vmem_limit_bytes=48 * 1024 * 1024)


def whole():
    return pl.BlockSpec(memory_space=pltpu.VMEM)


def call(kernel, inputs, out_shape, scratch=(), cost=None):
    return pl.pallas_call(
        kernel,
        out_shape=out_shape,
        in_specs=[whole()] * len(inputs),
        out_specs=jax.tree.map(lambda _: whole(), out_shape),
        scratch_shapes=list(scratch),
        compiler_params=PARAMS,
        cost_estimate=cost,
    )(*inputs)


def cost(us):
    return pl.CostEstimate(flops=int(us * 4e8), bytes_accessed=1 << 20, transcendentals=0)


def lanes(shape):
    return lax.broadcasted_iota(jnp.int32, shape, len(shape) - 1)


def rows(shape):
    return lax.broadcasted_iota(jnp.int32, shape, len(shape) - 2)


def split3(value):
    high = value.astype(BF16)
    rest = value - high.astype(F32)
    middle = rest.astype(BF16)
    return high, middle, (rest - middle.astype(F32)).astype(BF16)


def group_sum(value):
    lane, width = lanes(value.shape), value.shape[1]
    for k in (1, 2, 4):
        up, down = pltpu.roll(value, k, 1), pltpu.roll(value, width - k, 1)
        value = value + jnp.where((lane & k) != 0, up, down)
    return value


def group_stats(total, squares):
    members = T * H * W * (C // GROUPS)
    mean = group_sum(total) / members
    spread = jnp.maximum(group_sum(squares) / members - mean * mean, 0.0)
    return mean, lax.rsqrt(spread + epsilon)


def silu(v):
    return v * (0.5 * jnp.tanh(0.5 * v) + 0.5)


def pack_kernel(w_ref, out_ref):
    row, col = rows((C, C)), lanes((C, C))
    source = 64 * ((col // 16) % 4) + 16 * (col // 64) + col % 16
    swapped = col ^ 64
    other = 64 * ((swapped // 16) % 4) + 16 * (swapped // 64) + swapped % 16
    left = lanes((16, 128)) < 64
    w = w_ref[...].reshape(27 * 16, C)
    same = jnp.dot(w, (row == source).astype(BF16), preferred_element_type=F32)
    swap = jnp.dot(w, (row == other).astype(BF16), preferred_element_type=F32)

    def block(array, k, dw, j):
        dt, dh = k % 3, k // 3
        at = ((dt * 3 + dh) * 3 + dw) * 16
        return array[at : at + 16, 128 * (j // 2) : 128 * (j // 2) + 128]

    for j in range(4):
        first, second = (same, swap) if j % 2 == 0 else (swap, same)
        for m in range(14):
            if m < 9:
                a, b = block(first, m, 0, j), block(second, m, 1, j)
            else:
                a = block(first, m - 9, 2, j)
                b = block(second, m - 4, 2, j) if m < 13 else jnp.zeros((16, 128), F32)
            tile = jnp.where(left, a, b).astype(BF16)
            for x in range(4):
                out_ref[4 * x + j, m] = tile


def edge_kernel(l_ref, out_ref):
    me = lax.axis_index("x")
    total, squares = jnp.zeros((4, C), F32), jnp.zeros((4, C), F32)
    for q in range(4):
        v = l_ref[q].astype(F32)
        total += jnp.sum(v, axis=(0, 1))
        squares += jnp.sum(v * v, axis=(0, 1))
    total = jnp.sum(total, axis=0, keepdims=True)
    squares = jnp.sum(squares, axis=0, keepdims=True)
    zero = jnp.zeros((1, C), F32)
    for half, value in ((0, total), (1, squares)):
        pieces = [p.astype(F32) for p in split3(value)]
        slab = jnp.concatenate(pieces + [zero], axis=0).astype(BF16)
        for d in range(4):
            out_ref[d, T, half] = slab
    right, left = lax.rem(me + 1, 4), lax.rem(me + 3, 4)

    def frame(t, _):
        for pair in range(2):
            ends = [l_ref[3, t, 2 * pair + i].astype(F32)[2:4] for i in range(2)]
            out_ref[right, t, pair] = jnp.concatenate(ends, axis=0).astype(BF16)
            starts = [l_ref[0, t, 2 * pair + i].astype(F32)[0:2] for i in range(2)]
            out_ref[left, t, pair] = jnp.concatenate(starts, axis=0).astype(BF16)
        return 0

    lax.fori_loop(0, T, frame, 0)


def conv_one_kernel(l_ref, e_ref, w_ref, gain_ref, shift_ref, hid_ref, st_ref, act, wm):
    me = lax.axis_index("x")
    left = lanes((16, 128)) < 64
    nothing = jnp.zeros((16, 128), BF16)
    for p in range(16):
        for k in range(9):
            wm[k, 16 * p : 16 * p + 16, 0:128] = w_ref[p, k]
            if k < 5:
                last = jnp.where(left, w_ref[p, 9 + k], nothing)
            else:
                last = jnp.where(left, nothing, w_ref[p, 4 + k])
            wm[k, 16 * p : 16 * p + 16, 128:256] = last
    total, squares = jnp.zeros((4, C), F32), jnp.zeros((4, C), F32)
    for s in range(4):
        total += e_ref[s, T, 0].astype(F32)
        squares += e_ref[s, T, 1].astype(F32)
    total = jnp.broadcast_to(jnp.sum(total, axis=0, keepdims=True), (8, C))
    squares = jnp.broadcast_to(jnp.sum(squares, axis=0, keepdims=True), (8, C))
    mean, inv = group_stats(total, squares)
    scale = inv * gain_ref[...]
    mean, scale = mean[0:1], scale[0:1]
    shift = shift_ref[...]
    before, after = lax.rem(me + 3, 4), lax.rem(me + 1, 4)
    row = rows((ROW, C))
    inside = (row >= jnp.where(me == 0, 4, 0)) & (row < jnp.where(me == 3, 20, ROW))
    act[:, 0:2] = jnp.zeros((4, 2, ROW, C), BF16)

    def frame(t, _):
        for h in range(4):
            lo = e_ref[before, t, h // 2].astype(F32)
            hi = e_ref[after, t, h // 2].astype(F32)
            if h % 2 == 0:
                lo = jnp.concatenate([lo[2:4], lo[0:2]], axis=0)
            else:
                hi = jnp.concatenate([hi[2:4], hi[0:2]], axis=0)
            own = [l_ref[q, t, h].astype(F32) for q in range(4)]
            v = jnp.concatenate([lo, *own, hi], axis=0)
            y = silu((v - mean) * scale + shift)
            act[h, t + 2] = jnp.where(inside, y, 0.0).astype(BF16)
        return 0

    lax.fori_loop(0, T, frame, 0)

    size = T * ROW
    lane = lanes((size, 128))
    place = rows((size, 128)) % ROW
    own = (place >= 4) & (place < 20)
    s1, s2 = jnp.zeros((1, 128), F32), jnp.zeros((1, 128), F32)
    for h in range(4):
        taps = [dh for dh in range(3) if 0 <= h + dh - 1 < 4]
        lhs = jnp.concatenate(
            [act[h + dh - 1, dt : dt + T].reshape(size, C) for dh in taps for dt in range(3)], axis=1
        )
        rhs = wm[3 * taps[0] : 3 * taps[-1] + 3].reshape(-1, C)
        y = jnp.dot(lhs, rhs, preferred_element_type=F32)
        y0, y1 = y[:, 0:128], y[:, 128:256]
        z = jnp.where(lane < 64, pltpu.roll(y0, 1, 0), y0) + pltpu.roll(y1, size - 1, 0)
        hidden = (z + pltpu.roll(z, 64, 1)).astype(BF16)
        hid_ref[h] = hidden.reshape(T, ROW, 128)
        counted = jnp.where(own, hidden.astype(F32), 0.0)
        s1 += jnp.sum(counted, axis=0, keepdims=True)
        s2 += jnp.sum(counted * counted, axis=0, keepdims=True)
    stats = jnp.concatenate([s1, s2, jnp.zeros((6, 128), F32)], axis=0)
    for d in range(4):
        st_ref[d] = stats


def conv_two_kernel(hid_ref, st_ref, w_ref, gain_ref, shift_ref, part_ref, act, wm):
    me = lax.axis_index("x")
    j = 2 * lax.axis_index("yl") + lax.axis_index("core")
    for dh in range(3):
        for dt in range(3):
            k = 3 * dh + dt
            for dw in range(3):
                for x in range(4):
                    at = 64 * dw + 16 * x
                    wm[k, at : at + 16] = w_ref[x, dt, dh, dw]
            wm[k, 192:256] = jnp.zeros((64, C), BF16)
    stats = st_ref[0] + st_ref[1] + st_ref[2] + st_ref[3]
    mean, inv = group_stats(
        jnp.broadcast_to(stats[0:1], (8, 128)), jnp.broadcast_to(stats[1:2], (8, 128))
    )
    row, lane = rows((C, 128)), lanes((C, 128))
    mine = (row == 64 * ((lane // 16) % 4) + 16 * j + lane % 16).astype(F32)
    pick = lambda ref: jnp.dot(
        jnp.broadcast_to(ref[...], (8, C)), mine, precision=lax.Precision.HIGHEST,
        preferred_element_type=F32,
    )
    scale = (inv * pick(gain_ref))[0:1]
    shift = pick(shift_ref)[0:1]
    mean = mean[0:1]
    row = rows((ROW, 128))
    inside = (row >= jnp.where(me == 0, 4, 0)) & (row < jnp.where(me == 3, 20, ROW))
    left = lanes((16, 128)) < 64
    act[:, 0:2] = jnp.zeros((4, 2, 16, C), BF16)

    def frame(t, _):
        for h in range(4):
            v = hid_ref[h, t].astype(F32)
            y = silu((v - mean) * scale + shift)
            y = jnp.where(inside, y, 0.0)
            a0, a1, a2 = (pltpu.roll(y, ROW - 3 - dw, 0)[0:16] for dw in range(3))
            act[h, t + 2, :, 0:128] = jnp.where(left, a0, a1).astype(BF16)
            act[h, t + 2, :, 128:256] = jnp.where(left, a2, 0.0).astype(BF16)
        return 0

    lax.fori_loop(0, T, frame, 0)
    for h in range(4):
        taps = [dh for dh in range(3) if 0 <= h + dh - 1 < 4]
        lhs = jnp.concatenate(
            [act[h + dh - 1, dt : dt + T].reshape(T * 16, C) for dh in taps for dt in range(3)], axis=1
        )
        rhs = wm[3 * taps[0] : 3 * taps[-1] + 3].reshape(-1, C)
        y = jnp.dot(lhs, rhs, preferred_element_type=F32).reshape(T, 16, C)
        for d in range(4):
            part_ref[d, :, h] = y[:, 4 * d : 4 * d + 4].astype(BF16)


def decode(part_ref, latent_ref, bias, t):
    branch = part_ref[0, t].astype(F32)
    for s in range(1, 4):
        branch = branch + part_ref[s, t].astype(F32)
    return (latent_ref[t].astype(F32) + (branch + bias)).astype(BF16)


def tail_kernel(part_ref, latent_ref, bias_ref, tail_ref):
    for i in range(OVMAX):
        tail_ref[i] = decode(part_ref, latent_ref, bias_ref[...], T - OVMAX + i)


def blend_kernel(shared_ref, part_ref, latent_ref, bias_ref, received_ref, out_ref):
    shared = shared_ref[0]
    bias = bias_ref[...]
    for t in range(T):
        own = decode(part_ref, latent_ref, bias, t)
        if t < OVMAX:
            source = jnp.clip(OVMAX - shared + t, 0, OVMAX - 1)
            other = received_ref[source].astype(F32)
            top = jnp.full((1, 1, C), t + 1, jnp.int32).astype(F32)
            share = top / jnp.full((1, 1, C), shared + 1, jnp.int32).astype(F32)
            head = own.astype(F32)
            mixed = share * head + (1.0 - share) * other
            active = jnp.full((1, 1, C), shared, jnp.int32) > t
            own = jnp.where(active, mixed, head).astype(BF16)
        out_ref[t] = own


def exchange(array, axis):
    return lax.all_to_all(array, axis, split_axis=0, concat_axis=0, tiled=True)


def shards(latent, intersections, gain_one, shift_one, weight_one, gain_two, shift_two, weight_two, bias):
    source = latent[0]
    flat = lambda v: v.reshape(1, C)
    sds = jax.ShapeDtypeStruct
    packed = call(pack_kernel, (weight_one,), sds((16, 14, 16, 128), BF16), cost=cost(1))
    kernel_one = exchange(packed, COL)
    wide = lax.all_gather(source, JAX_, axis=0, tiled=False)
    edges = call(edge_kernel, (wide,), sds((4, T + 1, 2, 4, C), BF16), cost=cost(1))
    edges = exchange(edges, "x")
    kernel_two = exchange(jnp.broadcast_to(weight_two[None], (4, *weight_two.shape)), "x")
    hidden, stats = call(
        conv_one_kernel,
        (wide, edges, kernel_one, flat(gain_one), flat(shift_one)),
        (sds((4, T, ROW, 128), BF16), sds((4, 8, 128), F32)),
        (pltpu.VMEM((4, T + 2, ROW, C), BF16), pltpu.VMEM((9, C, C), BF16)),
        cost=cost(4),
    )
    stats = exchange(stats, "x")
    part = call(
        conv_two_kernel,
        (hidden, stats, kernel_two, flat(gain_two), flat(shift_two)),
        sds((4, T, 4, 4, C), BF16),
        (pltpu.VMEM((4, T + 2, 16, C), BF16), pltpu.VMEM((9, C, C), BF16)),
        cost=cost(4),
    )
    part = exchange(part, JAX_)
    tail = call(tail_kernel, (part, source, flat(bias)), sds((OVMAX, 4, 4, C), BF16), cost=cost(1))
    tiles = lax.axis_size(TILE)
    received = lax.ppermute(tail, TILE, [(i, i + 1) for i in range(tiles - 1)])
    out = pl.pallas_call(
        blend_kernel,
        out_shape=sds((T, 4, 4, C), BF16),
        in_specs=[pl.BlockSpec(memory_space=pltpu.SMEM)] + [whole()] * 4,
        out_specs=whole(),
        compiler_params=PARAMS,
        cost_estimate=cost(1),
    )(intersections, part, source, flat(bias), received)
    return out[None]


def solution(mesh):
    wide = Mesh(mesh.devices.reshape(8, 4, 4, 2, 2), ("z", "yh", "x", "yl", "core"))
    image = P(TILE, None, None, COL, None)
    kernel = P(None, None, None, COL, None)
    in_specs = (image, P(TILE), P(), P(), kernel, P(), P(), kernel, P())
    return jax.shard_map(shards, mesh=wide, in_specs=in_specs, out_specs=image, check_vma=False)
```

time: 128 us -> 91.1 us (0.71)
  the two profiles are of different devices: /device:TPU:64 before, /device:TPU:256 now
where the time goes in v1:
time: 91.1 us; the launch traced here: 90.6 us
  blocking collectives  45.3 us (50%)
  waiting for transfers between devices  21.2 us (23%)
  starting transfers between devices  12.6 us (14%)
  Pallas kernels  7.84 us (9%)
  local copies, waits for them, and re-layouts  3.02 us (3%)
    all_to_all x3, blocking collectives, exchange(): return lax.all_to_all(array, axis, split_axis=0, concat_axis=0, tiled=True)  37.6 us
    all_to_all x2, waiting for transfers between devices, exchange(): return lax.all_to_all(array, axis, split_axis=0, concat_axis=0, tiled=True)  16.3 us
    all_to_all x2, starting transfers between devices, exchange(): return lax.all_to_all(array, axis, split_axis=0, concat_axis=0, tiled=True)  8.06 us
    all_gather x1, blocking collectives, shards(): wide = lax.all_gather(source, JAX_, axis=0, tiled=False)  7.63 us
    pallas_call x5, Pallas kernels, call(): pl.pallas_call(kernel, out_shape=out_shape, in_specs=[whole()] * len(inpu...  7.04 us
    ppermute x1, waiting for transfers between devices, shards(): received = lax.ppermute(tail, TILE, [(i, i + 1) for i in range(tiles - 1)])  4.88 us
    ppermute x1, starting transfers between devices, shards(): received = lax.ppermute(tail, TILE, [(i, i + 1) for i in range(tiles - 1)])  4.5 us
    unnamed x16, local copies, waits for them, and re-layouts  2.04 us
  transfers between devices with their start and end apart: 3, of which 3 were waited for; matrix products, arithmetic and copies ran while one was open for 0% of the time, Pallas kernels for 4%

profile of v1, /device:TPU:256, one launch (start us, length us, event | category | flops | bytes accessed | tf_op | source)
XLA Modules:
  0.0 90.6 jit_solution(14368482880102981333)
XLA Ops:
  0.0 7.6 %all_gather.3.l_ref = bf16[4,17,4,4,256]{4,3,2,1,0:T(4,128)(2,1)S(1)} all-gather(bf16[1,17,4,4,256]{4,3,2,1,0:T(4,128)(2,1)} %param.9), channel_id=1, replica_groups=mesh['z'=8,'yh'=4,'x'=4,'yl'=2,'core'=2] {'yl','core'}, dimensions={0}, use_global_device_ids=true | all-gather | bytes 696320 | tf_op jit(solution)/shard_map/all_gather | solution.py:289
  7.6 1.4 %shard_map.91 = bf16[4,18,2,4,256]{4,3,2,1,0:T(4,128)(2,1)} custom-call(bf16[4,17,4,4,256]{4,3,2,1,0:T(4,128)(2,1)S(1)} %all_gather.3.l_ref), custom_call_target="tpu_custom_call" | custom-call | flops 400000000 | bytes 1048576 | tf_op jit(solution)/shard_map/pallas_call | solution.py:27
  9.0 4.4 %all-to-all-start = ((bf16[4,18,2,4,256]{4,3,2,1,0:T(4,128)(2,1)}), bf16[4,18,2,4,256]{4,3,2,1,0:T(4,128)(2,1)S(1)}, u32[]{:S(2)}, u32[]{:S(2)}) async-start(bf16[4,18,2,4,256]{4,3,2,1,0:T(4,128)(2,1)} %shard_map.91), calls=%async_computation | async-start | bytes 589824 | tf_op jit(solution)/shard_map/all_to_all | solution.py:280
  13.4 0.0 copy-done.1
  13.4 0.3 shard_map.92
  13.7 0.0 copy-start.7
  13.7 7.2 %all-to-all-done.e_ref = bf16[4,18,2,4,256]{4,3,2,1,0:T(4,128)(2,1)S(1)} async-done(((bf16[4,18,2,4,256]{4,3,2,1,0:T(4,128)(2,1)}), bf16[4,18,2,4,256]{4,3,2,1,0:T(4,128)(2,1)S(1)}, u32[]{:S(2)}, u32[]{:S(2)}) %all-to-all-start) | async-done | bytes 294944 | tf_op jit(solution)/shard_map/all_to_all | solution.py:280
  20.9 17.9 %all_to_all.25.w_ref = bf16[16,14,16,128]{3,2,1,0:T(8,128)(2,1)S(1)} all-to-all(bf16[16,14,16,128]{3,2,1,0:T(8,128)(2,1)S(1)} %shard_map.92), channel_id=1, replica_groups=mesh['z'=8,'yh'=4,'x'=4,'yl'=2,'core'=2] {'x','yl','core'}, dimensions={0} | all-to-all | bytes 1835008 | tf_op jit(solution)/shard_map/all_to_all | solution.py:280
  38.8 0.0 copy-done.7
  38.9 1.0 %broadcast_in_dim.4 = bf16[4,3,3,3,16,256]{5,4,3,2,1,0:T(8,128)(2,1)} broadcast(bf16[3,3,3,16,256]{4,3,2,1,0:T(8,128)(2,1)S(1)} %copy-done.7), dimensions={1,2,3,4,5} | broadcast | bytes 1105920 | tf_op jit(solution)/shard_map/broadcast_in_dim | solution.py:292
  39.8 3.6 %all-to-all-start.3 = ((bf16[4,3,3,3,16,256]{5,4,3,2,1,0:T(8,128)(2,1)}), bf16[4,3,3,3,16,256]{5,4,3,2,1,0:T(8,128)(2,1)S(1)}, u32[]{:S(2)}, u32[]{:S(2)}) async-start(bf16[4,3,3,3,16,256]{5,4,3,2,1,0:T(8,128)(2,1)} %broadcast_in_dim.4), calls=%async_computation.3 | async-start | bytes 1769472 | tf_op jit(solution)/shard_map/all_to_all | solution.py:280
  43.5 0.0 copy-start.2
  43.5 0.7 copy-done.2
  44.2 3.2 %shard_map.93 = (bf16[4,17,24,128]{3,2,1,0:T(8,128)(2,1)S(1)}, f32[4,8,128]{2,1,0:T(8,128)S(1)}) custom-call(bf16[4,17,4,4,256]{4,3,2,1,0:T(4,128)(2,1)S(1)} %all_gather.3.l_ref, bf16[4,18,2,4,256]{4,3,2,1,0:T(4,128)(2,1)S(1)} %all-to-all-done.e_ref, bf16[16,14,16,128]{3,2,1,0:T(8,128)(2,1)S(1)} %all_to_all.25.w_ref, f32[1,256]{1,0:T(1,128)S(1)} %bitcast.9, ...), custom_call_target="tpu_custom_call" | custom-call | flops 1600000000 | bytes 1048576 | tf_op jit(solution)/shard_map/pallas_call | solution.py:27
  47.3 9.1 %all-to-all-done.3.w_ref = bf16[4,3,3,3,16,256]{5,4,3,2,1,0:T(8,128)(2,1)S(1)} async-done(((bf16[4,3,3,3,16,256]{5,4,3,2,1,0:T(8,128)(2,1)}), bf16[4,3,3,3,16,256]{5,4,3,2,1,0:T(8,128)(2,1)S(1)}, u32[]{:S(2)}, u32[]{:S(2)}) %all-to-all-start.3) | async-done | bytes 884768 | tf_op jit(solution)/shard_map/all_to_all | solution.py:280
  56.5 7.7 %all_to_all.26.st_ref = f32[4,8,128]{2,1,0:T(8,128)S(1)} all-to-all(f32[4,8,128]{2,1,0:T(8,128)S(1)} %get-tuple-element.8), channel_id=1, replica_groups=mesh['z'=8,'yh'=4,'x'=4,'yl'=2,'core'=2] {'x'}, dimensions={0} | all-to-all | bytes 32768 | tf_op jit(solution)/shard_map/all_to_all | solution.py:280
  64.2 0.7 copy-done.4
  64.8 2.2 %shard_map.94 = bf16[4,17,4,4,256]{4,3,2,1,0:T(4,128)(2,1)S(1)} custom-call(bf16[4,17,24,128]{3,2,1,0:T(8,128)(2,1)S(1)} %get-tuple-element.7.hid_ref, f32[4,8,128]{2,1,0:T(8,128)S(1)} %all_to_all.26.st_ref, bf16[4,3,3,3,16,256]{5,4,3,2,1,0:T(8,128)(2,1)S(1)} %all-to-all-done.3.w_ref, f32[1,256]{1,0:T(1,128)S(1)} %bitcast.11, f32[1,256]{1,0:T(1,128)S(1)} %bitcast.12), custom_call_target="tpu_custom_call" | custom-call | flops 1600000000 | bytes 1048576 | tf_op jit(solution)/shard_map/pallas_call | solution.py:27
  67.0 0.0 copy-start
  67.0 12.0 %all_to_all.27.part_ref = bf16[4,17,4,4,256]{4,3,2,1,0:T(4,128)(2,1)S(1)} all-to-all(bf16[4,17,4,4,256]{4,3,2,1,0:T(4,128)(2,1)S(1)} %shard_map.94), channel_id=1, replica_groups=mesh['z'=8,'yh'=4,'x'=4,'yl'=2,'core'=2] {'yl','core'}, dimensions={0} | all-to-all | bytes 1114112 | tf_op jit(solution)/shard_map/all_to_all | solution.py:280
  79.1 0.7 copy-done.6
  79.8 4.5 %collective-permute-start = (bf16[4,4,4,256]{3,2,1,0:T(4,128)(2,1)S(1)}, bf16[4,4,4,256]{3,2,1,0:T(4,128)(2,1)S(1)}, u32[]{:S(2)}, u32[]{:S(2)}) collective-permute-start(bf16[4,4,4,256]{3,2,1,0:T(4,128)(2,1)S(1)} %shard_map.95), channel_id=1, source_target_pairs={{0,16},{16,32},{32,48},{48,64},{64,80},{80,96},{96,112},{112,128},... | collective-permute-start | bytes 98312 | tf_op jit(solution)/shard_map/ppermute | solution.py:311
  84.9 4.9 %collective-permute-done.received_ref = bf16[4,4,4,256]{3,2,1,0:T(4,128)(2,1)S(1)} collective-permute-done((bf16[4,4,4,256]{3,2,1,0:T(4,128)(2,1)S(1)}, bf16[4,4,4,256]{3,2,1,0:T(4,128)(2,1)S(1)}, u32[]{:S(2)}, u32[]{:S(2)}) %collective-permute-start) | collective-permute-done | bytes 32800 | tf_op jit(solution)/shard_map/ppermute | solution.py:311
  89.8 0.8 shard_map.96
  (9 shorter events, 0.0 us)
Async XLA Ops:
  9.0 4.4 %copy-start.1 = (bf16[3,3,3,16,256]{4,3,2,1,0:T(8,128)(2,1)S(1)}, bf16[3,3,3,16,256]{4,3,2,1,0:T(8,128)(2,1)}, u32[]{:S(2)}) copy-start(bf16[3,3,3,16,256]{4,3,2,1,0:T(8,128)(2,1)} %w_ref.1) | copy-start | bytes 663556
  9.0 12.0 %all-to-all-start = ((bf16[4,18,2,4,256]{4,3,2,1,0:T(4,128)(2,1)}), bf16[4,18,2,4,256]{4,3,2,1,0:T(4,128)(2,1)S(1)}, u32[]{:S(2)}, u32[]{:S(2)}) async-start(bf16[4,18,2,4,256]{4,3,2,1,0:T(4,128)(2,1)} %shard_map.91), calls=%async_computation | async-start | bytes 589824 | tf_op jit(solution)/shard_map/all_to_all | solution.py:280
  13.7 25.1 %copy-start.7 = (bf16[3,3,3,16,256]{4,3,2,1,0:T(8,128)(2,1)S(1)}, bf16[3,3,3,16,256]{4,3,2,1,0:T(8,128)(2,1)}, u32[]{:S(2)}) copy-start(bf16[3,3,3,16,256]{4,3,2,1,0:T(8,128)(2,1)} %param.16) | copy-start | bytes 663556
  39.8 3.7 %copy-start.3 = (f32[256]{0:T(256)S(1)}, f32[256]{0:T(256)}, u32[]{:S(2)}) copy-start(f32[256]{0:T(256)} %param.12) | copy-start | bytes 3076
  39.8 16.6 %all-to-all-start.3 = ((bf16[4,3,3,3,16,256]{5,4,3,2,1,0:T(8,128)(2,1)}), bf16[4,3,3,3,16,256]{5,4,3,2,1,0:T(8,128)(2,1)S(1)}, u32[]{:S(2)}, u32[]{:S(2)}) async-start(bf16[4,3,3,3,16,256]{5,4,3,2,1,0:T(8,128)(2,1)} %broadcast_in_dim.4), calls=%async_computation.3 | async-start | bytes 1769472 | tf_op jit(solution)/shard_map/all_to_all | solution.py:280
  43.5 0.7 copy-start.2
  44.2 20.0 %copy-start.5 = (f32[256]{0:T(256)S(1)}, f32[256]{0:T(256)}, u32[]{:S(2)}) copy-start(f32[256]{0:T(256)} %param.15) | copy-start | bytes 3076
  64.2 0.7 copy-start.4
  67.0 12.1 %copy-start = (bf16[1,17,4,4,256]{4,3,2,1,0:T(4,128)(2,1)S(1)}, bf16[1,17,4,4,256]{4,3,2,1,0:T(4,128)(2,1)}, u32[]{:S(2)}) copy-start(bf16[1,17,4,4,256]{4,3,2,1,0:T(4,128)(2,1)} %param.9) | copy-start | bytes 417796
  79.1 0.7 copy-start.6
  79.8 10.0 %collective-permute-start = (bf16[4,4,4,256]{3,2,1,0:T(4,128)(2,1)S(1)}, bf16[4,4,4,256]{3,2,1,0:T(4,128)(2,1)S(1)}, u32[]{:S(2)}, u32[]{:S(2)}) collective-permute-start(bf16[4,4,4,256]{3,2,1,0:T(4,128)(2,1)S(1)} %shard_map.95), channel_id=1, source_target_pairs={{0,16},{16,32},{32,48},{48,64},{64,80},{80,96},{96,112},{112,128},... | collective-permute-start | bytes 98312 | tf_op jit(solution)/shard_map/ppermute | solution.py:311

commit v2 on v1

--- a/solution.py
+++ b/solution.py
@@ -73,7 +73,30 @@
     return v * (0.5 * jnp.tanh(0.5 * v) + 0.5)
 
 
-def pack_kernel(w_ref, out_ref):
+def pack_kernel(w_ref, latent_ref, g1_ref, s1_ref, g2_ref, s2_ref, b_ref, out_ref, edge_ref, vec_ref):
+    j = 2 * lax.axis_index("yl") + lax.axis_index("core")
+    for i, ref in enumerate((g1_ref, s1_ref, g2_ref, s2_ref, b_ref)):
+        vec_ref[i : i + 1] = ref[...]
+    vec_ref[5:8] = jnp.zeros((3, C), F32)
+    total, squares = jnp.zeros((4, C), F32), jnp.zeros((4, C), F32)
+    first = jnp.full((2, C), j, jnp.int32) == 0
+    for t in range(T):
+        ends = []
+        for h in range(H):
+            v = latent_ref[t, h].astype(F32)
+            total += v
+            squares += v * v
+            ends.append(jnp.where(first, v[0:2], v[2:4]))
+        for pair in range(2):
+            edge_ref[t, pair] = jnp.concatenate(ends[2 * pair : 2 * pair + 2], axis=0).astype(BF16)
+    pieces = []
+    for value in (total, squares):
+        for piece in split3(jnp.sum(value, axis=0, keepdims=True)):
+            piece = piece.astype(F32)
+            pieces += [piece[:, 0:128], piece[:, 128:256]]
+    sums = jnp.concatenate(pieces + [jnp.zeros((4, 128), F32)], axis=0).astype(BF16)
+    for d in range(16):
+        out_ref[d, 14] = sums
     row, col = rows((C, C)), lanes((C, C))
     source = 64 * ((col // 16) % 4) + 16 * (col // 64) + col % 16
     swapped = col ^ 64
@@ -101,35 +124,17 @@
                 out_ref[4 * x + j, m] = tile
 
 
-def edge_kernel(l_ref, out_ref):
-    me = lax.axis_index("x")
-    total, squares = jnp.zeros((4, C), F32), jnp.zeros((4, C), F32)
-    for q in range(4):
-        v = l_ref[q].astype(F32)
-        total += jnp.sum(v, axis=(0, 1))
-        squares += jnp.sum(v * v, axis=(0, 1))
-    total = jnp.sum(total, axis=0, keepdims=True)
-    squares = jnp.sum(squares, axis=0, keepdims=True)
-    zero = jnp.zeros((1, C), F32)
-    for half, value in ((0, total), (1, squares)):
-        pieces = [p.astype(F32) for p in split3(value)]
-        slab = jnp.concatenate(pieces + [zero], axis=0).astype(BF16)
-        for d in range(4):
-            out_ref[d, T, half] = slab
-    right, left = lax.rem(me + 1, 4), lax.rem(me + 3, 4)
-
-    def frame(t, _):
-        for pair in range(2):
-            ends = [l_ref[3, t, 2 * pair + i].astype(F32)[2:4] for i in range(2)]
-            out_ref[right, t, pair] = jnp.concatenate(ends, axis=0).astype(BF16)
-            starts = [l_ref[0, t, 2 * pair + i].astype(F32)[0:2] for i in range(2)]
-            out_ref[left, t, pair] = jnp.concatenate(starts, axis=0).astype(BF16)
-        return 0
-
-    lax.fori_loop(0, T, frame, 0)
-
-
-def conv_one_kernel(l_ref, e_ref, w_ref, gain_ref, shift_ref, hid_ref, st_ref, act, wm):
+def join_kernel(latent_ref, edge_ref, out_ref):
+    out_ref[:, 0:4] = latent_ref[...]
+    out_ref[:, 4:6] = edge_ref[...]
+
+
+def copies_kernel(w_ref, out_ref):
+    for d in range(4):
+        out_ref[d] = w_ref[...]
+
+
+def conv_one_kernel(l_ref, w_ref, vec_ref, hid_ref, st_ref, act, wm):
     me = lax.axis_index("x")
     left = lanes((16, 128)) < 64
     nothing = jnp.zeros((16, 128), BF16)
@@ -141,25 +146,25 @@
             else:
                 last = jnp.where(left, nothing, w_ref[p, 4 + k])
             wm[k, 16 * p : 16 * p + 16, 128:256] = last
-    total, squares = jnp.zeros((4, C), F32), jnp.zeros((4, C), F32)
-    for s in range(4):
-        total += e_ref[s, T, 0].astype(F32)
-        squares += e_ref[s, T, 1].astype(F32)
-    total = jnp.broadcast_to(jnp.sum(total, axis=0, keepdims=True), (8, C))
-    squares = jnp.broadcast_to(jnp.sum(squares, axis=0, keepdims=True), (8, C))
+    sums = sum(w_ref[p, 14].astype(F32) for p in range(16))
+    joined = lambda i: jnp.concatenate(
+        [sums[i + k : i + k + 1] + sums[i + k + 2 : i + k + 3] + sums[i + k + 4 : i + k + 5] for k in range(2)],
+        axis=1,
+    )
+    total = jnp.broadcast_to(joined(0), (8, C))
+    squares = jnp.broadcast_to(joined(6), (8, C))
     mean, inv = group_stats(total, squares)
-    scale = inv * gain_ref[...]
+    scale = inv * vec_ref[0:1]
     mean, scale = mean[0:1], scale[0:1]
-    shift = shift_ref[...]
-    before, after = lax.rem(me + 3, 4), lax.rem(me + 1, 4)
+    shift = vec_ref[1:2]
     row = rows((ROW, C))
     inside = (row >= jnp.where(me == 0, 4, 0)) & (row < jnp.where(me == 3, 20, ROW))
     act[:, 0:2] = jnp.zeros((4, 2, ROW, C), BF16)
 
     def frame(t, _):
         for h in range(4):
-            lo = e_ref[before, t, h // 2].astype(F32)
-            hi = e_ref[after, t, h // 2].astype(F32)
+            lo = l_ref[0, t, 4 + h // 2].astype(F32)
+            hi = l_ref[3, t, 4 + h // 2].astype(F32)
             if h % 2 == 0:
                 lo = jnp.concatenate([lo[2:4], lo[0:2]], axis=0)
             else:
@@ -192,11 +197,10 @@
         s1 += jnp.sum(counted, axis=0, keepdims=True)
         s2 += jnp.sum(counted * counted, axis=0, keepdims=True)
     stats = jnp.concatenate([s1, s2, jnp.zeros((6, 128), F32)], axis=0)
-    for d in range(4):
-        st_ref[d] = stats
-
-
-def conv_two_kernel(hid_ref, st_ref, w_ref, gain_ref, shift_ref, part_ref, act, wm):
+    st_ref[...] = stats
+
+
+def conv_two_kernel(hid_ref, st_ref, w_ref, vec_ref, part_ref, act, wm):
     me = lax.axis_index("x")
     j = 2 * lax.axis_index("yl") + lax.axis_index("core")
     for dh in range(3):
@@ -207,18 +211,14 @@
                     at = 64 * dw + 16 * x
                     wm[k, at : at + 16] = w_ref[x, dt, dh, dw]
             wm[k, 192:256] = jnp.zeros((64, C), BF16)
-    stats = st_ref[0] + st_ref[1] + st_ref[2] + st_ref[3]
+    stats = st_ref[...]
     mean, inv = group_stats(
         jnp.broadcast_to(stats[0:1], (8, 128)), jnp.broadcast_to(stats[1:2], (8, 128))
     )
     row, lane = rows((C, 128)), lanes((C, 128))
     mine = (row == 64 * ((lane // 16) % 4) + 16 * j + lane % 16).astype(F32)
-    pick = lambda ref: jnp.dot(
-        jnp.broadcast_to(ref[...], (8, C)), mine, precision=lax.Precision.HIGHEST,
-        preferred_element_type=F32,
-    )
-    scale = (inv * pick(gain_ref))[0:1]
-    shift = pick(shift_ref)[0:1]
+    picked = jnp.dot(vec_ref[...], mine, precision=lax.Precision.HIGHEST, preferred_element_type=F32)
+    scale, shift = inv[0:1] * picked[2:3], picked[3:4]
     mean = mean[0:1]
     row = rows((ROW, 128))
     inside = (row >= jnp.where(me == 0, 4, 0)) & (row < jnp.where(me == 3, 20, ROW))
@@ -247,23 +247,26 @@
             part_ref[d, :, h] = y[:, 4 * d : 4 * d + 4].astype(BF16)
 
 
-def decode(part_ref, latent_ref, bias, t):
-    branch = part_ref[0, t].astype(F32)
-    for s in range(1, 4):
-        branch = branch + part_ref[s, t].astype(F32)
-    return (latent_ref[t].astype(F32) + (branch + bias)).astype(BF16)
-
-
-def tail_kernel(part_ref, latent_ref, bias_ref, tail_ref):
+def decode(part_ref, at, latent, bias):
+    branch = part_ref[0, at].astype(F32)
+    for q in range(1, 4):
+        branch = branch + part_ref[q, at].astype(F32)
+    return (latent.astype(F32) + (branch + bias)).astype(BF16)
+
+
+def tail_kernel(part_ref, latent_ref, vec_ref, tail_ref):
     for i in range(OVMAX):
-        tail_ref[i] = decode(part_ref, latent_ref, bias_ref[...], T - OVMAX + i)
-
-
-def blend_kernel(shared_ref, part_ref, latent_ref, bias_ref, received_ref, out_ref):
+        tail_ref[i] = decode(part_ref, T - OVMAX + i, latent_ref[T - OVMAX + i], vec_ref[4:5])
+
+
+def blend_kernel(shared_ref, main_ref, tail_ref, latent_ref, vec_ref, received_ref, out_ref):
     shared = shared_ref[0]
-    bias = bias_ref[...]
+    bias = vec_ref[4:5]
     for t in range(T):
-        own = decode(part_ref, latent_ref, bias, t)
+        if t >= T - OVMAX:
+            out_ref[t] = tail_ref[t - T + OVMAX]
+            continue
+        own = decode(main_ref, t, latent_ref[t], bias)
         if t < OVMAX:
             source = jnp.clip(OVMAX - shared + t, 0, OVMAX - 1)
             other = received_ref[source].astype(F32)
@@ -280,43 +283,51 @@
     return lax.all_to_all(array, axis, split_axis=0, concat_axis=0, tiled=True)
 
 
-def shards(latent, intersections, gain_one, shift_one, weight_one, gain_two, shift_two, weight_two, bias):
+def block(latent, intersections, gain_one, shift_one, weight_one, gain_two, shift_two, weight_two, bias):
     source = latent[0]
     flat = lambda v: v.reshape(1, C)
     sds = jax.ShapeDtypeStruct
-    packed = call(pack_kernel, (weight_one,), sds((16, 14, 16, 128), BF16), cost=cost(1))
+    vectors = tuple(flat(v) for v in (gain_one, shift_one, gain_two, shift_two, bias))
+    packed, edge, vec = call(
+        pack_kernel,
+        (weight_one, source, *vectors),
+        (sds((16, 15, 16, 128), BF16), sds((T, 2, 4, C), BF16), sds((8, C), F32)),
+        cost=cost(1),
+    )
     kernel_one = exchange(packed, COL)
-    wide = lax.all_gather(source, JAX_, axis=0, tiled=False)
-    edges = call(edge_kernel, (wide,), sds((4, T + 1, 2, 4, C), BF16), cost=cost(1))
-    edges = exchange(edges, "x")
-    kernel_two = exchange(jnp.broadcast_to(weight_two[None], (4, *weight_two.shape)), "x")
+    route = [p for x in range(3) for p in ((4 * x + 3, 4 * x + 4), (4 * x + 4, 4 * x + 3))]
+    edge = lax.ppermute(edge, COL, route)
+    joined = call(join_kernel, (source, edge), sds((T, 6, 4, C), BF16), cost=cost(1))
+    wide = lax.all_gather(joined, JAX_, axis=0, tiled=False)
+    copies = call(copies_kernel, (weight_two,), sds((4, *weight_two.shape), BF16), cost=cost(1))
+    kernel_two = exchange(copies, "x")
     hidden, stats = call(
         conv_one_kernel,
-        (wide, edges, kernel_one, flat(gain_one), flat(shift_one)),
-        (sds((4, T, ROW, 128), BF16), sds((4, 8, 128), F32)),
+        (wide, kernel_one, vec),
+        (sds((4, T, ROW, 128), BF16), sds((8, 128), F32)),
         (pltpu.VMEM((4, T + 2, ROW, C), BF16), pltpu.VMEM((9, C, C), BF16)),
         cost=cost(4),
     )
-    stats = exchange(stats, "x")
+    stats = lax.psum(stats, "x")
     part = call(
         conv_two_kernel,
-        (hidden, stats, kernel_two, flat(gain_two), flat(shift_two)),
+        (hidden, stats, kernel_two, vec),
         sds((4, T, 4, 4, C), BF16),
         (pltpu.VMEM((4, T + 2, 16, C), BF16), pltpu.VMEM((9, C, C), BF16)),
         cost=cost(4),
     )
     part = exchange(part, JAX_)
-    tail = call(tail_kernel, (part, source, flat(bias)), sds((OVMAX, 4, 4, C), BF16), cost=cost(1))
+    tail = call(tail_kernel, (part, source, vec), sds((OVMAX, 4, 4, C), BF16), cost=cost(1))
     tiles = lax.axis_size(TILE)
     received = lax.ppermute(tail, TILE, [(i, i + 1) for i in range(tiles - 1)])
     out = pl.pallas_call(
         blend_kernel,
         out_shape=sds((T, 4, 4, C), BF16),
-        in_specs=[pl.BlockSpec(memory_space=pltpu.SMEM)] + [whole()] * 4,
+        in_specs=[pl.BlockSpec(memory_space=pltpu.SMEM)] + [whole()] * 5,
         out_specs=whole(),
         compiler_params=PARAMS,
         cost_estimate=cost(1),
-    )(intersections, part, source, flat(bias), received)
+    )(intersections, part, tail, source, vec, received)
     return out[None]
 
 
@@ -325,4 +336,4 @@
     image = P(TILE, None, None, COL, None)
     kernel = P(None, None, None, COL, None)
     in_specs = (image, P(TILE), P(), P(), kernel, P(), P(), kernel, P())
-    return jax.shard_map(shards, mesh=wide, in_specs=in_specs, out_specs=image, check_vma=False)
+    return jax.shard_map(block, mesh=wide, in_specs=in_specs, out_specs=image, check_vma=False)

time: 91.1 us -> 82.6 us (0.907)
  blocking collectives: 45.3 us -> 36.5 us
  starting transfers between devices: 12.6 us -> 14.2 us
  waiting for transfers between devices: 21.2 us -> 19.7 us
    all_to_all x3 -> x1, blocking collectives: 37.6 us -> 12.3 us  [exchange(): return lax.all_to_all(array, axis, split_axis=0, concat_axis=0, tiled=True)]
    psum x0 -> x1, blocking collectives: none -> 10.3 us  [block(): stats = lax.psum(stats, 'x')]
    all_gather x1, blocking collectives: 7.63 us -> 13.9 us  [block(): wide = lax.all_gather(joined, JAX_, axis=0, tiled=False)]
    all_to_all x2, waiting for transfers between devices: 16.3 us -> 14.8 us  [exchange(): return lax.all_to_all(array, axis, split_axis=0, concat_axis=0, tiled=True)]
    all_to_all x2, starting transfers between devices: 8.06 us -> 9.05 us  [exchange(): return lax.all_to_all(array, axis, split_axis=0, concat_axis=0, tiled=True)]
    broadcast_in_dim x1 -> x0, local copies, waits for them, and re-layouts: 0.97 us -> none  [shards(): jnp.broadcast_to(weight_two[None], (4, *weight_two.shape))]
    ppermute x1 -> x2, starting transfers between devices: 4.5 us -> 5.16 us  [the longest x1 4.5 us: block(): received = lax.ppermute(tail, TILE, [(i, i + 1) for i in range(tiles - 1)])]
    pallas_call x5 -> x6, Pallas kernels: 7.04 us -> 7.68 us  [call(): pl.pallas_call(kernel, out_shape=out_shape, in_specs=[whole()] * len(inpu...]
  transfers between devices with their start and end apart: 3 -> 4, of which waited for: 3 -> 2; matrix products, arithmetic and copies ran while one was open for 0% -> 0% of each run, Pallas kernels for 4% -> 5%
where the time goes in v2:
time: 82.6 us; the launch traced here: 82.2 us
  blocking collectives  36.5 us (44%)
  waiting for transfers between devices  19.7 us (24%)
  starting transfers between devices  14.2 us (17%)
  Pallas kernels  8.46 us (10%)
  local copies, waits for them, and re-layouts  2.57 us (3%)
    all_to_all x2, waiting for transfers between devices, exchange(): return lax.all_to_all(array, axis, split_axis=0, concat_axis=0, tiled=True)  14.8 us
    all_gather x1, blocking collectives, block(): wide = lax.all_gather(joined, JAX_, axis=0, tiled=False)  13.9 us
    all_to_all x1, blocking collectives, exchange(): return lax.all_to_all(array, axis, split_axis=0, concat_axis=0, tiled=True)  12.3 us
    psum x1, blocking collectives, block(): stats = lax.psum(stats, 'x')  10.3 us
    all_to_all x2, starting transfers between devices, exchange(): return lax.all_to_all(array, axis, split_axis=0, concat_axis=0, tiled=True)  9.05 us
    pallas_call x6, Pallas kernels, call(): pl.pallas_call(kernel, out_shape=out_shape, in_specs=[whole()] * len(inpu...  7.68 us
    ppermute x1, waiting for transfers between devices, block(): received = lax.ppermute(tail, TILE, [(i, i + 1) for i in range(tiles - 1)])  4.88 us
    ppermute x1, starting transfers between devices, block(): received = lax.ppermute(tail, TILE, [(i, i + 1) for i in range(tiles - 1)])  4.5 us
  transfers between devices with their start and end apart: 4, of which 2 were waited for; matrix products, arithmetic and copies ran while one was open for 0% of the time, Pallas kernels for 5%

profile of v2, /device:TPU:256, one launch (start us, length us, event | category | flops | bytes accessed | tf_op | source)
XLA Modules:
  0.0 82.2 jit_solution(61660749015241355)
XLA Ops:
  0.0 0.7 copy-done.7
  0.7 0.0 copy-done.8
  0.7 0.0 copy-done.5
  0.7 0.0 copy-done.6
  0.7 0.0 copy-done.4
  0.7 0.9 %copy-done = bf16[3,3,3,16,256]{4,3,2,1,0:T(8,128)(2,1)S(1)} copy-done((bf16[3,3,3,16,256]{4,3,2,1,0:T(8,128)(2,1)S(1)}, bf16[3,3,3,16,256]{4,3,2,1,0:T(8,128)(2,1)}, u32[]{:S(2)}) %copy-start) | copy-done | bytes 221208
  1.7 0.9 %copy-done.2 = bf16[1,17,4,4,256]{4,3,2,1,0:T(4,128)(2,1)S(1)} copy-done((bf16[1,17,4,4,256]{4,3,2,1,0:T(4,128)(2,1)S(1)}, bf16[1,17,4,4,256]{4,3,2,1,0:T(4,128)(2,1)}, u32[]{:S(2)}) %copy-start.2) | copy-done | bytes 139288
  2.6 1.3 %shard_map.91 = (bf16[16,15,16,128]{3,2,1,0:T(8,128)(2,1)}, bf16[17,2,4,256]{3,2,1,0:T(4,128)(2,1)S(1)}, f32[8,256]{1,0:T(8,128)S(1)}) custom-call(bf16[3,3,3,16,256]{4,3,2,1,0:T(8,128)(2,1)S(1)} %copy-done, bf16[17,4,4,256]{3,2,1,0:T(4,128)(2,1)S(1)} %bitcast.9, f32[1,256]{1,0:T(1,128)S(1)} %bitcast.13, f32[1,256]{1,0:T(1,128)S(1)} %bitcast.14, ...), custom_call_target="tpu_custom_call" | custom-call | flops 400000000 | bytes 1048576 | tf_op jit(solution)/shard_map/pallas_call | solution.py:27
  3.9 5.5 %all-to-all-start = ((bf16[16,15,16,128]{3,2,1,0:T(8,128)(2,1)}), bf16[16,15,16,128]{3,2,1,0:T(8,128)(2,1)S(1)}, u32[]{:S(2)}, u32[]{:S(2)}) async-start(bf16[16,15,16,128]{3,2,1,0:T(8,128)(2,1)} %get-tuple-element.11), calls=%async_computation | async-start | bytes 1966080 | tf_op jit(solution)/shard_map/all_to_all | solution.py:283
  9.4 0.0 copy-done.1
  9.4 1.0 %shard_map.94 = bf16[4,3,3,3,16,256]{5,4,3,2,1,0:T(8,128)(2,1)} custom-call(bf16[3,3,3,16,256]{4,3,2,1,0:T(8,128)(2,1)S(1)} %copy-done.1), custom_call_target="tpu_custom_call" | custom-call | flops 400000000 | bytes 1048576 | tf_op jit(solution)/shard_map/pallas_call | solution.py:27
  10.5 14.8 %all-to-all-done.w_ref = bf16[16,15,16,128]{3,2,1,0:T(8,128)(2,1)S(1)} async-done(((bf16[16,15,16,128]{3,2,1,0:T(8,128)(2,1)}), bf16[16,15,16,128]{3,2,1,0:T(8,128)(2,1)S(1)}, u32[]{:S(2)}, u32[]{:S(2)}) %all-to-all-start) | async-done | bytes 983072 | tf_op jit(solution)/shard_map/all_to_all | solution.py:283
  25.2 3.5 %all-to-all-start.1 = ((bf16[4,3,3,3,16,256]{5,4,3,2,1,0:T(8,128)(2,1)}), bf16[4,3,3,3,16,256]{5,4,3,2,1,0:T(8,128)(2,1)S(1)}, u32[]{:S(2)}, u32[]{:S(2)}) async-start(bf16[4,3,3,3,16,256]{5,4,3,2,1,0:T(8,128)(2,1)} %shard_map.94), calls=%async_computation.1 | async-start | bytes 1769472 | tf_op jit(solution)/shard_map/all_to_all | solution.py:283
  28.8 0.7 collective-permute-start
  29.4 0.0 collective-permute-done.edge_ref
  29.5 13.9 %all-gather = bf16[68,6,4,256]{3,2,1,0:T(4,128)(2,1)S(1)} all-gather(bf16[17,6,4,256]{3,2,1,0:T(4,128)(2,1)S(1)} %shard_map.92), channel_id=2, replica_groups=mesh['z'=8,'yh'=4,'x'=4,'yl'=2,'core'=2] {'yl','core'}, dimensions={0}, use_global_device_ids=true | all-gather | bytes 1044480 | tf_op jit(solution)/shard_map/all_gather | solution.py:301
  43.4 3.2 %shard_map.93 = (bf16[4,17,24,128]{3,2,1,0:T(8,128)(2,1)S(1)}, f32[8,128]{1,0:T(8,128)S(1)}) custom-call(bf16[4,17,6,4,256]{4,3,2,1,0:T(4,128)(2,1)S(1)} %bitcast.8, bf16[16,15,16,128]{3,2,1,0:T(8,128)(2,1)S(1)} %all-to-all-done.w_ref, f32[8,256]{1,0:T(8,128)S(1)} %get-tuple-element.12.vec_ref), custom_call_target="tpu_custom_call" | custom-call | flops 1600000000 | bytes 1048576 | tf_op jit(solution)/shard_map/pallas_call | solution.py:27
  46.6 10.3 %psum.7.st_ref = f32[8,128]{1,0:T(8,128)S(1)} all-reduce(f32[8,128]{1,0:T(8,128)S(1)} %get-tuple-element.14), channel_id=1, replica_groups=mesh['z'=8,'yh'=4,'x'=4,'yl'=2,'core'=2] {'x'}, use_global_device_ids=true, to_apply=%region_0.0 | all-reduce | flops 1024 | bytes 8192 | tf_op jit(solution)/shard_map/psum | solution.py:311
  56.9 0.0 all-to-all-done.1.w_ref
  56.9 2.1 %shard_map.95 = bf16[4,17,4,4,256]{4,3,2,1,0:T(4,128)(2,1)S(1)} custom-call(bf16[4,17,24,128]{3,2,1,0:T(8,128)(2,1)S(1)} %get-tuple-element.13.hid_ref, f32[8,128]{1,0:T(8,128)S(1)} %psum.7.st_ref, bf16[4,3,3,3,16,256]{5,4,3,2,1,0:T(8,128)(2,1)S(1)} %all-to-all-done.1.w_ref, f32[8,256]{1,0:T(8,128)S(1)} %get-tuple-element.12.vec_ref), custom_call_target="tpu_custom_call" | custom-call | flops 1600000000 | bytes 1048576 | tf_op jit(solution)/shard_map/pallas_call | solution.py:27
  59.0 12.3 %all_to_all.15.part_ref.main_ref = bf16[4,17,4,4,256]{4,3,2,1,0:T(4,128)(2,1)S(1)} all-to-all(bf16[4,17,4,4,256]{4,3,2,1,0:T(4,128)(2,1)S(1)} %shard_map.95), channel_id=1, replica_groups=mesh['z'=8,'yh'=4,'x'=4,'yl'=2,'core'=2] {'yl','core'}, dimensions={0} | all-to-all | bytes 1114112 | tf_op jit(solution)/shard_map/all_to_all | solution.py:283
  71.3 4.5 %collective-permute-start.1 = (bf16[4,4,4,256]{3,2,1,0:T(4,128)(2,1)S(1)}, bf16[4,4,4,256]{3,2,1,0:T(4,128)(2,1)S(1)}, u32[]{:S(2)}, u32[]{:S(2)}) collective-permute-start(bf16[4,4,4,256]{3,2,1,0:T(4,128)(2,1)S(1)} %shard_map.96.tail_ref), channel_id=1, source_target_pairs={{0,16},{16,32},{32,48},{48,64},{64,80},{80,96},{96,112},{112,128},... | collective-permute-start | bytes 98312 | tf_op jit(solution)/shard_map/ppermute | solution.py:322
  76.5 4.9 %collective-permute-done.1.received_ref = bf16[4,4,4,256]{3,2,1,0:T(4,128)(2,1)S(1)} collective-permute-done((bf16[4,4,4,256]{3,2,1,0:T(4,128)(2,1)S(1)}, bf16[4,4,4,256]{3,2,1,0:T(4,128)(2,1)S(1)}, u32[]{:S(2)}, u32[]{:S(2)}) %collective-permute-start.1) | collective-permute-done | bytes 32800 | tf_op jit(solution)/shard_map/ppermute | solution.py:322
  81.4 0.8 shard_map.97
  (12 shorter events, 0.1 us)
Async XLA Ops:
  0.0 0.7 copy-start.7
  0.0 0.7 copy-start.8
  0.0 0.7 copy-start.5
  0.0 0.7 copy-start.6
  0.0 0.7 copy-start.4
  0.7 0.9 %copy-start = (bf16[3,3,3,16,256]{4,3,2,1,0:T(8,128)(2,1)S(1)}, bf16[3,3,3,16,256]{4,3,2,1,0:T(8,128)(2,1)}, u32[]{:S(2)}) copy-start(bf16[3,3,3,16,256]{4,3,2,1,0:T(8,128)(2,1)} %w_ref.2) | copy-start | bytes 663556
  1.7 0.9 %copy-start.2 = (bf16[1,17,4,4,256]{4,3,2,1,0:T(4,128)(2,1)S(1)}, bf16[1,17,4,4,256]{4,3,2,1,0:T(4,128)(2,1)}, u32[]{:S(2)}) copy-start(bf16[1,17,4,4,256]{4,3,2,1,0:T(4,128)(2,1)} %param.9) | copy-start | bytes 417796
  3.9 5.6 %copy-start.1 = (bf16[3,3,3,16,256]{4,3,2,1,0:T(8,128)(2,1)S(1)}, bf16[3,3,3,16,256]{4,3,2,1,0:T(8,128)(2,1)}, u32[]{:S(2)}) copy-start(bf16[3,3,3,16,256]{4,3,2,1,0:T(8,128)(2,1)} %w_ref.3) | copy-start | bytes 663556
  3.9 21.4 %all-to-all-start = ((bf16[16,15,16,128]{3,2,1,0:T(8,128)(2,1)}), bf16[16,15,16,128]{3,2,1,0:T(8,128)(2,1)S(1)}, u32[]{:S(2)}, u32[]{:S(2)}) async-start(bf16[16,15,16,128]{3,2,1,0:T(8,128)(2,1)} %get-tuple-element.11), calls=%async_computation | async-start | bytes 1966080 | tf_op jit(solution)/shard_map/all_to_all | solution.py:283
  10.5 19.0 %copy-start.3 = (bf16[1,17,4,4,256]{4,3,2,1,0:T(4,128)(2,1)S(1)}, bf16[1,17,4,4,256]{4,3,2,1,0:T(4,128)(2,1)}, u32[]{:S(2)}) copy-start(bf16[1,17,4,4,256]{4,3,2,1,0:T(4,128)(2,1)} %param.9) | copy-start | bytes 417796
  25.2 31.7 %all-to-all-start.1 = ((bf16[4,3,3,3,16,256]{5,4,3,2,1,0:T(8,128)(2,1)}), bf16[4,3,3,3,16,256]{5,4,3,2,1,0:T(8,128)(2,1)S(1)}, u32[]{:S(2)}, u32[]{:S(2)}) async-start(bf16[4,3,3,3,16,256]{5,4,3,2,1,0:T(8,128)(2,1)} %shard_map.94), calls=%async_computation.1 | async-start | bytes 1769472 | tf_op jit(solution)/shard_map/all_to_all | solution.py:283
  28.8 0.7 collective-permute-start
  71.3 10.0 %collective-permute-start.1 = (bf16[4,4,4,256]{3,2,1,0:T(4,128)(2,1)S(1)}, bf16[4,4,4,256]{3,2,1,0:T(4,128)(2,1)S(1)}, u32[]{:S(2)}, u32[]{:S(2)}) collective-permute-start(bf16[4,4,4,256]{3,2,1,0:T(4,128)(2,1)S(1)} %shard_map.96.tail_ref), channel_id=1, source_target_pairs={{0,16},{16,32},{32,48},{48,64},{64,80},{80,96},{96,112},{112,128},... | collective-permute-start | bytes 98312 | tf_op jit(solution)/shard_map/ppermute | solution.py:322

commit v3 on v2

--- a/solution.py
+++ b/solution.py
@@ -73,22 +73,17 @@
     return v * (0.5 * jnp.tanh(0.5 * v) + 0.5)
 
 
-def pack_kernel(w_ref, latent_ref, g1_ref, s1_ref, g2_ref, s2_ref, b_ref, out_ref, edge_ref, vec_ref):
-    j = 2 * lax.axis_index("yl") + lax.axis_index("core")
+def pack_kernel(w_ref, latent_ref, g1_ref, s1_ref, g2_ref, s2_ref, b_ref, n_ref, out_ref, vec_ref):
     for i, ref in enumerate((g1_ref, s1_ref, g2_ref, s2_ref, b_ref)):
         vec_ref[i : i + 1] = ref[...]
-    vec_ref[5:8] = jnp.zeros((3, C), F32)
+    vec_ref[5:6] = jnp.broadcast_to(n_ref[...].astype(F32), (1, C))
+    vec_ref[6:8] = jnp.zeros((2, C), F32)
     total, squares = jnp.zeros((4, C), F32), jnp.zeros((4, C), F32)
-    first = jnp.full((2, C), j, jnp.int32) == 0
     for t in range(T):
-        ends = []
         for h in range(H):
             v = latent_ref[t, h].astype(F32)
             total += v
             squares += v * v
-            ends.append(jnp.where(first, v[0:2], v[2:4]))
-        for pair in range(2):
-            edge_ref[t, pair] = jnp.concatenate(ends[2 * pair : 2 * pair + 2], axis=0).astype(BF16)
     pieces = []
     for value in (total, squares):
         for piece in split3(jnp.sum(value, axis=0, keepdims=True)):
@@ -124,14 +119,18 @@
                 out_ref[4 * x + j, m] = tile
 
 
-def join_kernel(latent_ref, edge_ref, out_ref):
-    out_ref[:, 0:4] = latent_ref[...]
-    out_ref[:, 4:6] = edge_ref[...]
-
-
-def copies_kernel(w_ref, out_ref):
-    for d in range(4):
-        out_ref[d] = w_ref[...]
+def join_kernel(latent_ref, other_ref, near_ref, far_ref, out_ref):
+    out_ref[0] = latent_ref[...]
+    out_ref[1] = other_ref[...]
+    straight = lax.axis_index("yl") == lax.axis_index("core")
+
+    @pl.when(straight)
+    def _():
+        out_ref[2] = near_ref[...]
+
+    @pl.when(jnp.logical_not(straight))
+    def _():
+        out_ref[2] = far_ref[...]
 
 
 def conv_one_kernel(l_ref, w_ref, vec_ref, hid_ref, st_ref, act, wm):
@@ -157,19 +156,17 @@
     scale = inv * vec_ref[0:1]
     mean, scale = mean[0:1], scale[0:1]
     shift = vec_ref[1:2]
+    yl = lax.axis_index("yl")
+    slots = (yl, 1 - yl)
     row = rows((ROW, C))
     inside = (row >= jnp.where(me == 0, 4, 0)) & (row < jnp.where(me == 3, 20, ROW))
     act[:, 0:2] = jnp.zeros((4, 2, ROW, C), BF16)
 
     def frame(t, _):
         for h in range(4):
-            lo = l_ref[0, t, 4 + h // 2].astype(F32)
-            hi = l_ref[3, t, 4 + h // 2].astype(F32)
-            if h % 2 == 0:
-                lo = jnp.concatenate([lo[2:4], lo[0:2]], axis=0)
-            else:
-                hi = jnp.concatenate([hi[2:4], hi[0:2]], axis=0)
-            own = [l_ref[q, t, h].astype(F32) for q in range(4)]
+            lo = l_ref[0, 2, t, h].astype(F32)
+            hi = l_ref[1, 2, t, h].astype(F32)
+            own = [l_ref[q % 2, slots[q // 2], t, h].astype(F32) for q in range(4)]
             v = jnp.concatenate([lo, *own, hi], axis=0)
             y = silu((v - mean) * scale + shift)
             act[h, t + 2] = jnp.where(inside, y, 0.0).astype(BF16)
@@ -197,21 +194,22 @@
         s1 += jnp.sum(counted, axis=0, keepdims=True)
         s2 += jnp.sum(counted * counted, axis=0, keepdims=True)
     stats = jnp.concatenate([s1, s2, jnp.zeros((6, 128), F32)], axis=0)
-    st_ref[...] = stats
-
-
-def conv_two_kernel(hid_ref, st_ref, w_ref, vec_ref, part_ref, act, wm):
+    for d in range(4):
+        st_ref[d] = stats
+
+
+def conv_two_kernel(hid_ref, st_ref, w0_ref, w1_ref, w2_ref, w3_ref, vec_ref, part_ref, act, wm):
     me = lax.axis_index("x")
     j = 2 * lax.axis_index("yl") + lax.axis_index("core")
-    for dh in range(3):
-        for dt in range(3):
-            k = 3 * dh + dt
+    for step, w_ref in enumerate((w0_ref, w1_ref, w2_ref, w3_ref)):
+        x = lax.rem(me + 4 - step, 4)
+        for k in range(9):
             for dw in range(3):
-                for x in range(4):
-                    at = 64 * dw + 16 * x
-                    wm[k, at : at + 16] = w_ref[x, dt, dh, dw]
-            wm[k, 192:256] = jnp.zeros((64, C), BF16)
-    stats = st_ref[...]
+                at = pl.multiple_of(64 * dw + 16 * x, 16)
+                wm[k, pl.ds(at, 16)] = w_ref[k % 3, k // 3, dw]
+    for k in range(9):
+        wm[k, 192:256] = jnp.zeros((64, C), BF16)
+    stats = st_ref[0] + st_ref[1] + st_ref[2] + st_ref[3]
     mean, inv = group_stats(
         jnp.broadcast_to(stats[0:1], (8, 128)), jnp.broadcast_to(stats[1:2], (8, 128))
     )
@@ -259,23 +257,21 @@
         tail_ref[i] = decode(part_ref, T - OVMAX + i, latent_ref[T - OVMAX + i], vec_ref[4:5])
 
 
-def blend_kernel(shared_ref, main_ref, tail_ref, latent_ref, vec_ref, received_ref, out_ref):
-    shared = shared_ref[0]
-    bias = vec_ref[4:5]
+def blend_kernel(main_ref, tail_ref, latent_ref, vec_ref, received_ref, out_ref):
+    bias, shared = vec_ref[4:5], vec_ref[5:6]
     for t in range(T):
         if t >= T - OVMAX:
             out_ref[t] = tail_ref[t - T + OVMAX]
             continue
         own = decode(main_ref, t, latent_ref[t], bias)
         if t < OVMAX:
-            source = jnp.clip(OVMAX - shared + t, 0, OVMAX - 1)
-            other = received_ref[source].astype(F32)
-            top = jnp.full((1, 1, C), t + 1, jnp.int32).astype(F32)
-            share = top / jnp.full((1, 1, C), shared + 1, jnp.int32).astype(F32)
+            other = received_ref[OVMAX - 1].astype(F32)
+            for n in range(t + 2, OVMAX + 1):
+                other = jnp.where((shared == n)[None], received_ref[OVMAX - n + t].astype(F32), other)
+            share = jnp.full((1, C), t + 1, F32) / (shared + 1.0)
             head = own.astype(F32)
             mixed = share * head + (1.0 - share) * other
-            active = jnp.full((1, 1, C), shared, jnp.int32) > t
-            own = jnp.where(active, mixed, head).astype(BF16)
+            own = jnp.where((shared > t)[None], mixed, head).astype(BF16)
         out_ref[t] = own
 
 
@@ -288,30 +284,34 @@
     flat = lambda v: v.reshape(1, C)
     sds = jax.ShapeDtypeStruct
     vectors = tuple(flat(v) for v in (gain_one, shift_one, gain_two, shift_two, bias))
-    packed, edge, vec = call(
+    other = lax.ppermute(source, "yl", [(0, 1), (1, 0)])
+    near = [p for x in range(3) for p in ((4 * x + 3, 4 * x + 4), (4 * x + 4, 4 * x + 3))]
+    far = [p for x in range(3) for p in ((4 * x + 3, 4 * x + 6), (4 * x + 4, 4 * x + 1))]
+    near = lax.ppermute(source, COL, near)
+    far = lax.ppermute(source, COL, far)
+    packed, vec = call(
         pack_kernel,
-        (weight_one, source, *vectors),
-        (sds((16, 15, 16, 128), BF16), sds((T, 2, 4, C), BF16), sds((8, C), F32)),
+        (weight_one, source, *vectors, intersections.reshape(1, 1)),
+        (sds((16, 15, 16, 128), BF16), sds((8, C), F32)),
         cost=cost(1),
     )
     kernel_one = exchange(packed, COL)
-    route = [p for x in range(3) for p in ((4 * x + 3, 4 * x + 4), (4 * x + 4, 4 * x + 3))]
-    edge = lax.ppermute(edge, COL, route)
-    joined = call(join_kernel, (source, edge), sds((T, 6, 4, C), BF16), cost=cost(1))
-    wide = lax.all_gather(joined, JAX_, axis=0, tiled=False)
-    copies = call(copies_kernel, (weight_two,), sds((4, *weight_two.shape), BF16), cost=cost(1))
-    kernel_two = exchange(copies, "x")
+    joined = call(join_kernel, (source, other, near, far), sds((3, T, 4, 4, C), BF16), cost=cost(1))
+    wide = lax.all_gather(joined, "core", axis=0, tiled=False)
+    kernel_two = [weight_two]
+    for step in range(1, 4):
+        kernel_two.append(lax.ppermute(weight_two, "x", [(x, (x + step) % 4) for x in range(4)]))
     hidden, stats = call(
         conv_one_kernel,
         (wide, kernel_one, vec),
-        (sds((4, T, ROW, 128), BF16), sds((8, 128), F32)),
+        (sds((4, T, ROW, 128), BF16), sds((4, 8, 128), F32)),
         (pltpu.VMEM((4, T + 2, ROW, C), BF16), pltpu.VMEM((9, C, C), BF16)),
         cost=cost(4),
     )
-    stats = lax.psum(stats, "x")
+    stats = exchange(stats, "x")
     part = call(
         conv_two_kernel,
-        (hidden, stats, kernel_two, vec),
+        (hidden, stats, *kernel_two, vec),
         sds((4, T, 4, 4, C), BF16),
         (pltpu.VMEM((4, T + 2, 16, C), BF16), pltpu.VMEM((9, C, C), BF16)),
         cost=cost(4),
@@ -320,14 +320,7 @@
     tail = call(tail_kernel, (part, source, vec), sds((OVMAX, 4, 4, C), BF16), cost=cost(1))
     tiles = lax.axis_size(TILE)
     received = lax.ppermute(tail, TILE, [(i, i + 1) for i in range(tiles - 1)])
-    out = pl.pallas_call(
-        blend_kernel,
-        out_shape=sds((T, 4, 4, C), BF16),
-        in_specs=[pl.BlockSpec(memory_space=pltpu.SMEM)] + [whole()] * 5,
-        out_specs=whole(),
-        compiler_params=PARAMS,
-        cost_estimate=cost(1),
-    )(intersections, part, tail, source, vec, received)
+    out = call(blend_kernel, (part, tail, source, vec, received), sds((T, 4, 4, C), BF16), cost=cost(1))
     return out[None]
 
 

time: 82.6 us -> 71.3 us (0.86)
  blocking collectives: 36.5 us -> 13.9 us
  starting transfers between devices: 14.2 us -> 32.6 us
  waiting for transfers between devices: 19.7 us -> 12.7 us
    ppermute x1 -> x6, starting transfers between devices: 0.67 us -> 19.3 us  [the longest x3 14.2 us: block(): lax.ppermute(weight_two, 'x', [(x, (x + step) % 4) for x in range(4)])]
    all_gather x1, blocking collectives: 13.9 us -> 2.4 us  [block(): wide = lax.all_gather(joined, 'core', axis=0, tiled=False)]
    psum x1 -> x0, blocking collectives: 10.3 us -> none  [block(): stats = lax.psum(stats, 'x')]
    all_to_all x2, waiting for transfers between devices: 14.8 us -> 5.3 us  [exchange(): return lax.all_to_all(array, axis, split_axis=0, concat_axis=0, tiled=True)]
    ppermute x1 -> x6, waiting for transfers between devices: 0.01 us -> 1.89 us  [the longest x1 1.88 us: block(): other = lax.ppermute(source, 'yl', [(0, 1), (1, 0)])]
  transfers between devices with their start and end apart: 4 -> 9, of which waited for: 2 -> 3; matrix products, arithmetic and copies ran while one was open for 0% -> 0% of each run, Pallas kernels for 5% -> 5%
where the time goes in v3:
time: 71.3 us; the launch traced here: 70.7 us
  starting transfers between devices  32.6 us (46%)
  blocking collectives  13.9 us (19%)
  waiting for transfers between devices  12.7 us (18%)
  Pallas kernels  8.04 us (11%)
  local copies, waits for them, and re-layouts  2.55 us (4%)
  between operations  0.85 us (1%)
    ppermute x3, starting transfers between devices, block(): lax.ppermute(weight_two, 'x', [(x, (x + step) % 4) for x in range(4)])  14.2 us
    all_to_all x1, blocking collectives, exchange(): return lax.all_to_all(array, axis, split_axis=0, concat_axis=0, tiled=True)  11.5 us
    all_to_all x2, starting transfers between devices, exchange(): return lax.all_to_all(array, axis, split_axis=0, concat_axis=0, tiled=True)  8.8 us
    pallas_call x6, Pallas kernels, call(): pl.pallas_call(kernel, out_shape=out_shape, in_specs=[whole()] * len(inpu...  8.04 us
    ppermute x1, waiting for transfers between devices, block(): received = lax.ppermute(tail, TILE, [(i, i + 1) for i in range(tiles - 1)])  5.52 us
    all_to_all x2, waiting for transfers between devices, exchange(): return lax.all_to_all(array, axis, split_axis=0, concat_axis=0, tiled=True)  5.3 us
    ppermute x1, starting transfers between devices, block(): received = lax.ppermute(tail, TILE, [(i, i + 1) for i in range(tiles - 1)])  4.5 us
    ppermute x1, starting transfers between devices, block(): other = lax.ppermute(source, 'yl', [(0, 1), (1, 0)])  3.83 us
  transfers between devices with their start and end apart: 9, of which 3 were waited for; matrix products, arithmetic and copies ran while one was open for 0% of the time, Pallas kernels for 5%

profile of v3, /device:TPU:256, one launch (start us, length us, event | category | flops | bytes accessed | tf_op | source)
XLA Modules:
  0.0 70.7 jit_solution(2219731019103012975)
XLA Ops:
  0.7 0.6 copy-done.7
  1.3 0.0 copy-done.8
  1.3 0.0 copy-done.5
  1.4 0.0 copy-done.6
  1.4 0.9 %copy-done = bf16[3,3,3,16,256]{4,3,2,1,0:T(8,128)(2,1)S(1)} copy-done((bf16[3,3,3,16,256]{4,3,2,1,0:T(8,128)(2,1)S(1)}, bf16[3,3,3,16,256]{4,3,2,1,0:T(8,128)(2,1)}, u32[]{:S(2)}) %copy-start) | copy-done | bytes 221208
  2.3 0.9 %copy-done.2 = bf16[1,17,4,4,256]{4,3,2,1,0:T(4,128)(2,1)S(1)} copy-done((bf16[1,17,4,4,256]{4,3,2,1,0:T(4,128)(2,1)S(1)}, bf16[1,17,4,4,256]{4,3,2,1,0:T(4,128)(2,1)}, u32[]{:S(2)}) %copy-start.2) | copy-done | bytes 139288
  3.2 1.3 %shard_map.92 = (bf16[16,15,16,128]{3,2,1,0:T(8,128)(2,1)}, f32[8,256]{1,0:T(8,128)S(1)}) custom-call(bf16[3,3,3,16,256]{4,3,2,1,0:T(8,128)(2,1)S(1)} %copy-done, bf16[17,4,4,256]{3,2,1,0:T(4,128)(2,1)S(1)} %bitcast.11, f32[1,256]{1,0:T(1,128)S(1)} %bitcast.18, f32[1,256]{1,0:T(1,128)S(1)} %bitcast.19, f32[1,256]{1,0:T(1,128)S(1)} %bitcast.20, ...), custom_call_target="tpu_custom_call" | custom-call | flops 400000000 | bytes 1048576 | tf_op jit(solution)/shard_map/pallas_call | solution.py:27
  4.5 5.5 %all-to-all-start = ((bf16[16,15,16,128]{3,2,1,0:T(8,128)(2,1)}), bf16[16,15,16,128]{3,2,1,0:T(8,128)(2,1)S(1)}, u32[]{:S(2)}, u32[]{:S(2)}) async-start(bf16[16,15,16,128]{3,2,1,0:T(8,128)(2,1)} %get-tuple-element.9), calls=%async_computation | async-start | bytes 1966080 | tf_op jit(solution)/shard_map/all_to_all | solution.py:279
  10.1 3.8 %collective-permute-start = (bf16[17,4,4,256]{3,2,1,0:T(4,128)(2,1)S(1)}, bf16[17,4,4,256]{3,2,1,0:T(4,128)(2,1)S(1)}, u32[]{:S(2)}, u32[]{:S(2)}) collective-permute-start(bf16[17,4,4,256]{3,2,1,0:T(4,128)(2,1)S(1)} %bitcast.12), channel_id=1, source_target_pairs={{0,2},{2,0},{1,3},{3,1},{4,6},{6,4},{5,7},{7,5},{8,10},{10,8},{9,1... | collective-permute-start | bytes 417800 | tf_op jit(solution)/shard_map/ppermute | solution.py:287
  13.9 0.7 collective-permute-start.1
  14.6 0.7 collective-permute-start.2
  15.3 5.3 %collective-permute-start.3 = (bf16[3,3,3,16,256]{4,3,2,1,0:T(8,128)(2,1)S(1)}, bf16[3,3,3,16,256]{4,3,2,1,0:T(8,128)(2,1)S(1)}, u32[]{:S(2)}, u32[]{:S(2)}) collective-permute-start(bf16[3,3,3,16,256]{4,3,2,1,0:T(8,128)(2,1)S(1)} %copy-done.1), channel_id=1, source_target_pairs={{0,4},{4,8},{8,12},{12,0},{1,5},{5,9},{9,13},{13,1},{2,6},{6,10},{... | collective-permute-start | bytes 663560 | tf_op jit(solution)/shard_map/ppermute | solution.py:303
  20.6 4.9 %collective-permute-start.4 = (bf16[3,3,3,16,256]{4,3,2,1,0:T(8,128)(2,1)S(1)}, bf16[3,3,3,16,256]{4,3,2,1,0:T(8,128)(2,1)S(1)}, u32[]{:S(2)}, u32[]{:S(2)}) collective-permute-start(bf16[3,3,3,16,256]{4,3,2,1,0:T(8,128)(2,1)S(1)} %copy-done.1), channel_id=1, source_target_pairs={{0,8},{4,12},{8,0},{12,4},{1,9},{5,13},{9,1},{13,5},{2,10},{6,14},... | collective-permute-start | bytes 663560 | tf_op jit(solution)/shard_map/ppermute | solution.py:303
  25.4 1.9 %collective-permute-done.other_ref = bf16[17,4,4,256]{3,2,1,0:T(4,128)(2,1)S(1)} collective-permute-done((bf16[17,4,4,256]{3,2,1,0:T(4,128)(2,1)S(1)}, bf16[17,4,4,256]{3,2,1,0:T(4,128)(2,1)S(1)}, u32[]{:S(2)}, u32[]{:S(2)}) %collective-permute-start) | collective-permute-done | bytes 139296 | tf_op jit(solution)/shard_map/ppermute | solution.py:287
  27.3 4.0 %collective-permute-start.5 = (bf16[3,3,3,16,256]{4,3,2,1,0:T(8,128)(2,1)S(1)}, bf16[3,3,3,16,256]{4,3,2,1,0:T(8,128)(2,1)S(1)}, u32[]{:S(2)}, u32[]{:S(2)}) collective-permute-start(bf16[3,3,3,16,256]{4,3,2,1,0:T(8,128)(2,1)S(1)} %copy-done.1), channel_id=1, source_target_pairs={{0,12},{4,0},{8,4},{12,8},{1,13},{5,1},{9,5},{13,9},{2,14},{6,2},{... | collective-permute-start | bytes 663560 | tf_op jit(solution)/shard_map/ppermute | solution.py:303
  31.4 2.4 %all-gather = bf16[6,17,4,4,256]{4,3,2,1,0:T(4,128)(2,1)S(1)} all-gather(bf16[3,17,4,4,256]{4,3,2,1,0:T(4,128)(2,1)S(1)} %shard_map.91), channel_id=2, replica_groups=mesh['z'=8,'yh'=4,'x'=4,'yl'=2,'core'=2] {'core'}, dimensions={0}, use_global_device_ids=true | all-gather | bytes 1253376 | tf_op jit(solution)/shard_map/all_gather | solution.py:300
  33.8 3.7 %shard_map.93 = (bf16[4,17,24,128]{3,2,1,0:T(8,128)(2,1)S(1)}, f32[4,8,128]{2,1,0:T(8,128)}) custom-call(bf16[2,3,17,4,4,256]{5,4,3,2,1,0:T(4,128)(2,1)S(1)} %bitcast.10, bf16[16,15,16,128]{3,2,1,0:T(8,128)(2,1)S(1)} %all-to-all-done.w_ref, f32[8,256]{1,0:T(8,128)S(1)} %get-tuple-element.10.vec_ref), custom_call_target="tpu_custom_call" | custom-call | flops 1600000000 | bytes 1048576 | tf_op jit(solution)/shard_map/pallas_call | solution.py:27
  37.6 3.3 %all-to-all-start.1 = ((f32[4,8,128]{2,1,0:T(8,128)}), f32[4,8,128]{2,1,0:T(8,128)S(1)}, u32[]{:S(2)}, u32[]{:S(2)}) async-start(f32[4,8,128]{2,1,0:T(8,128)} %get-tuple-element.12), calls=%async_computation.1 | async-start | bytes 32768 | tf_op jit(solution)/shard_map/all_to_all | solution.py:279
  40.9 5.3 %all-to-all-done.1.st_ref = f32[4,8,128]{2,1,0:T(8,128)S(1)} async-done(((f32[4,8,128]{2,1,0:T(8,128)}), f32[4,8,128]{2,1,0:T(8,128)S(1)}, u32[]{:S(2)}, u32[]{:S(2)}) %all-to-all-start.1) | async-done | bytes 16416 | tf_op jit(solution)/shard_map/all_to_all | solution.py:279
  46.2 2.2 %shard_map.94 = bf16[4,17,4,4,256]{4,3,2,1,0:T(4,128)(2,1)S(1)} custom-call(bf16[4,17,24,128]{3,2,1,0:T(8,128)(2,1)S(1)} %get-tuple-element.11.hid_ref, f32[4,8,128]{2,1,0:T(8,128)S(1)} %all-to-all-done.1.st_ref, bf16[3,3,3,16,256]{4,3,2,1,0:T(8,128)(2,1)S(1)} %copy-done.1, bf16[3,3,3,16,256]{4,3,2,1,0:T(8,128)(2,1)S(1)} %collective-permute-done.3.w1_ref, ...), custom_call_target="tpu_custom_call" | custom-call | flops 1600000000 | bytes 1048576 | tf_op jit(solution)/shard_map/pallas_call | solution.py:27
  48.3 11.5 %all_to_all.15.part_ref.main_ref = bf16[4,17,4,4,256]{4,3,2,1,0:T(4,128)(2,1)S(1)} all-to-all(bf16[4,17,4,4,256]{4,3,2,1,0:T(4,128)(2,1)S(1)} %shard_map.94), channel_id=1, replica_groups=mesh['z'=8,'yh'=4,'x'=4,'yl'=2,'core'=2] {'yl','core'}, dimensions={0} | all-to-all | bytes 1114112 | tf_op jit(solution)/shard_map/all_to_all | solution.py:279
  59.9 4.5 %collective-permute-start.6 = (bf16[4,4,4,256]{3,2,1,0:T(4,128)(2,1)S(1)}, bf16[4,4,4,256]{3,2,1,0:T(4,128)(2,1)S(1)}, u32[]{:S(2)}, u32[]{:S(2)}) collective-permute-start(bf16[4,4,4,256]{3,2,1,0:T(4,128)(2,1)S(1)} %shard_map.95.tail_ref), channel_id=1, source_target_pairs={{0,16},{16,32},{32,48},{48,64},{64,80},{80,96},{96,112},{112,128},... | collective-permute-start | bytes 98312 | tf_op jit(solution)/shard_map/ppermute | solution.py:322
  64.4 5.5 %collective-permute-done.6.received_ref = bf16[4,4,4,256]{3,2,1,0:T(4,128)(2,1)S(1)} collective-permute-done((bf16[4,4,4,256]{3,2,1,0:T(4,128)(2,1)S(1)}, bf16[4,4,4,256]{3,2,1,0:T(4,128)(2,1)S(1)}, u32[]{:S(2)}, u32[]{:S(2)}) %collective-permute-start.6) | collective-permute-done | bytes 32800 | tf_op jit(solution)/shard_map/ppermute | solution.py:322
  69.9 0.8 %shard_map.96 = bf16[17,4,4,256]{3,2,1,0:T(4,128)(2,1)} custom-call(bf16[4,17,4,4,256]{4,3,2,1,0:T(4,128)(2,1)S(1)} %all_to_all.15.part_ref.main_ref, bf16[4,4,4,256]{3,2,1,0:T(4,128)(2,1)S(1)} %shard_map.95.tail_ref, bf16[17,4,4,256]{3,2,1,0:T(4,128)(2,1)S(1)} %bitcast.17, f32[8,256]{1,0:T(8,128)S(1)} %get-tuple-element.10.vec_ref, ...), custom_call_target="tpu_custom_call" | custom-call | flops 400000000 | bytes 1048576 | tf_op jit(solution)/shard_map/pallas_call | solution.py:27
  (20 shorter events, 0.1 us)
Async XLA Ops:
  0.7 0.7 copy-start.7
  0.7 0.7 copy-start.8
  0.7 0.7 copy-start.5
  0.7 0.7 copy-start.6
  0.7 0.7 copy-start.4
  1.4 0.9 %copy-start = (bf16[3,3,3,16,256]{4,3,2,1,0:T(8,128)(2,1)S(1)}, bf16[3,3,3,16,256]{4,3,2,1,0:T(8,128)(2,1)}, u32[]{:S(2)}) copy-start(bf16[3,3,3,16,256]{4,3,2,1,0:T(8,128)(2,1)} %w_ref.1) | copy-start | bytes 663556
  2.3 0.9 %copy-start.2 = (bf16[1,17,4,4,256]{4,3,2,1,0:T(4,128)(2,1)S(1)}, bf16[1,17,4,4,256]{4,3,2,1,0:T(4,128)(2,1)}, u32[]{:S(2)}) copy-start(bf16[1,17,4,4,256]{4,3,2,1,0:T(4,128)(2,1)} %param.9) | copy-start | bytes 417796
  4.5 5.6 %copy-start.3 = (bf16[1,17,4,4,256]{4,3,2,1,0:T(4,128)(2,1)S(1)}, bf16[1,17,4,4,256]{4,3,2,1,0:T(4,128)(2,1)}, u32[]{:S(2)}) copy-start(bf16[1,17,4,4,256]{4,3,2,1,0:T(4,128)(2,1)} %param.9) | copy-start | bytes 417796
  4.5 10.8 %copy-start.1 = (bf16[3,3,3,16,256]{4,3,2,1,0:T(8,128)(2,1)S(1)}, bf16[3,3,3,16,256]{4,3,2,1,0:T(8,128)(2,1)}, u32[]{:S(2)}) copy-start(bf16[3,3,3,16,256]{4,3,2,1,0:T(8,128)(2,1)} %w0_ref.1) | copy-start | bytes 663556
  4.5 29.3 %all-to-all-start = ((bf16[16,15,16,128]{3,2,1,0:T(8,128)(2,1)}), bf16[16,15,16,128]{3,2,1,0:T(8,128)(2,1)S(1)}, u32[]{:S(2)}, u32[]{:S(2)}) async-start(bf16[16,15,16,128]{3,2,1,0:T(8,128)(2,1)} %get-tuple-element.9), calls=%async_computation | async-start | bytes 1966080 | tf_op jit(solution)/shard_map/all_to_all | solution.py:279
  10.1 17.2 %collective-permute-start = (bf16[17,4,4,256]{3,2,1,0:T(4,128)(2,1)S(1)}, bf16[17,4,4,256]{3,2,1,0:T(4,128)(2,1)S(1)}, u32[]{:S(2)}, u32[]{:S(2)}) collective-permute-start(bf16[17,4,4,256]{3,2,1,0:T(4,128)(2,1)S(1)} %bitcast.12), channel_id=1, source_target_pairs={{0,2},{2,0},{1,3},{3,1},{4,6},{6,4},{5,7},{7,5},{8,10},{10,8},{9,1... | collective-permute-start | bytes 417800 | tf_op jit(solution)/shard_map/ppermute | solution.py:287
  13.9 17.4 %collective-permute-start.1 = (bf16[17,4,4,256]{3,2,1,0:T(4,128)(2,1)S(1)}, bf16[17,4,4,256]{3,2,1,0:T(4,128)(2,1)S(1)}, u32[]{:S(2)}, u32[]{:S(2)}) collective-permute-start(bf16[17,4,4,256]{3,2,1,0:T(4,128)(2,1)S(1)} %bitcast.13), channel_id=1, source_target_pairs={{3,4},{4,3},{7,8},{8,7},{11,12},{12,11},{19,20},{20,19},{23,24},{2... | collective-permute-start | bytes 417800 | tf_op jit(solution)/shard_map/ppermute | solution.py:290
  14.6 16.8 %collective-permute-start.2 = (bf16[17,4,4,256]{3,2,1,0:T(4,128)(2,1)S(1)}, bf16[17,4,4,256]{3,2,1,0:T(4,128)(2,1)S(1)}, u32[]{:S(2)}, u32[]{:S(2)}) collective-permute-start(bf16[17,4,4,256]{3,2,1,0:T(4,128)(2,1)S(1)} %bitcast.14), channel_id=1, source_target_pairs={{3,6},{4,1},{7,10},{8,5},{11,14},{12,9},{19,22},{20,17},{23,26},{2... | collective-permute-start | bytes 417800 | tf_op jit(solution)/shard_map/ppermute | solution.py:291
  15.3 25.6 %collective-permute-start.3 = (bf16[3,3,3,16,256]{4,3,2,1,0:T(8,128)(2,1)S(1)}, bf16[3,3,3,16,256]{4,3,2,1,0:T(8,128)(2,1)S(1)}, u32[]{:S(2)}, u32[]{:S(2)}) collective-permute-start(bf16[3,3,3,16,256]{4,3,2,1,0:T(8,128)(2,1)S(1)} %copy-done.1), channel_id=1, source_target_pairs={{0,4},{4,8},{8,12},{12,0},{1,5},{5,9},{9,13},{13,1},{2,6},{6,10},{... | collective-permute-start | bytes 663560 | tf_op jit(solution)/shard_map/ppermute | solution.py:303
  20.6 20.3 %collective-permute-start.4 = (bf16[3,3,3,16,256]{4,3,2,1,0:T(8,128)(2,1)S(1)}, bf16[3,3,3,16,256]{4,3,2,1,0:T(8,128)(2,1)S(1)}, u32[]{:S(2)}, u32[]{:S(2)}) collective-permute-start(bf16[3,3,3,16,256]{4,3,2,1,0:T(8,128)(2,1)S(1)} %copy-done.1), channel_id=1, source_target_pairs={{0,8},{4,12},{8,0},{12,4},{1,9},{5,13},{9,1},{13,5},{2,10},{6,14},... | collective-permute-start | bytes 663560 | tf_op jit(solution)/shard_map/ppermute | solution.py:303
  27.3 13.6 %collective-permute-start.5 = (bf16[3,3,3,16,256]{4,3,2,1,0:T(8,128)(2,1)S(1)}, bf16[3,3,3,16,256]{4,3,2,1,0:T(8,128)(2,1)S(1)}, u32[]{:S(2)}, u32[]{:S(2)}) collective-permute-start(bf16[3,3,3,16,256]{4,3,2,1,0:T(8,128)(2,1)S(1)} %copy-done.1), channel_id=1, source_target_pairs={{0,12},{4,0},{8,4},{12,8},{1,13},{5,1},{9,5},{13,9},{2,14},{6,2},{... | collective-permute-start | bytes 663560 | tf_op jit(solution)/shard_map/ppermute | solution.py:303
  37.6 8.6 %all-to-all-start.1 = ((f32[4,8,128]{2,1,0:T(8,128)}), f32[4,8,128]{2,1,0:T(8,128)S(1)}, u32[]{:S(2)}, u32[]{:S(2)}) async-start(f32[4,8,128]{2,1,0:T(8,128)} %get-tuple-element.12), calls=%async_computation.1 | async-start | bytes 32768 | tf_op jit(solution)/shard_map/all_to_all | solution.py:279
  59.9 10.0 %collective-permute-start.6 = (bf16[4,4,4,256]{3,2,1,0:T(4,128)(2,1)S(1)}, bf16[4,4,4,256]{3,2,1,0:T(4,128)(2,1)S(1)}, u32[]{:S(2)}, u32[]{:S(2)}) collective-permute-start(bf16[4,4,4,256]{3,2,1,0:T(4,128)(2,1)S(1)} %shard_map.95.tail_ref), channel_id=1, source_target_pairs={{0,16},{16,32},{32,48},{48,64},{64,80},{80,96},{96,112},{112,128},... | collective-permute-start | bytes 98312 | tf_op jit(solution)/shard_map/ppermute | solution.py:322

commit v4 on v3

--- a/solution.py
+++ b/solution.py
@@ -73,17 +73,34 @@
     return v * (0.5 * jnp.tanh(0.5 * v) + 0.5)
 
 
-def pack_kernel(w_ref, latent_ref, g1_ref, s1_ref, g2_ref, s2_ref, b_ref, n_ref, out_ref, vec_ref):
-    for i, ref in enumerate((g1_ref, s1_ref, g2_ref, s2_ref, b_ref)):
-        vec_ref[i : i + 1] = ref[...]
-    vec_ref[5:6] = jnp.broadcast_to(n_ref[...].astype(F32), (1, C))
-    vec_ref[6:8] = jnp.zeros((2, C), F32)
-    total, squares = jnp.zeros((4, C), F32), jnp.zeros((4, C), F32)
-    for t in range(T):
-        for h in range(H):
+def pack_kernel(
+    w_hbm, latent_hbm, g1, s1, g2, s2, b, out_ref, vec_ref, w_ref, latent_ref, line, sems
+):
+    copies = [
+        pltpu.make_async_copy(source, target, sems.at[i])
+        for i, (source, target) in enumerate(
+            [(latent_hbm, latent_ref), (w_hbm, w_ref)]
+            + [(source, line.at[i]) for i, source in enumerate((g1, s1, g2, s2, b))]
+        )
+    ]
+    for copy in copies:
+        copy.start()
+    for copy in copies:
+        copy.wait()
+    for i in range(5):
+        vec_ref[i : i + 1] = line[i]
+    vec_ref[5:8] = jnp.zeros((3, C), F32)
+    totals, powers = [], []
+    for h in range(H):
+        total, squares = jnp.zeros((4, C), F32), jnp.zeros((4, C), F32)
+        for t in range(T):
             v = latent_ref[t, h].astype(F32)
             total += v
             squares += v * v
+        totals.append(total)
+        powers.append(squares)
+    total = (totals[0] + totals[1]) + (totals[2] + totals[3])
+    squares = (powers[0] + powers[1]) + (powers[2] + powers[3])
     pieces = []
     for value in (total, squares):
         for piece in split3(jnp.sum(value, axis=0, keepdims=True)):
@@ -198,7 +215,9 @@
         st_ref[d] = stats
 
 
-def conv_two_kernel(hid_ref, st_ref, w0_ref, w1_ref, w2_ref, w3_ref, vec_ref, part_ref, act, wm):
+def conv_two_kernel(hid_ref, st_ref, w0_ref, w1_ref, w2_ref, w3_ref, vec_ref, *outs):
+    *parts, act, wm = outs
+    tails, mains = parts[:4], parts[4:]
     me = lax.axis_index("x")
     j = 2 * lax.axis_index("yl") + lax.axis_index("core")
     for step, w_ref in enumerate((w0_ref, w1_ref, w2_ref, w3_ref)):
@@ -221,6 +240,8 @@
     row = rows((ROW, 128))
     inside = (row >= jnp.where(me == 0, 4, 0)) & (row < jnp.where(me == 3, 20, ROW))
     left = lanes((16, 128)) < 64
+    place = jnp.full((8, 128), j, jnp.int32)
+    odd, upper = (place & 1) != 0, (place & 2) != 0
     act[:, 0:2] = jnp.zeros((4, 2, 16, C), BF16)
 
     def frame(t, _):
@@ -229,8 +250,11 @@
             y = silu((v - mean) * scale + shift)
             y = jnp.where(inside, y, 0.0)
             a0, a1, a2 = (pltpu.roll(y, ROW - 3 - dw, 0)[0:16] for dw in range(3))
-            act[h, t + 2, :, 0:128] = jnp.where(left, a0, a1).astype(BF16)
-            act[h, t + 2, :, 128:256] = jnp.where(left, a2, 0.0).astype(BF16)
+            for at, tile in ((0, jnp.where(left, a0, a1)), (128, jnp.where(left, a2, 0.0))):
+                low, high = jnp.where(upper, tile[8:16], tile[0:8]), jnp.where(upper, tile[0:8], tile[8:16])
+                low = jnp.where(odd, pltpu.roll(low, 4, 0), low)
+                high = jnp.where(odd, pltpu.roll(high, 4, 0), high)
+                act[h, t + 2, :, at : at + 128] = jnp.concatenate([low, high], axis=0).astype(BF16)
         return 0
 
     lax.fori_loop(0, T, frame, 0)
@@ -242,28 +266,32 @@
         rhs = wm[3 * taps[0] : 3 * taps[-1] + 3].reshape(-1, C)
         y = jnp.dot(lhs, rhs, preferred_element_type=F32).reshape(T, 16, C)
         for d in range(4):
-            part_ref[d, :, h] = y[:, 4 * d : 4 * d + 4].astype(BF16)
-
-
-def decode(part_ref, at, latent, bias):
-    branch = part_ref[0, at].astype(F32)
-    for q in range(1, 4):
-        branch = branch + part_ref[q, at].astype(F32)
+            columns = y[:, 4 * d : 4 * d + 4].astype(mains[d].dtype)
+            mains[d][:, h] = columns[: T - OVMAX]
+            tails[d][:, h] = columns[T - OVMAX :]
+
+
+def decode(parts, at, latent, bias):
+    branch = parts[0][at]
+    for part in parts[1:]:
+        branch = branch + part[at].astype(F32)
     return (latent.astype(F32) + (branch + bias)).astype(BF16)
 
 
-def tail_kernel(part_ref, latent_ref, vec_ref, tail_ref):
+def tail_kernel(*refs):
+    *parts, latent_ref, vec_ref, tail_ref = refs
     for i in range(OVMAX):
-        tail_ref[i] = decode(part_ref, T - OVMAX + i, latent_ref[T - OVMAX + i], vec_ref[4:5])
-
-
-def blend_kernel(main_ref, tail_ref, latent_ref, vec_ref, received_ref, out_ref):
-    bias, shared = vec_ref[4:5], vec_ref[5:6]
+        tail_ref[i] = decode(parts, i, latent_ref[T - OVMAX + i], vec_ref[4:5])
+
+
+def blend_kernel(*refs):
+    *parts, tail_ref, latent_ref, vec_ref, shared_ref, received_ref, out_ref = refs
+    bias, shared = vec_ref[4:5], shared_ref[...]
     for t in range(T):
         if t >= T - OVMAX:
             out_ref[t] = tail_ref[t - T + OVMAX]
             continue
-        own = decode(main_ref, t, latent_ref[t], bias)
+        own = decode(parts, t, latent_ref[t], bias)
         if t < OVMAX:
             other = received_ref[OVMAX - 1].astype(F32)
             for n in range(t + 2, OVMAX + 1):
@@ -284,18 +312,27 @@
     flat = lambda v: v.reshape(1, C)
     sds = jax.ShapeDtypeStruct
     vectors = tuple(flat(v) for v in (gain_one, shift_one, gain_two, shift_two, bias))
+    packed, vec = pl.pallas_call(
+        pack_kernel,
+        out_shape=(sds((16, 15, 16, 128), BF16), sds((8, C), F32)),
+        in_specs=[pl.BlockSpec(memory_space=pl.ANY)] * 7,
+        out_specs=(whole(), whole()),
+        scratch_shapes=[
+            pltpu.VMEM(weight_one.shape, BF16),
+            pltpu.VMEM(source.shape, BF16),
+            pltpu.VMEM((5, 1, C), F32),
+            pltpu.SemaphoreType.DMA((7,)),
+        ],
+        compiler_params=pltpu.CompilerParams(vmem_limit_bytes=67043328),
+        cost_estimate=cost(1),
+    )(weight_one, source, *vectors)
+    kernel_one = exchange(packed, COL)
     other = lax.ppermute(source, "yl", [(0, 1), (1, 0)])
     near = [p for x in range(3) for p in ((4 * x + 3, 4 * x + 4), (4 * x + 4, 4 * x + 3))]
     far = [p for x in range(3) for p in ((4 * x + 3, 4 * x + 6), (4 * x + 4, 4 * x + 1))]
     near = lax.ppermute(source, COL, near)
     far = lax.ppermute(source, COL, far)
-    packed, vec = call(
-        pack_kernel,
-        (weight_one, source, *vectors, intersections.reshape(1, 1)),
-        (sds((16, 15, 16, 128), BF16), sds((8, C), F32)),
-        cost=cost(1),
-    )
-    kernel_one = exchange(packed, COL)
+    shared = jnp.broadcast_to(intersections.astype(F32).reshape(1, 1), (1, C))
     joined = call(join_kernel, (source, other, near, far), sds((3, T, 4, 4, C), BF16), cost=cost(1))
     wide = lax.all_gather(joined, "core", axis=0, tiled=False)
     kernel_two = [weight_two]
@@ -309,18 +346,22 @@
         cost=cost(4),
     )
     stats = exchange(stats, "x")
-    part = call(
+    kinds = (F32, BF16, BF16, BF16)
+    parts = call(
         conv_two_kernel,
         (hidden, stats, *kernel_two, vec),
-        sds((4, T, 4, 4, C), BF16),
+        tuple(sds((n, 4, 4, C), kind) for n in (OVMAX, T - OVMAX) for kind in kinds),
         (pltpu.VMEM((4, T + 2, 16, C), BF16), pltpu.VMEM((9, C, C), BF16)),
         cost=cost(4),
     )
-    part = exchange(part, JAX_)
-    tail = call(tail_kernel, (part, source, vec), sds((OVMAX, 4, 4, C), BF16), cost=cost(1))
+    tails, mains = list(parts[:4]), list(parts[4:])
+    for arrays in (tails, mains):
+        for k in range(1, 4):
+            arrays[k] = lax.ppermute(arrays[k], JAX_, [(i, i ^ k) for i in range(4)])
+    tail = call(tail_kernel, (*tails, source, vec), sds((OVMAX, 4, 4, C), BF16), cost=cost(1))
     tiles = lax.axis_size(TILE)
     received = lax.ppermute(tail, TILE, [(i, i + 1) for i in range(tiles - 1)])
-    out = call(blend_kernel, (part, tail, source, vec, received), sds((T, 4, 4, C), BF16), cost=cost(1))
+    out = call(blend_kernel, (*mains, tail, source, vec, shared, received), sds((T, 4, 4, C), BF16), cost=cost(1))
     return out[None]
 
 

time: 71.3 us -> 74.3 us (1.042)
  starting transfers between devices: 32.6 us -> 48.1 us
  blocking collectives: 13.9 us -> 2.4 us
  local copies, waits for them, and re-layouts: 2.55 us -> 0.02 us
  Pallas kernels: 8.04 us -> 9.21 us
    ppermute x0 -> x6, starting transfers between devices: none -> 15.5 us  [block(): arrays[k] = lax.ppermute(arrays[k], JAX_, [(i, i ^ k) for i in range(4)])]
    all_to_all x1 -> x0, blocking collectives: 11.5 us -> none  [exchange(): return lax.all_to_all(array, axis, split_axis=0, concat_axis=0, tiled=True)]
    unnamed x18 -> x6, local copies, waits for them, and re-layouts: 2.55 us -> 0.02 us
    pallas_call x0 -> x1, Pallas kernels: none -> 2.34 us  [block(): pl.pallas_call(pack_kernel, out_shape=(sds((16, 15, 16, 128), BF16), sds(...]
    pallas_call x6 -> x5, Pallas kernels: 8.04 us -> 6.87 us  [call(): pl.pallas_call(kernel, out_shape=out_shape, in_specs=[whole()] * len(inpu...]
    ppermute x0 -> x6, waiting for transfers between devices: none -> 0.97 us  [block(): arrays[k] = lax.ppermute(arrays[k], JAX_, [(i, i ^ k) for i in range(4)])]
  transfers between devices with their start and end apart: 9 -> 15, of which waited for: 3 -> 4; matrix products, arithmetic and copies ran while one was open for 0% -> 0% of each run, Pallas kernels for 5% -> 5%
where the time goes in v4:
time: 74.3 us; the launch traced here: 73.7 us
  starting transfers between devices  48.1 us (65%)
  waiting for transfers between devices  13 us (17%)
  Pallas kernels  9.21 us (12%)
  blocking collectives  2.4 us (3%)
  between operations  0.9 us (1%)
    ppermute x6, starting transfers between devices, block(): arrays[k] = lax.ppermute(arrays[k], JAX_, [(i, i ^ k) for i in range(4)])  15.5 us
    ppermute x3, starting transfers between devices, block(): lax.ppermute(weight_two, 'x', [(x, (x + step) % 4) for x in range(4)])  14.2 us
    all_to_all x2, starting transfers between devices, exchange(): return lax.all_to_all(array, axis, split_axis=0, concat_axis=0, tiled=True)  8.81 us
    pallas_call x5, Pallas kernels, call(): pl.pallas_call(kernel, out_shape=out_shape, in_specs=[whole()] * len(inpu...  6.87 us
    all_to_all x2, waiting for transfers between devices, exchange(): return lax.all_to_all(array, axis, split_axis=0, concat_axis=0, tiled=True)  5.3 us
    ppermute x1, waiting for transfers between devices, block(): received = lax.ppermute(tail, TILE, [(i, i + 1) for i in range(tiles - 1)])  4.87 us
    ppermute x1, starting transfers between devices, block(): received = lax.ppermute(tail, TILE, [(i, i + 1) for i in range(tiles - 1)])  4.5 us
    ppermute x1, starting transfers between devices, block(): other = lax.ppermute(source, 'yl', [(0, 1), (1, 0)])  3.83 us
  transfers between devices with their start and end apart: 15, of which 4 were waited for; matrix products, arithmetic and copies ran while one was open for 0% of the time, Pallas kernels for 5%

profile of v4, /device:TPU:256, one launch (start us, length us, event | category | flops | bytes accessed | tf_op | source)
XLA Modules:
  0.0 73.7 jit_solution(12810566367380602366)
XLA Ops:
  0.0 2.3 %shard_map.92 = (bf16[16,15,16,128]{3,2,1,0:T(8,128)(2,1)}, f32[8,256]{1,0:T(8,128)}) custom-call(bf16[3,3,3,16,256]{4,3,2,1,0:T(8,128)(2,1)} %w_hbm.1, bf16[17,4,4,256]{3,2,1,0:T(4,128)(2,1)} %bitcast.10, f32[1,256]{1,0:T(1,128)} %bitcast.17, f32[1,256]{1,0:T(1,128)} %bitcast.18, f32[1,256]{1,0:T(1,128)} %bitcast.19, f32[1,256]{1,0:T(1,128)} %bitcast.20, ...), custom_call_target="tpu_custom_call" | custom-call | flops 400000000 | bytes 1048576 | tf_op jit(solution)/shard_map/pallas_call | solution.py:315
  2.4 5.6 %all-to-all-start = ((bf16[16,15,16,128]{3,2,1,0:T(8,128)(2,1)}), bf16[16,15,16,128]{3,2,1,0:T(8,128)(2,1)S(1)}, u32[]{:S(2)}, u32[]{:S(2)}) async-start(bf16[16,15,16,128]{3,2,1,0:T(8,128)(2,1)} %get-tuple-element.17), calls=%async_computation | async-start | bytes 1966080 | tf_op jit(solution)/shard_map/all_to_all | solution.py:307
  8.0 3.8 %collective-permute-start = (bf16[17,4,4,256]{3,2,1,0:T(4,128)(2,1)S(1)}, bf16[17,4,4,256]{3,2,1,0:T(4,128)(2,1)S(1)}, u32[]{:S(2)}, u32[]{:S(2)}) collective-permute-start(bf16[17,4,4,256]{3,2,1,0:T(4,128)(2,1)S(1)} %bitcast.11), channel_id=1, source_target_pairs={{0,2},{2,0},{1,3},{3,1},{4,6},{6,4},{5,7},{7,5},{8,10},{10,8},{9,1... | collective-permute-start | bytes 417800 | tf_op jit(solution)/shard_map/ppermute | solution.py:330
  11.8 0.7 collective-permute-start.1
  12.5 0.7 collective-permute-start.2
  13.2 5.3 %collective-permute-start.3 = (bf16[3,3,3,16,256]{4,3,2,1,0:T(8,128)(2,1)S(1)}, bf16[3,3,3,16,256]{4,3,2,1,0:T(8,128)(2,1)S(1)}, u32[]{:S(2)}, u32[]{:S(2)}) collective-permute-start(bf16[3,3,3,16,256]{4,3,2,1,0:T(8,128)(2,1)S(1)} %copy-done), channel_id=1, source_target_pairs={{0,4},{4,8},{8,12},{12,0},{1,5},{5,9},{9,13},{13,1},{2,6},{6,10},{... | collective-permute-start | bytes 663560 | tf_op jit(solution)/shard_map/ppermute | solution.py:340
  18.4 4.9 %collective-permute-start.4 = (bf16[3,3,3,16,256]{4,3,2,1,0:T(8,128)(2,1)S(1)}, bf16[3,3,3,16,256]{4,3,2,1,0:T(8,128)(2,1)S(1)}, u32[]{:S(2)}, u32[]{:S(2)}) collective-permute-start(bf16[3,3,3,16,256]{4,3,2,1,0:T(8,128)(2,1)S(1)} %copy-done), channel_id=1, source_target_pairs={{0,8},{4,12},{8,0},{12,4},{1,9},{5,13},{9,1},{13,5},{2,10},{6,14},... | collective-permute-start | bytes 663560 | tf_op jit(solution)/shard_map/ppermute | solution.py:340
  23.3 1.9 %collective-permute-done.other_ref = bf16[17,4,4,256]{3,2,1,0:T(4,128)(2,1)S(1)} collective-permute-done((bf16[17,4,4,256]{3,2,1,0:T(4,128)(2,1)S(1)}, bf16[17,4,4,256]{3,2,1,0:T(4,128)(2,1)S(1)}, u32[]{:S(2)}, u32[]{:S(2)}) %collective-permute-start) | collective-permute-done | bytes 139296 | tf_op jit(solution)/shard_map/ppermute | solution.py:330
  25.2 4.0 %collective-permute-start.5 = (bf16[3,3,3,16,256]{4,3,2,1,0:T(8,128)(2,1)S(1)}, bf16[3,3,3,16,256]{4,3,2,1,0:T(8,128)(2,1)S(1)}, u32[]{:S(2)}, u32[]{:S(2)}) collective-permute-start(bf16[3,3,3,16,256]{4,3,2,1,0:T(8,128)(2,1)S(1)} %copy-done), channel_id=1, source_target_pairs={{0,12},{4,0},{8,4},{12,8},{1,13},{5,1},{9,5},{13,9},{2,14},{6,2},{... | collective-permute-start | bytes 663560 | tf_op jit(solution)/shard_map/ppermute | solution.py:340
  29.3 2.4 %all-gather = bf16[6,17,4,4,256]{4,3,2,1,0:T(4,128)(2,1)S(1)} all-gather(bf16[3,17,4,4,256]{4,3,2,1,0:T(4,128)(2,1)S(1)} %shard_map.91), channel_id=2, replica_groups=mesh['z'=8,'yh'=4,'x'=4,'yl'=2,'core'=2] {'core'}, dimensions={0}, use_global_device_ids=true | all-gather | bytes 1253376 | tf_op jit(solution)/shard_map/all_gather | solution.py:337
  31.7 3.7 %shard_map.93 = (bf16[4,17,24,128]{3,2,1,0:T(8,128)(2,1)S(1)}, f32[4,8,128]{2,1,0:T(8,128)}) custom-call(bf16[2,3,17,4,4,256]{5,4,3,2,1,0:T(4,128)(2,1)S(1)} %bitcast.9, bf16[16,15,16,128]{3,2,1,0:T(8,128)(2,1)S(1)} %all-to-all-done.w_ref, f32[8,256]{1,0:T(8,128)S(1)} %copy-done.2), custom_call_target="tpu_custom_call" | custom-call | flops 1600000000 | bytes 1048576 | tf_op jit(solution)/shard_map/pallas_call | solution.py:27
  35.5 3.3 %all-to-all-start.1 = ((f32[4,8,128]{2,1,0:T(8,128)}), f32[4,8,128]{2,1,0:T(8,128)S(1)}, u32[]{:S(2)}, u32[]{:S(2)}) async-start(f32[4,8,128]{2,1,0:T(8,128)} %get-tuple-element.20), calls=%async_computation.1 | async-start | bytes 32768 | tf_op jit(solution)/shard_map/all_to_all | solution.py:307
  38.8 5.3 %all-to-all-done.1.st_ref = f32[4,8,128]{2,1,0:T(8,128)S(1)} async-done(((f32[4,8,128]{2,1,0:T(8,128)}), f32[4,8,128]{2,1,0:T(8,128)S(1)}, u32[]{:S(2)}, u32[]{:S(2)}) %all-to-all-start.1) | async-done | bytes 16416 | tf_op jit(solution)/shard_map/all_to_all | solution.py:307
  44.0 2.3 %shard_map.94 = (f32[4,4,4,256]{3,2,1,0:T(4,128)S(1)}, bf16[4,4,4,256]{3,2,1,0:T(4,128)(2,1)S(1)}, bf16[4,4,4,256]{3,2,1,0:T(4,128)(2,1)S(1)}, bf16[4,4,4,256]{3...) custom-call(bf16[4,17,24,128]{3,2,1,0:T(8,128)(2,1)S(1)} %get-tuple-, ...), custom_call_target="tpu_custom_call" | custom-call | flops 1600000000 | bytes 1048576 | tf_op jit(solution)/shard_map/pallas_call | solution.py:27
  46.3 2.5 %collective-permute-start.10 = (bf16[4,4,4,256]{3,2,1,0:T(4,128)(2,1)S(1)}, bf16[4,4,4,256]{3,2,1,0:T(4,128)(2,1)S(1)}, u32[]{:S(2)}, u32[]{:S(2)}) collective-permute-start(bf16[4,4,4,256]{3,2,1,0:T(4,128)(2,1)S(1)} %get-tuple-element.27), channel_id=1, source_target_pairs={{0,2},{1,3},{2,0},{3,1},{4,6},{5,7},{6,4},{7,5},{8,10},{9,11},{10,... | collective-permute-start | bytes 98312 | tf_op jit(solution)/shard_map/ppermute | solution.py:360
  48.8 1.9 %collective-permute-start.6 = (bf16[13,4,4,256]{3,2,1,0:T(4,128)(2,1)S(1)}, bf16[13,4,4,256]{3,2,1,0:T(4,128)(2,1)S(1)}, u32[]{:S(2)}, u32[]{:S(2)}) collective-permute-start(bf16[13,4,4,256]{3,2,1,0:T(4,128)(2,1)S(1)} %get-tuple-element.22), channel_id=1, source_target_pairs={{0,1},{1,0},{2,3},{3,2},{4,5},{5,4},{6,7},{7,6},{8,9},{9,8},{10,11... | collective-permute-start | bytes 319496 | tf_op jit(solution)/shard_map/ppermute | solution.py:360
  50.7 3.4 %collective-permute-start.7 = (bf16[13,4,4,256]{3,2,1,0:T(4,128)(2,1)S(1)}, bf16[13,4,4,256]{3,2,1,0:T(4,128)(2,1)S(1)}, u32[]{:S(2)}, u32[]{:S(2)}) collective-permute-start(bf16[13,4,4,256]{3,2,1,0:T(4,128)(2,1)S(1)} %get-tuple-element.23), channel_id=1, source_target_pairs={{0,2},{1,3},{2,0},{3,1},{4,6},{5,7},{6,4},{7,5},{8,10},{9,11},{10,... | collective-permute-start | bytes 319496 | tf_op jit(solution)/shard_map/ppermute | solution.py:360
  54.1 2.3 %collective-permute-start.8 = (bf16[13,4,4,256]{3,2,1,0:T(4,128)(2,1)S(1)}, bf16[13,4,4,256]{3,2,1,0:T(4,128)(2,1)S(1)}, u32[]{:S(2)}, u32[]{:S(2)}) collective-permute-start(bf16[13,4,4,256]{3,2,1,0:T(4,128)(2,1)S(1)} %get-tuple-element.24), channel_id=1, source_target_pairs={{0,3},{1,2},{2,1},{3,0},{4,7},{5,6},{6,5},{7,4},{8,11},{9,10},{10,... | collective-permute-start | bytes 319496 | tf_op jit(solution)/shard_map/ppermute | solution.py:360
  56.4 3.3 %collective-permute-start.11 = (bf16[4,4,4,256]{3,2,1,0:T(4,128)(2,1)S(1)}, bf16[4,4,4,256]{3,2,1,0:T(4,128)(2,1)S(1)}, u32[]{:S(2)}, u32[]{:S(2)}) collective-permute-start(bf16[4,4,4,256]{3,2,1,0:T(4,128)(2,1)S(1)} %get-tuple-element.28), channel_id=1, source_target_pairs={{0,3},{1,2},{2,1},{3,0},{4,7},{5,6},{6,5},{7,4},{8,11},{9,10},{10,... | collective-permute-start | bytes 98312 | tf_op jit(solution)/shard_map/ppermute | solution.py:360
  59.7 2.1 %collective-permute-start.9 = (bf16[4,4,4,256]{3,2,1,0:T(4,128)(2,1)S(1)}, bf16[4,4,4,256]{3,2,1,0:T(4,128)(2,1)S(1)}, u32[]{:S(2)}, u32[]{:S(2)}) collective-permute-start(bf16[4,4,4,256]{3,2,1,0:T(4,128)(2,1)S(1)} %get-tuple-element.26), channel_id=1, source_target_pairs={{0,1},{1,0},{2,3},{3,2},{4,5},{5,4},{6,7},{7,6},{8,9},{9,8},{10,11... | collective-permute-start | bytes 98312 | tf_op jit(solution)/shard_map/ppermute | solution.py:360
  61.8 1.0 %collective-permute-done.9.refs_1_ = bf16[4,4,4,256]{3,2,1,0:T(4,128)(2,1)S(1)} collective-permute-done((bf16[4,4,4,256]{3,2,1,0:T(4,128)(2,1)S(1)}, bf16[4,4,4,256]{3,2,1,0:T(4,128)(2,1)S(1)}, u32[]{:S(2)}, u32[]{:S(2)}) %collective-permute-start.9) | collective-permute-done | bytes 32800 | tf_op jit(solution)/shard_map/ppermute | solution.py:360
  62.8 4.5 %collective-permute-start.12 = (bf16[4,4,4,256]{3,2,1,0:T(4,128)(2,1)S(1)}, bf16[4,4,4,256]{3,2,1,0:T(4,128)(2,1)S(1)}, u32[]{:S(2)}, u32[]{:S(2)}) collective-permute-start(bf16[4,4,4,256]{3,2,1,0:T(4,128)(2,1)S(1)} %shard_map.95.refs_4_), channel_id=1, source_target_pairs={{0,16},{16,32},{32,48},{48,64},{64,80},{80,96},{96,112},{112,128},... | collective-permute-start | bytes 98312 | tf_op jit(solution)/shard_map/ppermute | solution.py:363
  68.0 4.9 %collective-permute-done.12.refs_8_ = bf16[4,4,4,256]{3,2,1,0:T(4,128)(2,1)S(1)} collective-permute-done((bf16[4,4,4,256]{3,2,1,0:T(4,128)(2,1)S(1)}, bf16[4,4,4,256]{3,2,1,0:T(4,128)(2,1)S(1)}, u32[]{:S(2)}, u32[]{:S(2)}) %collective-permute-start.12) | collective-permute-done | bytes 32800 | tf_op jit(solution)/shard_map/ppermute | solution.py:363
  72.9 0.8 %shard_map.96 = bf16[17,4,4,256]{3,2,1,0:T(4,128)(2,1)} custom-call(f32[13,4,4,256]{3,2,1,0:T(4,128)S(1)} %get-tuple-element.21.refs_0_, bf16[13,4,4,256]{3,2,1,0:T(4,128)(2,1)S(1)} %collective-permute-done.6.refs_1_, bf16[13,4,4,256]{3,2,1,0:T(4,128)(2,1)S(1)} %collective-permute-done.7.refs_2_, bf16[13,4,4,256]{3,2,1,0:T(4,128)(2,1)S(1)} %collective-permute-done.8.refs_3_, ...), custom_call_target="tpu_custom_call" | custom-call | flops 400000000 | bytes 1048576 | tf_op jit(solution)/shard_map/pallas_call | solution.py:27
  (20 shorter events, 0.1 us)
Async XLA Ops:
  2.3 5.6 %copy-start.1 = (bf16[1,17,4,4,256]{4,3,2,1,0:T(4,128)(2,1)S(1)}, bf16[1,17,4,4,256]{4,3,2,1,0:T(4,128)(2,1)}, u32[]{:S(2)}) copy-start(bf16[1,17,4,4,256]{4,3,2,1,0:T(4,128)(2,1)} %param.9) | copy-start | bytes 417796
  2.4 10.8 %copy-start = (bf16[3,3,3,16,256]{4,3,2,1,0:T(8,128)(2,1)S(1)}, bf16[3,3,3,16,256]{4,3,2,1,0:T(8,128)(2,1)}, u32[]{:S(2)}) copy-start(bf16[3,3,3,16,256]{4,3,2,1,0:T(8,128)(2,1)} %w0_ref.1) | copy-start | bytes 663556
  2.4 29.3 %all-to-all-start = ((bf16[16,15,16,128]{3,2,1,0:T(8,128)(2,1)}), bf16[16,15,16,128]{3,2,1,0:T(8,128)(2,1)S(1)}, u32[]{:S(2)}, u32[]{:S(2)}) async-start(bf16[16,15,16,128]{3,2,1,0:T(8,128)(2,1)} %get-tuple-element.17), calls=%async_computation | async-start | bytes 1966080 | tf_op jit(solution)/shard_map/all_to_all | solution.py:307
  8.0 17.2 %collective-permute-start = (bf16[17,4,4,256]{3,2,1,0:T(4,128)(2,1)S(1)}, bf16[17,4,4,256]{3,2,1,0:T(4,128)(2,1)S(1)}, u32[]{:S(2)}, u32[]{:S(2)}) collective-permute-start(bf16[17,4,4,256]{3,2,1,0:T(4,128)(2,1)S(1)} %bitcast.11), channel_id=1, source_target_pairs={{0,2},{2,0},{1,3},{3,1},{4,6},{6,4},{5,7},{7,5},{8,10},{10,8},{9,1... | collective-permute-start | bytes 417800 | tf_op jit(solution)/shard_map/ppermute | solution.py:330
  11.8 17.4 %collective-permute-start.1 = (bf16[17,4,4,256]{3,2,1,0:T(4,128)(2,1)S(1)}, bf16[17,4,4,256]{3,2,1,0:T(4,128)(2,1)S(1)}, u32[]{:S(2)}, u32[]{:S(2)}) collective-permute-start(bf16[17,4,4,256]{3,2,1,0:T(4,128)(2,1)S(1)} %bitcast.12), channel_id=1, source_target_pairs={{3,4},{4,3},{7,8},{8,7},{11,12},{12,11},{19,20},{20,19},{23,24},{2... | collective-permute-start | bytes 417800 | tf_op jit(solution)/shard_map/ppermute | solution.py:333
  12.5 16.8 %collective-permute-start.2 = (bf16[17,4,4,256]{3,2,1,0:T(4,128)(2,1)S(1)}, bf16[17,4,4,256]{3,2,1,0:T(4,128)(2,1)S(1)}, u32[]{:S(2)}, u32[]{:S(2)}) collective-permute-start(bf16[17,4,4,256]{3,2,1,0:T(4,128)(2,1)S(1)} %bitcast.13), channel_id=1, source_target_pairs={{3,6},{4,1},{7,10},{8,5},{11,14},{12,9},{19,22},{20,17},{23,26},{2... | collective-permute-start | bytes 417800 | tf_op jit(solution)/shard_map/ppermute | solution.py:334
  13.2 25.6 %collective-permute-start.3 = (bf16[3,3,3,16,256]{4,3,2,1,0:T(8,128)(2,1)S(1)}, bf16[3,3,3,16,256]{4,3,2,1,0:T(8,128)(2,1)S(1)}, u32[]{:S(2)}, u32[]{:S(2)}) collective-permute-start(bf16[3,3,3,16,256]{4,3,2,1,0:T(8,128)(2,1)S(1)} %copy-done), channel_id=1, source_target_pairs={{0,4},{4,8},{8,12},{12,0},{1,5},{5,9},{9,13},{13,1},{2,6},{6,10},{... | collective-permute-start | bytes 663560 | tf_op jit(solution)/shard_map/ppermute | solution.py:340
  18.4 20.3 %collective-permute-start.4 = (bf16[3,3,3,16,256]{4,3,2,1,0:T(8,128)(2,1)S(1)}, bf16[3,3,3,16,256]{4,3,2,1,0:T(8,128)(2,1)S(1)}, u32[]{:S(2)}, u32[]{:S(2)}) collective-permute-start(bf16[3,3,3,16,256]{4,3,2,1,0:T(8,128)(2,1)S(1)} %copy-done), channel_id=1, source_target_pairs={{0,8},{4,12},{8,0},{12,4},{1,9},{5,13},{9,1},{13,5},{2,10},{6,14},... | collective-permute-start | bytes 663560 | tf_op jit(solution)/shard_map/ppermute | solution.py:340
  25.2 13.6 %collective-permute-start.5 = (bf16[3,3,3,16,256]{4,3,2,1,0:T(8,128)(2,1)S(1)}, bf16[3,3,3,16,256]{4,3,2,1,0:T(8,128)(2,1)S(1)}, u32[]{:S(2)}, u32[]{:S(2)}) collective-permute-start(bf16[3,3,3,16,256]{4,3,2,1,0:T(8,128)(2,1)S(1)} %copy-done), channel_id=1, source_target_pairs={{0,12},{4,0},{8,4},{12,8},{1,13},{5,1},{9,5},{13,9},{2,14},{6,2},{... | collective-permute-start | bytes 663560 | tf_op jit(solution)/shard_map/ppermute | solution.py:340
  29.3 2.4 %copy-start.2 = (f32[8,256]{1,0:T(8,128)S(1)}, f32[8,256]{1,0:T(8,128)}, u32[]{:S(2)}) copy-start(f32[8,256]{1,0:T(8,128)} %get-tuple-element.18.vec_ref.refs_5_.refs_6_) | copy-start | bytes 24580
  35.5 8.6 %all-to-all-start.1 = ((f32[4,8,128]{2,1,0:T(8,128)}), f32[4,8,128]{2,1,0:T(8,128)S(1)}, u32[]{:S(2)}, u32[]{:S(2)}) async-start(f32[4,8,128]{2,1,0:T(8,128)} %get-tuple-element.20), calls=%async_computation.1 | async-start | bytes 32768 | tf_op jit(solution)/shard_map/all_to_all | solution.py:307
  46.3 13.4 %collective-permute-start.10 = (bf16[4,4,4,256]{3,2,1,0:T(4,128)(2,1)S(1)}, bf16[4,4,4,256]{3,2,1,0:T(4,128)(2,1)S(1)}, u32[]{:S(2)}, u32[]{:S(2)}) collective-permute-start(bf16[4,4,4,256]{3,2,1,0:T(4,128)(2,1)S(1)} %get-tuple-element.27), channel_id=1, source_target_pairs={{0,2},{1,3},{2,0},{3,1},{4,6},{5,7},{6,4},{7,5},{8,10},{9,11},{10,... | collective-permute-start | bytes 98312 | tf_op jit(solution)/shard_map/ppermute | solution.py:360
  48.8 24.1 %collective-permute-start.6 = (bf16[13,4,4,256]{3,2,1,0:T(4,128)(2,1)S(1)}, bf16[13,4,4,256]{3,2,1,0:T(4,128)(2,1)S(1)}, u32[]{:S(2)}, u32[]{:S(2)}) collective-permute-start(bf16[13,4,4,256]{3,2,1,0:T(4,128)(2,1)S(1)} %get-tuple-element.22), channel_id=1, source_target_pairs={{0,1},{1,0},{2,3},{3,2},{4,5},{5,4},{6,7},{7,6},{8,9},{9,8},{10,11... | collective-permute-start | bytes 319496 | tf_op jit(solution)/shard_map/ppermute | solution.py:360
  50.7 22.1 %collective-permute-start.7 = (bf16[13,4,4,256]{3,2,1,0:T(4,128)(2,1)S(1)}, bf16[13,4,4,256]{3,2,1,0:T(4,128)(2,1)S(1)}, u32[]{:S(2)}, u32[]{:S(2)}) collective-permute-start(bf16[13,4,4,256]{3,2,1,0:T(4,128)(2,1)S(1)} %get-tuple-element.23), channel_id=1, source_target_pairs={{0,2},{1,3},{2,0},{3,1},{4,6},{5,7},{6,4},{7,5},{8,10},{9,11},{10,... | collective-permute-start | bytes 319496 | tf_op jit(solution)/shard_map/ppermute | solution.py:360
  54.1 18.8 %collective-permute-start.8 = (bf16[13,4,4,256]{3,2,1,0:T(4,128)(2,1)S(1)}, bf16[13,4,4,256]{3,2,1,0:T(4,128)(2,1)S(1)}, u32[]{:S(2)}, u32[]{:S(2)}) collective-permute-start(bf16[13,4,4,256]{3,2,1,0:T(4,128)(2,1)S(1)} %get-tuple-element.24), channel_id=1, source_target_pairs={{0,3},{1,2},{2,1},{3,0},{4,7},{5,6},{6,5},{7,4},{8,11},{9,10},{10,... | collective-permute-start | bytes 319496 | tf_op jit(solution)/shard_map/ppermute | solution.py:360
  56.4 5.4 %collective-permute-start.11 = (bf16[4,4,4,256]{3,2,1,0:T(4,128)(2,1)S(1)}, bf16[4,4,4,256]{3,2,1,0:T(4,128)(2,1)S(1)}, u32[]{:S(2)}, u32[]{:S(2)}) collective-permute-start(bf16[4,4,4,256]{3,2,1,0:T(4,128)(2,1)S(1)} %get-tuple-element.28), channel_id=1, source_target_pairs={{0,3},{1,2},{2,1},{3,0},{4,7},{5,6},{6,5},{7,4},{8,11},{9,10},{10,... | collective-permute-start | bytes 98312 | tf_op jit(solution)/shard_map/ppermute | solution.py:360
  59.7 3.1 %collective-permute-start.9 = (bf16[4,4,4,256]{3,2,1,0:T(4,128)(2,1)S(1)}, bf16[4,4,4,256]{3,2,1,0:T(4,128)(2,1)S(1)}, u32[]{:S(2)}, u32[]{:S(2)}) collective-permute-start(bf16[4,4,4,256]{3,2,1,0:T(4,128)(2,1)S(1)} %get-tuple-element.26), channel_id=1, source_target_pairs={{0,1},{1,0},{2,3},{3,2},{4,5},{5,4},{6,7},{7,6},{8,9},{9,8},{10,11... | collective-permute-start | bytes 98312 | tf_op jit(solution)/shard_map/ppermute | solution.py:360
  62.8 10.0 %collective-permute-start.12 = (bf16[4,4,4,256]{3,2,1,0:T(4,128)(2,1)S(1)}, bf16[4,4,4,256]{3,2,1,0:T(4,128)(2,1)S(1)}, u32[]{:S(2)}, u32[]{:S(2)}) collective-permute-start(bf16[4,4,4,256]{3,2,1,0:T(4,128)(2,1)S(1)} %shard_map.95.refs_4_), channel_id=1, source_target_pairs={{0,16},{16,32},{32,48},{48,64},{64,80},{80,96},{96,112},{112,128},... | collective-permute-start | bytes 98312 | tf_op jit(solution)/shard_map/ppermute | solution.py:363

commit v5 on v4

--- a/solution.py
+++ b/solution.py
@@ -12,7 +12,6 @@
 F32, BF16 = jnp.float32, jnp.bfloat16
 
 COL = ("x", "yl", "core")
-JAX_ = ("yl", "core")
 TILE = ("z", "yh")
 T, H, W, C = 17, 4, 64, 256
 ROW = 24
@@ -136,7 +135,8 @@
                 out_ref[4 * x + j, m] = tile
 
 
-def join_kernel(latent_ref, other_ref, near_ref, far_ref, out_ref):
+def join_kernel(n_ref, latent_ref, other_ref, near_ref, far_ref, out_ref, shared_ref):
+    shared_ref[...] = jnp.full((1, C), n_ref[0], jnp.int32).astype(F32)
     out_ref[0] = latent_ref[...]
     out_ref[1] = other_ref[...]
     straight = lax.axis_index("yl") == lax.axis_index("core")
@@ -215,9 +215,7 @@
         st_ref[d] = stats
 
 
-def conv_two_kernel(hid_ref, st_ref, w0_ref, w1_ref, w2_ref, w3_ref, vec_ref, *outs):
-    *parts, act, wm = outs
-    tails, mains = parts[:4], parts[4:]
+def conv_two_kernel(hid_ref, st_ref, w0_ref, w1_ref, w2_ref, w3_ref, vec_ref, home_ref, away_ref, act, wm):
     me = lax.axis_index("x")
     j = 2 * lax.axis_index("yl") + lax.axis_index("core")
     for step, w_ref in enumerate((w0_ref, w1_ref, w2_ref, w3_ref)):
@@ -266,32 +264,38 @@
         rhs = wm[3 * taps[0] : 3 * taps[-1] + 3].reshape(-1, C)
         y = jnp.dot(lhs, rhs, preferred_element_type=F32).reshape(T, 16, C)
         for d in range(4):
-            columns = y[:, 4 * d : 4 * d + 4].astype(mains[d].dtype)
-            mains[d][:, h] = columns[: T - OVMAX]
-            tails[d][:, h] = columns[T - OVMAX :]
-
-
-def decode(parts, at, latent, bias):
-    branch = parts[0][at]
-    for part in parts[1:]:
-        branch = branch + part[at].astype(F32)
-    return (latent.astype(F32) + (branch + bias)).astype(BF16)
-
-
-def tail_kernel(*refs):
-    *parts, latent_ref, vec_ref, tail_ref = refs
+            target = away_ref if d % 2 else home_ref
+            target[d // 2, :, h] = y[:, 4 * d : 4 * d + 4].astype(target.dtype)
+
+
+def pair_kernel(home_ref, got_ref, own_ref, tail_ref, main_ref):
+    other = 1 - lax.axis_index("core")
+    for t in range(T):
+        own_ref[t] = home_ref[0, t] + got_ref[other, 0, t].astype(F32)
+        send = (home_ref[1, t] + got_ref[other, 1, t].astype(F32)).astype(BF16)
+        if t < T - OVMAX:
+            main_ref[t] = send
+        else:
+            tail_ref[t - T + OVMAX] = send
+
+
+def decode(own, other, latent, bias):
+    return (latent.astype(F32) + (own + other.astype(F32) + bias)).astype(BF16)
+
+
+def tail_kernel(own_ref, other_ref, latent_ref, vec_ref, tail_ref):
     for i in range(OVMAX):
-        tail_ref[i] = decode(parts, i, latent_ref[T - OVMAX + i], vec_ref[4:5])
-
-
-def blend_kernel(*refs):
-    *parts, tail_ref, latent_ref, vec_ref, shared_ref, received_ref, out_ref = refs
+        t = T - OVMAX + i
+        tail_ref[i] = decode(own_ref[t], other_ref[i], latent_ref[t], vec_ref[4:5])
+
+
+def blend_kernel(own_ref, other_ref, tail_ref, latent_ref, vec_ref, shared_ref, received_ref, out_ref):
     bias, shared = vec_ref[4:5], shared_ref[...]
     for t in range(T):
         if t >= T - OVMAX:
             out_ref[t] = tail_ref[t - T + OVMAX]
             continue
-        own = decode(parts, t, latent_ref[t], bias)
+        own = decode(own_ref[t], other_ref[t], latent_ref[t], bias)
         if t < OVMAX:
             other = received_ref[OVMAX - 1].astype(F32)
             for n in range(t + 2, OVMAX + 1):
@@ -332,12 +336,20 @@
     far = [p for x in range(3) for p in ((4 * x + 3, 4 * x + 6), (4 * x + 4, 4 * x + 1))]
     near = lax.ppermute(source, COL, near)
     far = lax.ppermute(source, COL, far)
-    shared = jnp.broadcast_to(intersections.astype(F32).reshape(1, 1), (1, C))
-    joined = call(join_kernel, (source, other, near, far), sds((3, T, 4, 4, C), BF16), cost=cost(1))
+    joined, shared = pl.pallas_call(
+        join_kernel,
+        out_shape=(sds((3, T, 4, 4, C), BF16), sds((1, C), F32)),
+        in_specs=[pl.BlockSpec(memory_space=pltpu.SMEM)] + [whole()] * 4,
+        out_specs=(whole(), whole()),
+        compiler_params=PARAMS,
+        cost_estimate=cost(1),
+    )(intersections, source, other, near, far)
     wide = lax.all_gather(joined, "core", axis=0, tiled=False)
-    kernel_two = [weight_two]
-    for step in range(1, 4):
-        kernel_two.append(lax.ppermute(weight_two, "x", [(x, (x + step) % 4) for x in range(4)]))
+    ring = lambda array, step: lax.ppermute(array, "x", [(x, (x + step) % 4) for x in range(4)])
+    after = ring(weight_two, 3)
+    before = ring(weight_two, 1)
+    opposite = ring(after, 3)
+    kernel_two = [weight_two, before, opposite, after]
     hidden, stats = call(
         conv_one_kernel,
         (wide, kernel_one, vec),
@@ -345,23 +357,29 @@
         (pltpu.VMEM((4, T + 2, ROW, C), BF16), pltpu.VMEM((9, C, C), BF16)),
         cost=cost(4),
     )
+    stats, *kernel_two = lax.optimization_barrier((stats, *kernel_two))
     stats = exchange(stats, "x")
-    kinds = (F32, BF16, BF16, BF16)
-    parts = call(
+    home, away = call(
         conv_two_kernel,
         (hidden, stats, *kernel_two, vec),
-        tuple(sds((n, 4, 4, C), kind) for n in (OVMAX, T - OVMAX) for kind in kinds),
+        (sds((2, T, 4, 4, C), F32), sds((2, T, 4, 4, C), BF16)),
         (pltpu.VMEM((4, T + 2, 16, C), BF16), pltpu.VMEM((9, C, C), BF16)),
         cost=cost(4),
     )
-    tails, mains = list(parts[:4]), list(parts[4:])
-    for arrays in (tails, mains):
-        for k in range(1, 4):
-            arrays[k] = lax.ppermute(arrays[k], JAX_, [(i, i ^ k) for i in range(4)])
-    tail = call(tail_kernel, (*tails, source, vec), sds((OVMAX, 4, 4, C), BF16), cost=cost(1))
+    got = lax.all_gather(away, "core", axis=0, tiled=False)
+    own, rest_tail, rest = call(
+        pair_kernel,
+        (home, got),
+        (sds((T, 4, 4, C), F32), sds((OVMAX, 4, 4, C), BF16), sds((T - OVMAX, 4, 4, C), BF16)),
+        cost=cost(1),
+    )
+    swap = [(0, 1), (1, 0)]
+    rest_tail = lax.ppermute(rest_tail, "yl", swap)
+    rest = lax.ppermute(rest, "yl", swap)
+    tail = call(tail_kernel, (own, rest_tail, source, vec), sds((OVMAX, 4, 4, C), BF16), cost=cost(1))
     tiles = lax.axis_size(TILE)
     received = lax.ppermute(tail, TILE, [(i, i + 1) for i in range(tiles - 1)])
-    out = call(blend_kernel, (*mains, tail, source, vec, shared, received), sds((T, 4, 4, C), BF16), cost=cost(1))
+    out = call(blend_kernel, (own, rest, tail, source, vec, shared, received), sds((T, 4, 4, C), BF16), cost=cost(1))
     return out[None]
 
 

time: 74.3 us -> 70.7 us (0.952)
  starting transfers between devices: 48.1 us -> 35.4 us
  blocking collectives: 2.4 us -> 13.3 us
  waiting for transfers between devices: 13 us -> 12 us
    ppermute x9 -> x5, starting transfers between devices: 29.6 us -> 20.7 us  [the longest x3 14.8 us: block(): lax.ppermute(array, 'x', [(x, (x + step) % 4) for x in range(4)])]
    all_to_all x0 -> x1, blocking collectives: none -> 8.73 us  [exchange(): return lax.all_to_all(array, axis, split_axis=0, concat_axis=0, tiled=True)]
    all_to_all x2 -> x1, waiting for transfers between devices: 5.3 us -> 0.01 us  [exchange(): return lax.all_to_all(array, axis, split_axis=0, concat_axis=0, tiled=True)]
    ppermute x9 -> x5, waiting for transfers between devices: 0.98 us -> 4.64 us  [the longest x1 3.54 us: block(): rest_tail = lax.ppermute(rest_tail, 'yl', swap)]
    all_to_all x2 -> x1, starting transfers between devices: 8.81 us -> 5.56 us  [exchange(): return lax.all_to_all(array, axis, split_axis=0, concat_axis=0, tiled=True)]
    all_gather x0 -> x1, blocking collectives: none -> 2.2 us  [block(): got = lax.all_gather(away, 'core', axis=0, tiled=False)]
  transfers between devices with their start and end apart: 15 -> 10, of which waited for: 4 -> 4; matrix products, arithmetic and copies ran while one was open for 0% -> 0% of each run, Pallas kernels for 5% -> 5%
where the time goes in v5:
time: 70.7 us; the launch traced here: 70.2 us
  starting transfers between devices  35.4 us (50%)
  blocking collectives  13.3 us (19%)
  waiting for transfers between devices  12 us (17%)
  Pallas kernels  8.61 us (12%)
  between operations  0.82 us (1%)
    ppermute x3, starting transfers between devices, block(): lax.ppermute(array, 'x', [(x, (x + step) % 4) for x in range(4)])  14.8 us
    all_to_all x1, blocking collectives, exchange(): return lax.all_to_all(array, axis, split_axis=0, concat_axis=0, tiled=True)  8.73 us
    pallas_call x5, Pallas kernels, call(): pl.pallas_call(kernel, out_shape=out_shape, in_specs=[whole()] * len(inpu...  6.24 us
    all_to_all x1, starting transfers between devices, exchange(): return lax.all_to_all(array, axis, split_axis=0, concat_axis=0, tiled=True)  5.56 us
    ppermute x1, waiting for transfers between devices, block(): received = lax.ppermute(tail, TILE, [(i, i + 1) for i in range(tiles - 1)])  5.52 us
    ppermute x1, starting transfers between devices, block(): received = lax.ppermute(tail, TILE, [(i, i + 1) for i in range(tiles - 1)])  4.5 us
    ppermute x1, starting transfers between devices, block(): rest = lax.ppermute(rest, 'yl', swap)  3.58 us
    ppermute x1, waiting for transfers between devices, block(): rest_tail = lax.ppermute(rest_tail, 'yl', swap)  3.54 us
  transfers between devices with their start and end apart: 10, of which 4 were waited for; matrix products, arithmetic and copies ran while one was open for 0% of the time, Pallas kernels for 5%

profile of v5, /device:TPU:256, one launch (start us, length us, event | category | flops | bytes accessed | tf_op | source)
XLA Modules:
  0.0 70.2 jit_solution(6711913287683637569)
XLA Ops:
  0.0 2.3 %shard_map.92 = (bf16[16,15,16,128]{3,2,1,0:T(8,128)(2,1)}, f32[8,256]{1,0:T(8,128)}) custom-call(bf16[3,3,3,16,256]{4,3,2,1,0:T(8,128)(2,1)} %w_hbm.1, bf16[17,4,4,256]{3,2,1,0:T(4,128)(2,1)} %bitcast.11, f32[1,256]{1,0:T(1,128)} %bitcast.18, f32[1,256]{1,0:T(1,128)} %bitcast.19, f32[1,256]{1,0:T(1,128)} %bitcast.20, f32[1,256]{1,0:T(1,128)} %bitcast.21, ...), custom_call_target="tpu_custom_call" | custom-call | flops 400000000 | bytes 1048576 | tf_op jit(solution)/shard_map/pallas_call | solution.py:319
  2.4 0.0 copy-start
  2.4 5.6 %all-to-all-start = ((bf16[16,15,16,128]{3,2,1,0:T(8,128)(2,1)}), bf16[16,15,16,128]{3,2,1,0:T(8,128)(2,1)S(1)}, u32[]{:S(2)}, u32[]{:S(2)}) async-start(bf16[16,15,16,128]{3,2,1,0:T(8,128)(2,1)} %get-tuple-element.22), calls=%async_computation | async-start | bytes 1966080 | tf_op jit(solution)/shard_map/all_to_all | solution.py:311
  8.0 5.0 %collective-permute-start.4 = (bf16[3,3,3,16,256]{4,3,2,1,0:T(8,128)(2,1)S(1)}, bf16[3,3,3,16,256]{4,3,2,1,0:T(8,128)(2,1)S(1)}, u32[]{:S(2)}, u32[]{:S(2)}) collective-permute-start(bf16[3,3,3,16,256]{4,3,2,1,0:T(8,128)(2,1)S(1)} %copy-done), channel_id=1, source_target_pairs={{0,12},{4,0},{8,4},{12,8},{1,13},{5,1},{9,5},{13,9},{2,14},{6,2},{... | collective-permute-start | bytes 663560 | tf_op jit(solution)/shard_map/ppermute | solution.py:348
  13.0 3.4 %collective-permute-start = (bf16[17,4,4,256]{3,2,1,0:T(4,128)(2,1)S(1)}, bf16[17,4,4,256]{3,2,1,0:T(4,128)(2,1)S(1)}, u32[]{:S(2)}, u32[]{:S(2)}) collective-permute-start(bf16[17,4,4,256]{3,2,1,0:T(4,128)(2,1)S(1)} %bitcast.12), channel_id=1, source_target_pairs={{0,2},{2,0},{1,3},{3,1},{4,6},{6,4},{5,7},{7,5},{8,10},{10,8},{9,1... | collective-permute-start | bytes 417800 | tf_op jit(solution)/shard_map/ppermute | solution.py:334
  16.4 0.7 collective-permute-start.1
  17.1 0.7 collective-permute-start.2
  17.8 5.0 %collective-permute-start.3 = (bf16[3,3,3,16,256]{4,3,2,1,0:T(8,128)(2,1)S(1)}, bf16[3,3,3,16,256]{4,3,2,1,0:T(8,128)(2,1)S(1)}, u32[]{:S(2)}, u32[]{:S(2)}) collective-permute-start(bf16[3,3,3,16,256]{4,3,2,1,0:T(8,128)(2,1)S(1)} %copy-done), channel_id=1, source_target_pairs={{0,4},{4,8},{8,12},{12,0},{1,5},{5,9},{9,13},{13,1},{2,6},{6,10},{... | collective-permute-start | bytes 663560 | tf_op jit(solution)/shard_map/ppermute | solution.py:348
  23.4 1.8 %collective-permute-done.other_ref = bf16[17,4,4,256]{3,2,1,0:T(4,128)(2,1)S(1)} collective-permute-done((bf16[17,4,4,256]{3,2,1,0:T(4,128)(2,1)S(1)}, bf16[17,4,4,256]{3,2,1,0:T(4,128)(2,1)S(1)}, u32[]{:S(2)}, u32[]{:S(2)}) %collective-permute-start) | collective-permute-done | bytes 139296 | tf_op jit(solution)/shard_map/ppermute | solution.py:334
  25.2 1.1 %collective-permute-done.4.w3_ref = bf16[3,3,3,16,256]{4,3,2,1,0:T(8,128)(2,1)S(1)} collective-permute-done((bf16[3,3,3,16,256]{4,3,2,1,0:T(8,128)(2,1)S(1)}, bf16[3,3,3,16,256]{4,3,2,1,0:T(8,128)(2,1)S(1)}, u32[]{:S(2)}, u32[]{:S(2)}) %collective-permute-start.4) | collective-permute-done | bytes 221216 | tf_op jit(solution)/shard_map/ppermute | solution.py:348
  26.3 4.8 %collective-permute-start.5 = (bf16[3,3,3,16,256]{4,3,2,1,0:T(8,128)(2,1)S(1)}, bf16[3,3,3,16,256]{4,3,2,1,0:T(8,128)(2,1)S(1)}, u32[]{:S(2)}, u32[]{:S(2)}) collective-permute-start(bf16[3,3,3,16,256]{4,3,2,1,0:T(8,128)(2,1)S(1)} %collective-permute-done.4.w3_ref), channel_id=1, source_target_pairs={{0,12},{4,0},{8,4},{12,8},{1,13},{5,1},{9,5},{13,9},{2,14},{6,2},{... | collective-permute-start | bytes 663560 | tf_op jit(solution)/shard_map/ppermute | solution.py:348
  31.1 0.0 copy-start.2
  31.1 2.4 %all-gather = bf16[6,17,4,4,256]{4,3,2,1,0:T(4,128)(2,1)S(1)} all-gather(bf16[3,17,4,4,256]{4,3,2,1,0:T(4,128)(2,1)S(1)} %get-tuple-element.21), channel_id=2, replica_groups=mesh['z'=8,'yh'=4,'x'=4,'yl'=2,'core'=2] {'core'}, dimensions={0}, use_global_device_ids=true | all-gather | bytes 1253376 | tf_op jit(solution)/shard_map/all_gather | solution.py:347
  33.6 3.1 %shard_map.93 = (bf16[4,17,24,128]{3,2,1,0:T(8,128)(2,1)S(1)}, f32[4,8,128]{2,1,0:T(8,128)S(1)}) custom-call(bf16[2,3,17,4,4,256]{5,4,3,2,1,0:T(4,128)(2,1)S(1)} %bitcast.9, bf16[16,15,16,128]{3,2,1,0:T(8,128)(2,1)S(1)} %all-to-all-done.w_ref, f32[8,256]{1,0:T(8,128)S(1)} %copy-done.2), custom_call_target="tpu_custom_call" | custom-call | flops 1600000000 | bytes 1048576 | tf_op jit(solution)/shard_map/pallas_call | solution.py:26
  36.7 8.7 %all_to_all.10.st_ref = f32[4,8,128]{2,1,0:T(8,128)S(1)} all-to-all(f32[4,8,128]{2,1,0:T(8,128)S(1)} %get-tuple-element.26), channel_id=1, replica_groups=mesh['z'=8,'yh'=4,'x'=4,'yl'=2,'core'=2] {'x'}, dimensions={0} | all-to-all | bytes 32768 | tf_op jit(solution)/shard_map/all_to_all | solution.py:311
  45.4 2.3 %shard_map.94 = (f32[2,17,4,4,256]{4,3,2,1,0:T(4,128)S(1)}, bf16[2,17,4,4,256]{4,3,2,1,0:T(4,128)(2,1)S(1)}) custom-call(bf16[4,17,24,128]{3,2,1,0:T(8,128)(2,1)S(1)} %get-tuple-element.24.hid_ref, f32[4,8,128]{2,1,0:T(8,128)S(1)} %all_to_all.10.st_ref, bf16[3,3,3,16,256]{4,3,2,1,0:T(8,128)(2,1)S(1)} %copy-done, ...), custom_call_target="tpu_custom_call" | custom-call | flops 1600000000 | bytes 1048576 | tf_op jit(solution)/shard_map/pallas_call | solution.py:26
  47.7 2.2 %all-gather.1 = bf16[4,17,4,4,256]{4,3,2,1,0:T(4,128)(2,1)S(1)} all-gather(bf16[2,17,4,4,256]{4,3,2,1,0:T(4,128)(2,1)S(1)} %get-tuple-element.32), channel_id=3, replica_groups=mesh['z'=8,'yh'=4,'x'=4,'yl'=2,'core'=2] {'core'}, dimensions={0}, use_global_device_ids=true | all-gather | bytes 835584 | tf_op jit(solution)/shard_map/all_gather | solution.py:369
  49.9 0.1 shard_map.95
  50.0 3.6 %collective-permute-start.6 = (bf16[13,4,4,256]{3,2,1,0:T(4,128)(2,1)S(1)}, bf16[13,4,4,256]{3,2,1,0:T(4,128)(2,1)S(1)}, u32[]{:S(2)}, u32[]{:S(2)}) collective-permute-start(bf16[13,4,4,256]{3,2,1,0:T(4,128)(2,1)S(1)} %get-tuple-element.34), channel_id=1, source_target_pairs={{0,2},{2,0},{1,3},{3,1},{4,6},{6,4},{5,7},{7,5},{8,10},{10,8},{9,1... | collective-permute-start | bytes 319496 | tf_op jit(solution)/shard_map/ppermute | solution.py:378
  53.6 2.3 %collective-permute-start.7 = (bf16[4,4,4,256]{3,2,1,0:T(4,128)(2,1)S(1)}, bf16[4,4,4,256]{3,2,1,0:T(4,128)(2,1)S(1)}, u32[]{:S(2)}, u32[]{:S(2)}) collective-permute-start(bf16[4,4,4,256]{3,2,1,0:T(4,128)(2,1)S(1)} %get-tuple-element.35), channel_id=1, source_target_pairs={{0,2},{2,0},{1,3},{3,1},{4,6},{6,4},{5,7},{7,5},{8,10},{10,8},{9,1... | collective-permute-start | bytes 98312 | tf_op jit(solution)/shard_map/ppermute | solution.py:377
  55.8 3.5 %collective-permute-done.7.other_ref = bf16[4,4,4,256]{3,2,1,0:T(4,128)(2,1)S(1)} collective-permute-done((bf16[4,4,4,256]{3,2,1,0:T(4,128)(2,1)S(1)}, bf16[4,4,4,256]{3,2,1,0:T(4,128)(2,1)S(1)}, u32[]{:S(2)}, u32[]{:S(2)}) %collective-permute-start.7) | collective-permute-done | bytes 32800 | tf_op jit(solution)/shard_map/ppermute | solution.py:377
  59.4 4.5 %collective-permute-start.8 = (bf16[4,4,4,256]{3,2,1,0:T(4,128)(2,1)S(1)}, bf16[4,4,4,256]{3,2,1,0:T(4,128)(2,1)S(1)}, u32[]{:S(2)}, u32[]{:S(2)}) collective-permute-start(bf16[4,4,4,256]{3,2,1,0:T(4,128)(2,1)S(1)} %shard_map.96.tail_ref), channel_id=1, source_target_pairs={{0,16},{16,32},{32,48},{48,64},{64,80},{80,96},{96,112},{112,128},... | collective-permute-start | bytes 98312 | tf_op jit(solution)/shard_map/ppermute | solution.py:381
  63.9 5.5 %collective-permute-done.8.received_ref = bf16[4,4,4,256]{3,2,1,0:T(4,128)(2,1)S(1)} collective-permute-done((bf16[4,4,4,256]{3,2,1,0:T(4,128)(2,1)S(1)}, bf16[4,4,4,256]{3,2,1,0:T(4,128)(2,1)S(1)}, u32[]{:S(2)}, u32[]{:S(2)}) %collective-permute-start.8) | collective-permute-done | bytes 32800 | tf_op jit(solution)/shard_map/ppermute | solution.py:381
  69.4 0.8 %shard_map.97 = bf16[17,4,4,256]{3,2,1,0:T(4,128)(2,1)} custom-call(f32[17,4,4,256]{3,2,1,0:T(4,128)S(1)} %get-tuple-element.33.own_ref, bf16[13,4,4,256]{3,2,1,0:T(4,128)(2,1)S(1)} %collective-permute-done.6.other_ref, bf16[4,4,4,256]{3,2,1,0:T(4,128)(2,1)S(1)} %shard_map.96.tail_ref, bf16[17,4,4,256]{3,2,1,0:T(4,128)(2,1)S(1)} %bitcast.17, ...), custom_call_target="tpu_custom_call" | custom-call | flops 400000000 | bytes 1048576 | tf_op jit(solution)/shard_map/pallas_call | solution.py:26
  (12 shorter events, 0.1 us)
Async XLA Ops:
  2.4 5.6 %copy-start = (bf16[3,3,3,16,256]{4,3,2,1,0:T(8,128)(2,1)S(1)}, bf16[3,3,3,16,256]{4,3,2,1,0:T(8,128)(2,1)}, u32[]{:S(2)}) copy-start(bf16[3,3,3,16,256]{4,3,2,1,0:T(8,128)(2,1)} %w0_ref) | copy-start | bytes 663556
  2.4 10.6 %copy-start.1 = (bf16[1,17,4,4,256]{4,3,2,1,0:T(4,128)(2,1)S(1)}, bf16[1,17,4,4,256]{4,3,2,1,0:T(4,128)(2,1)}, u32[]{:S(2)}) copy-start(bf16[1,17,4,4,256]{4,3,2,1,0:T(4,128)(2,1)} %param.9) | copy-start | bytes 417796
  2.4 31.2 %all-to-all-start = ((bf16[16,15,16,128]{3,2,1,0:T(8,128)(2,1)}), bf16[16,15,16,128]{3,2,1,0:T(8,128)(2,1)S(1)}, u32[]{:S(2)}, u32[]{:S(2)}) async-start(bf16[16,15,16,128]{3,2,1,0:T(8,128)(2,1)} %get-tuple-element.22), calls=%async_computation | async-start | bytes 1966080 | tf_op jit(solution)/shard_map/all_to_all | solution.py:311
  8.0 18.4 %collective-permute-start.4 = (bf16[3,3,3,16,256]{4,3,2,1,0:T(8,128)(2,1)S(1)}, bf16[3,3,3,16,256]{4,3,2,1,0:T(8,128)(2,1)S(1)}, u32[]{:S(2)}, u32[]{:S(2)}) collective-permute-start(bf16[3,3,3,16,256]{4,3,2,1,0:T(8,128)(2,1)S(1)} %copy-done), channel_id=1, source_target_pairs={{0,12},{4,0},{8,4},{12,8},{1,13},{5,1},{9,5},{13,9},{2,14},{6,2},{... | collective-permute-start | bytes 663560 | tf_op jit(solution)/shard_map/ppermute | solution.py:348
  13.0 12.2 %collective-permute-start = (bf16[17,4,4,256]{3,2,1,0:T(4,128)(2,1)S(1)}, bf16[17,4,4,256]{3,2,1,0:T(4,128)(2,1)S(1)}, u32[]{:S(2)}, u32[]{:S(2)}) collective-permute-start(bf16[17,4,4,256]{3,2,1,0:T(4,128)(2,1)S(1)} %bitcast.12), channel_id=1, source_target_pairs={{0,2},{2,0},{1,3},{3,1},{4,6},{6,4},{5,7},{7,5},{8,10},{10,8},{9,1... | collective-permute-start | bytes 417800 | tf_op jit(solution)/shard_map/ppermute | solution.py:334
  16.4 8.8 %collective-permute-start.1 = (bf16[17,4,4,256]{3,2,1,0:T(4,128)(2,1)S(1)}, bf16[17,4,4,256]{3,2,1,0:T(4,128)(2,1)S(1)}, u32[]{:S(2)}, u32[]{:S(2)}) collective-permute-start(bf16[17,4,4,256]{3,2,1,0:T(4,128)(2,1)S(1)} %bitcast.13), channel_id=1, source_target_pairs={{3,4},{4,3},{7,8},{8,7},{11,12},{12,11},{19,20},{20,19},{23,24},{2... | collective-permute-start | bytes 417800 | tf_op jit(solution)/shard_map/ppermute | solution.py:337
  17.1 8.1 %collective-permute-start.2 = (bf16[17,4,4,256]{3,2,1,0:T(4,128)(2,1)S(1)}, bf16[17,4,4,256]{3,2,1,0:T(4,128)(2,1)S(1)}, u32[]{:S(2)}, u32[]{:S(2)}) collective-permute-start(bf16[17,4,4,256]{3,2,1,0:T(4,128)(2,1)S(1)} %bitcast.14), channel_id=1, source_target_pairs={{3,6},{4,1},{7,10},{8,5},{11,14},{12,9},{19,22},{20,17},{23,26},{2... | collective-permute-start | bytes 417800 | tf_op jit(solution)/shard_map/ppermute | solution.py:338
  17.8 18.9 %collective-permute-start.3 = (bf16[3,3,3,16,256]{4,3,2,1,0:T(8,128)(2,1)S(1)}, bf16[3,3,3,16,256]{4,3,2,1,0:T(8,128)(2,1)S(1)}, u32[]{:S(2)}, u32[]{:S(2)}) collective-permute-start(bf16[3,3,3,16,256]{4,3,2,1,0:T(8,128)(2,1)S(1)} %copy-done), channel_id=1, source_target_pairs={{0,4},{4,8},{8,12},{12,0},{1,5},{5,9},{9,13},{13,1},{2,6},{6,10},{... | collective-permute-start | bytes 663560 | tf_op jit(solution)/shard_map/ppermute | solution.py:348
  26.3 10.4 %collective-permute-start.5 = (bf16[3,3,3,16,256]{4,3,2,1,0:T(8,128)(2,1)S(1)}, bf16[3,3,3,16,256]{4,3,2,1,0:T(8,128)(2,1)S(1)}, u32[]{:S(2)}, u32[]{:S(2)}) collective-permute-start(bf16[3,3,3,16,256]{4,3,2,1,0:T(8,128)(2,1)S(1)} %collective-permute-done.4.w3_ref), channel_id=1, source_target_pairs={{0,12},{4,0},{8,4},{12,8},{1,13},{5,1},{9,5},{13,9},{2,14},{6,2},{... | collective-permute-start | bytes 663560 | tf_op jit(solution)/shard_map/ppermute | solution.py:348
  31.1 2.4 %copy-start.2 = (f32[8,256]{1,0:T(8,128)S(1)}, f32[8,256]{1,0:T(8,128)}, u32[]{:S(2)}) copy-start(f32[8,256]{1,0:T(8,128)} %get-tuple-element.23.vec_ref) | copy-start | bytes 24580
  50.0 19.4 %collective-permute-start.6 = (bf16[13,4,4,256]{3,2,1,0:T(4,128)(2,1)S(1)}, bf16[13,4,4,256]{3,2,1,0:T(4,128)(2,1)S(1)}, u32[]{:S(2)}, u32[]{:S(2)}) collective-permute-start(bf16[13,4,4,256]{3,2,1,0:T(4,128)(2,1)S(1)} %get-tuple-element.34), channel_id=1, source_target_pairs={{0,2},{2,0},{1,3},{3,1},{4,6},{6,4},{5,7},{7,5},{8,10},{10,8},{9,1... | collective-permute-start | bytes 319496 | tf_op jit(solution)/shard_map/ppermute | solution.py:378
  53.6 5.8 %collective-permute-start.7 = (bf16[4,4,4,256]{3,2,1,0:T(4,128)(2,1)S(1)}, bf16[4,4,4,256]{3,2,1,0:T(4,128)(2,1)S(1)}, u32[]{:S(2)}, u32[]{:S(2)}) collective-permute-start(bf16[4,4,4,256]{3,2,1,0:T(4,128)(2,1)S(1)} %get-tuple-element.35), channel_id=1, source_target_pairs={{0,2},{2,0},{1,3},{3,1},{4,6},{6,4},{5,7},{7,5},{8,10},{10,8},{9,1... | collective-permute-start | bytes 98312 | tf_op jit(solution)/shard_map/ppermute | solution.py:377
  59.4 10.0 %collective-permute-start.8 = (bf16[4,4,4,256]{3,2,1,0:T(4,128)(2,1)S(1)}, bf16[4,4,4,256]{3,2,1,0:T(4,128)(2,1)S(1)}, u32[]{:S(2)}, u32[]{:S(2)}) collective-permute-start(bf16[4,4,4,256]{3,2,1,0:T(4,128)(2,1)S(1)} %shard_map.96.tail_ref), channel_id=1, source_target_pairs={{0,16},{16,32},{32,48},{48,64},{64,80},{80,96},{96,112},{112,128},... | collective-permute-start | bytes 98312 | tf_op jit(solution)/shard_map/ppermute | solution.py:381

commit v6 on v5

--- a/solution.py
+++ b/solution.py
@@ -331,6 +331,9 @@
         cost_estimate=cost(1),
     )(weight_one, source, *vectors)
     kernel_one = exchange(packed, COL)
+    kernel_two = [weight_two]
+    for step in range(1, 4):
+        kernel_two.append(lax.ppermute(weight_two, "x", [(x, (x + step) % 4) for x in range(4)]))
     other = lax.ppermute(source, "yl", [(0, 1), (1, 0)])
     near = [p for x in range(3) for p in ((4 * x + 3, 4 * x + 4), (4 * x + 4, 4 * x + 3))]
     far = [p for x in range(3) for p in ((4 * x + 3, 4 * x + 6), (4 * x + 4, 4 * x + 1))]
@@ -345,11 +348,6 @@
         cost_estimate=cost(1),
     )(intersections, source, other, near, far)
     wide = lax.all_gather(joined, "core", axis=0, tiled=False)
-    ring = lambda array, step: lax.ppermute(array, "x", [(x, (x + step) % 4) for x in range(4)])
-    after = ring(weight_two, 3)
-    before = ring(weight_two, 1)
-    opposite = ring(after, 3)
-    kernel_two = [weight_two, before, opposite, after]
     hidden, stats = call(
         conv_one_kernel,
         (wide, kernel_one, vec),

time: 70.7 us -> 68.1 us (0.963)
  the two profiles are of different devices: /device:TPU:256 before, /device:TPU:264 now
where the time goes in v6:
time: 68.1 us; the launch traced here: 67.6 us
  starting transfers between devices  33.3 us (49%)
  blocking collectives  13.4 us (20%)
  waiting for transfers between devices  11.4 us (17%)
  Pallas kernels  8.61 us (13%)
  between operations  0.83 us (1%)
    ppermute x3, starting transfers between devices, block(): lax.ppermute(weight_two, 'x', [(x, (x + step) % 4) for x in range(4)])  13.7 us
    all_to_all x1, blocking collectives, exchange(): return lax.all_to_all(array, axis, split_axis=0, concat_axis=0, tiled=True)  8.83 us
    pallas_call x5, Pallas kernels, call(): pl.pallas_call(kernel, out_shape=out_shape, in_specs=[whole()] * len(inpu...  6.24 us
    all_to_all x1, starting transfers between devices, exchange(): return lax.all_to_all(array, axis, split_axis=0, concat_axis=0, tiled=True)  5.92 us
    ppermute x1, waiting for transfers between devices, block(): received = lax.ppermute(tail, TILE, [(i, i + 1) for i in range(tiles - 1)])  5.87 us
    ppermute x1, starting transfers between devices, block(): received = lax.ppermute(tail, TILE, [(i, i + 1) for i in range(tiles - 1)])  4.5 us
    ppermute x1, starting transfers between devices, block(): rest = lax.ppermute(rest, 'yl', swap)  3.37 us
    ppermute x1, waiting for transfers between devices, block(): rest_tail = lax.ppermute(rest_tail, 'yl', swap)  3.33 us
  transfers between devices with their start and end apart: 10, of which 3 were waited for; matrix products, arithmetic and copies ran while one was open for 0% of the time, Pallas kernels for 5%

profile of v6, /device:TPU:264, one launch (start us, length us, event | category | flops | bytes accessed | tf_op | source)
XLA Modules:
  0.0 67.6 jit_solution(17633559702159210422)
XLA Ops:
  0.0 2.3 %shard_map.92 = (bf16[16,15,16,128]{3,2,1,0:T(8,128)(2,1)}, f32[8,256]{1,0:T(8,128)}) custom-call(bf16[3,3,3,16,256]{4,3,2,1,0:T(8,128)(2,1)} %w_hbm.1, bf16[17,4,4,256]{3,2,1,0:T(4,128)(2,1)} %bitcast.11, f32[1,256]{1,0:T(1,128)} %bitcast.18, f32[1,256]{1,0:T(1,128)} %bitcast.19, f32[1,256]{1,0:T(1,128)} %bitcast.20, f32[1,256]{1,0:T(1,128)} %bitcast.21, ...), custom_call_target="tpu_custom_call" | custom-call | flops 400000000 | bytes 1048576 | tf_op jit(solution)/shard_map/pallas_call | solution.py:319
  2.4 0.0 copy-start.1
  2.4 0.0 copy-start
  2.4 5.9 %all-to-all-start = ((bf16[16,15,16,128]{3,2,1,0:T(8,128)(2,1)}), bf16[16,15,16,128]{3,2,1,0:T(8,128)(2,1)S(1)}, u32[]{:S(2)}, u32[]{:S(2)}) async-start(bf16[16,15,16,128]{3,2,1,0:T(8,128)(2,1)} %get-tuple-element.22), calls=%async_computation | async-start | bytes 1966080 | tf_op jit(solution)/shard_map/all_to_all | solution.py:311
  8.3 2.0 %collective-permute-start = (bf16[17,4,4,256]{3,2,1,0:T(4,128)(2,1)S(1)}, bf16[17,4,4,256]{3,2,1,0:T(4,128)(2,1)S(1)}, u32[]{:S(2)}, u32[]{:S(2)}) collective-permute-start(bf16[17,4,4,256]{3,2,1,0:T(4,128)(2,1)S(1)} %bitcast.12), channel_id=1, source_target_pairs={{0,2},{2,0},{1,3},{3,1},{4,6},{6,4},{5,7},{7,5},{8,10},{10,8},{9,1... | collective-permute-start | bytes 417800 | tf_op jit(solution)/shard_map/ppermute | solution.py:337
  10.3 0.7 collective-permute-start.1
  11.0 0.7 collective-permute-start.2
  11.7 4.5 %collective-permute-start.3 = (bf16[3,3,3,16,256]{4,3,2,1,0:T(8,128)(2,1)S(1)}, bf16[3,3,3,16,256]{4,3,2,1,0:T(8,128)(2,1)S(1)}, u32[]{:S(2)}, u32[]{:S(2)}) collective-permute-start(bf16[3,3,3,16,256]{4,3,2,1,0:T(8,128)(2,1)S(1)} %copy-done), channel_id=1, source_target_pairs={{0,4},{4,8},{8,12},{12,0},{1,5},{5,9},{9,13},{13,1},{2,6},{6,10},{... | collective-permute-start | bytes 663560 | tf_op jit(solution)/shard_map/ppermute | solution.py:336
  16.1 4.6 %collective-permute-start.4 = (bf16[3,3,3,16,256]{4,3,2,1,0:T(8,128)(2,1)S(1)}, bf16[3,3,3,16,256]{4,3,2,1,0:T(8,128)(2,1)S(1)}, u32[]{:S(2)}, u32[]{:S(2)}) collective-permute-start(bf16[3,3,3,16,256]{4,3,2,1,0:T(8,128)(2,1)S(1)} %copy-done), channel_id=1, source_target_pairs={{0,8},{4,12},{8,0},{12,4},{1,9},{5,13},{9,1},{13,5},{2,10},{6,14},... | collective-permute-start | bytes 663560 | tf_op jit(solution)/shard_map/ppermute | solution.py:336
  21.4 2.1 %collective-permute-done.other_ref = bf16[17,4,4,256]{3,2,1,0:T(4,128)(2,1)S(1)} collective-permute-done((bf16[17,4,4,256]{3,2,1,0:T(4,128)(2,1)S(1)}, bf16[17,4,4,256]{3,2,1,0:T(4,128)(2,1)S(1)}, u32[]{:S(2)}, u32[]{:S(2)}) %collective-permute-start) | collective-permute-done | bytes 139296 | tf_op jit(solution)/shard_map/ppermute | solution.py:337
  23.5 4.7 %collective-permute-start.5 = (bf16[3,3,3,16,256]{4,3,2,1,0:T(8,128)(2,1)S(1)}, bf16[3,3,3,16,256]{4,3,2,1,0:T(8,128)(2,1)S(1)}, u32[]{:S(2)}, u32[]{:S(2)}) collective-permute-start(bf16[3,3,3,16,256]{4,3,2,1,0:T(8,128)(2,1)S(1)} %copy-done), channel_id=1, source_target_pairs={{0,12},{4,0},{8,4},{12,8},{1,13},{5,1},{9,5},{13,9},{2,14},{6,2},{... | collective-permute-start | bytes 663560 | tf_op jit(solution)/shard_map/ppermute | solution.py:336
  28.3 0.0 copy-start.2
  28.3 2.4 %all-gather = bf16[6,17,4,4,256]{4,3,2,1,0:T(4,128)(2,1)S(1)} all-gather(bf16[3,17,4,4,256]{4,3,2,1,0:T(4,128)(2,1)S(1)} %get-tuple-element.21), channel_id=2, replica_groups=mesh['z'=8,'yh'=4,'x'=4,'yl'=2,'core'=2] {'core'}, dimensions={0}, use_global_device_ids=true | all-gather | bytes 1253376 | tf_op jit(solution)/shard_map/all_gather | solution.py:350
  30.7 3.1 %shard_map.93 = (bf16[4,17,24,128]{3,2,1,0:T(8,128)(2,1)S(1)}, f32[4,8,128]{2,1,0:T(8,128)S(1)}) custom-call(bf16[2,3,17,4,4,256]{5,4,3,2,1,0:T(4,128)(2,1)S(1)} %bitcast.9, bf16[16,15,16,128]{3,2,1,0:T(8,128)(2,1)S(1)} %all-to-all-done.w_ref, f32[8,256]{1,0:T(8,128)S(1)} %copy-done.2), custom_call_target="tpu_custom_call" | custom-call | flops 1600000000 | bytes 1048576 | tf_op jit(solution)/shard_map/pallas_call | solution.py:26
  33.9 8.8 %all_to_all.10.st_ref = f32[4,8,128]{2,1,0:T(8,128)S(1)} all-to-all(f32[4,8,128]{2,1,0:T(8,128)S(1)} %get-tuple-element.26), channel_id=1, replica_groups=mesh['z'=8,'yh'=4,'x'=4,'yl'=2,'core'=2] {'x'}, dimensions={0} | all-to-all | bytes 32768 | tf_op jit(solution)/shard_map/all_to_all | solution.py:311
  42.7 2.3 %shard_map.94 = (f32[2,17,4,4,256]{4,3,2,1,0:T(4,128)S(1)}, bf16[2,17,4,4,256]{4,3,2,1,0:T(4,128)(2,1)S(1)}) custom-call(bf16[4,17,24,128]{3,2,1,0:T(8,128)(2,1)S(1)} %get-tuple-element.24.hid_ref, f32[4,8,128]{2,1,0:T(8,128)S(1)} %all_to_all.10.st_ref, bf16[3,3,3,16,256]{4,3,2,1,0:T(8,128)(2,1)S(1)} %copy-done, ...), custom_call_target="tpu_custom_call" | custom-call | flops 1600000000 | bytes 1048576 | tf_op jit(solution)/shard_map/pallas_call | solution.py:26
  45.0 2.2 %all-gather.1 = bf16[4,17,4,4,256]{4,3,2,1,0:T(4,128)(2,1)S(1)} all-gather(bf16[2,17,4,4,256]{4,3,2,1,0:T(4,128)(2,1)S(1)} %get-tuple-element.32), channel_id=3, replica_groups=mesh['z'=8,'yh'=4,'x'=4,'yl'=2,'core'=2] {'core'}, dimensions={0}, use_global_device_ids=true | all-gather | bytes 835584 | tf_op jit(solution)/shard_map/all_gather | solution.py:367
  47.2 0.1 shard_map.95
  47.2 3.4 %collective-permute-start.6 = (bf16[13,4,4,256]{3,2,1,0:T(4,128)(2,1)S(1)}, bf16[13,4,4,256]{3,2,1,0:T(4,128)(2,1)S(1)}, u32[]{:S(2)}, u32[]{:S(2)}) collective-permute-start(bf16[13,4,4,256]{3,2,1,0:T(4,128)(2,1)S(1)} %get-tuple-element.34), channel_id=1, source_target_pairs={{0,2},{2,0},{1,3},{3,1},{4,6},{6,4},{5,7},{7,5},{8,10},{10,8},{9,1... | collective-permute-start | bytes 319496 | tf_op jit(solution)/shard_map/ppermute | solution.py:376
  50.6 2.5 %collective-permute-start.7 = (bf16[4,4,4,256]{3,2,1,0:T(4,128)(2,1)S(1)}, bf16[4,4,4,256]{3,2,1,0:T(4,128)(2,1)S(1)}, u32[]{:S(2)}, u32[]{:S(2)}) collective-permute-start(bf16[4,4,4,256]{3,2,1,0:T(4,128)(2,1)S(1)} %get-tuple-element.35), channel_id=1, source_target_pairs={{0,2},{2,0},{1,3},{3,1},{4,6},{6,4},{5,7},{7,5},{8,10},{10,8},{9,1... | collective-permute-start | bytes 98312 | tf_op jit(solution)/shard_map/ppermute | solution.py:375
  53.1 3.3 %collective-permute-done.7.other_ref = bf16[4,4,4,256]{3,2,1,0:T(4,128)(2,1)S(1)} collective-permute-done((bf16[4,4,4,256]{3,2,1,0:T(4,128)(2,1)S(1)}, bf16[4,4,4,256]{3,2,1,0:T(4,128)(2,1)S(1)}, u32[]{:S(2)}, u32[]{:S(2)}) %collective-permute-start.7) | collective-permute-done | bytes 32800 | tf_op jit(solution)/shard_map/ppermute | solution.py:375
  56.4 4.5 %collective-permute-start.8 = (bf16[4,4,4,256]{3,2,1,0:T(4,128)(2,1)S(1)}, bf16[4,4,4,256]{3,2,1,0:T(4,128)(2,1)S(1)}, u32[]{:S(2)}, u32[]{:S(2)}) collective-permute-start(bf16[4,4,4,256]{3,2,1,0:T(4,128)(2,1)S(1)} %shard_map.96.tail_ref), channel_id=1, source_target_pairs={{0,16},{16,32},{32,48},{48,64},{64,80},{80,96},{96,112},{112,128},... | collective-permute-start | bytes 98312 | tf_op jit(solution)/shard_map/ppermute | solution.py:379
  61.0 5.9 %collective-permute-done.8.received_ref = bf16[4,4,4,256]{3,2,1,0:T(4,128)(2,1)S(1)} collective-permute-done((bf16[4,4,4,256]{3,2,1,0:T(4,128)(2,1)S(1)}, bf16[4,4,4,256]{3,2,1,0:T(4,128)(2,1)S(1)}, u32[]{:S(2)}, u32[]{:S(2)}) %collective-permute-start.8) | collective-permute-done | bytes 32800 | tf_op jit(solution)/shard_map/ppermute | solution.py:379
  66.8 0.8 %shard_map.97 = bf16[17,4,4,256]{3,2,1,0:T(4,128)(2,1)} custom-call(f32[17,4,4,256]{3,2,1,0:T(4,128)S(1)} %get-tuple-element.33.own_ref, bf16[13,4,4,256]{3,2,1,0:T(4,128)(2,1)S(1)} %collective-permute-done.6.other_ref, bf16[4,4,4,256]{3,2,1,0:T(4,128)(2,1)S(1)} %shard_map.96.tail_ref, bf16[17,4,4,256]{3,2,1,0:T(4,128)(2,1)S(1)} %bitcast.17, ...), custom_call_target="tpu_custom_call" | custom-call | flops 400000000 | bytes 1048576 | tf_op jit(solution)/shard_map/pallas_call | solution.py:26
  (12 shorter events, 0.1 us)
Async XLA Ops:
  2.4 5.9 %copy-start.1 = (bf16[1,17,4,4,256]{4,3,2,1,0:T(4,128)(2,1)S(1)}, bf16[1,17,4,4,256]{4,3,2,1,0:T(4,128)(2,1)}, u32[]{:S(2)}) copy-start(bf16[1,17,4,4,256]{4,3,2,1,0:T(4,128)(2,1)} %param.9) | copy-start | bytes 417796
  2.4 9.3 %copy-start = (bf16[3,3,3,16,256]{4,3,2,1,0:T(8,128)(2,1)S(1)}, bf16[3,3,3,16,256]{4,3,2,1,0:T(8,128)(2,1)}, u32[]{:S(2)}) copy-start(bf16[3,3,3,16,256]{4,3,2,1,0:T(8,128)(2,1)} %w0_ref) | copy-start | bytes 663556
  2.4 28.3 %all-to-all-start = ((bf16[16,15,16,128]{3,2,1,0:T(8,128)(2,1)}), bf16[16,15,16,128]{3,2,1,0:T(8,128)(2,1)S(1)}, u32[]{:S(2)}, u32[]{:S(2)}) async-start(bf16[16,15,16,128]{3,2,1,0:T(8,128)(2,1)} %get-tuple-element.22), calls=%async_computation | async-start | bytes 1966080 | tf_op jit(solution)/shard_map/all_to_all | solution.py:311
  8.3 15.2 %collective-permute-start = (bf16[17,4,4,256]{3,2,1,0:T(4,128)(2,1)S(1)}, bf16[17,4,4,256]{3,2,1,0:T(4,128)(2,1)S(1)}, u32[]{:S(2)}, u32[]{:S(2)}) collective-permute-start(bf16[17,4,4,256]{3,2,1,0:T(4,128)(2,1)S(1)} %bitcast.12), channel_id=1, source_target_pairs={{0,2},{2,0},{1,3},{3,1},{4,6},{6,4},{5,7},{7,5},{8,10},{10,8},{9,1... | collective-permute-start | bytes 417800 | tf_op jit(solution)/shard_map/ppermute | solution.py:337
  10.3 17.9 %collective-permute-start.1 = (bf16[17,4,4,256]{3,2,1,0:T(4,128)(2,1)S(1)}, bf16[17,4,4,256]{3,2,1,0:T(4,128)(2,1)S(1)}, u32[]{:S(2)}, u32[]{:S(2)}) collective-permute-start(bf16[17,4,4,256]{3,2,1,0:T(4,128)(2,1)S(1)} %bitcast.13), channel_id=1, source_target_pairs={{3,4},{4,3},{7,8},{8,7},{11,12},{12,11},{19,20},{20,19},{23,24},{2... | collective-permute-start | bytes 417800 | tf_op jit(solution)/shard_map/ppermute | solution.py:340
  11.0 17.2 %collective-permute-start.2 = (bf16[17,4,4,256]{3,2,1,0:T(4,128)(2,1)S(1)}, bf16[17,4,4,256]{3,2,1,0:T(4,128)(2,1)S(1)}, u32[]{:S(2)}, u32[]{:S(2)}) collective-permute-start(bf16[17,4,4,256]{3,2,1,0:T(4,128)(2,1)S(1)} %bitcast.14), channel_id=1, source_target_pairs={{3,6},{4,1},{7,10},{8,5},{11,14},{12,9},{19,22},{20,17},{23,26},{2... | collective-permute-start | bytes 417800 | tf_op jit(solution)/shard_map/ppermute | solution.py:341
  11.7 22.2 %collective-permute-start.3 = (bf16[3,3,3,16,256]{4,3,2,1,0:T(8,128)(2,1)S(1)}, bf16[3,3,3,16,256]{4,3,2,1,0:T(8,128)(2,1)S(1)}, u32[]{:S(2)}, u32[]{:S(2)}) collective-permute-start(bf16[3,3,3,16,256]{4,3,2,1,0:T(8,128)(2,1)S(1)} %copy-done), channel_id=1, source_target_pairs={{0,4},{4,8},{8,12},{12,0},{1,5},{5,9},{9,13},{13,1},{2,6},{6,10},{... | collective-permute-start | bytes 663560 | tf_op jit(solution)/shard_map/ppermute | solution.py:336
  16.1 17.7 %collective-permute-start.4 = (bf16[3,3,3,16,256]{4,3,2,1,0:T(8,128)(2,1)S(1)}, bf16[3,3,3,16,256]{4,3,2,1,0:T(8,128)(2,1)S(1)}, u32[]{:S(2)}, u32[]{:S(2)}) collective-permute-start(bf16[3,3,3,16,256]{4,3,2,1,0:T(8,128)(2,1)S(1)} %copy-done), channel_id=1, source_target_pairs={{0,8},{4,12},{8,0},{12,4},{1,9},{5,13},{9,1},{13,5},{2,10},{6,14},... | collective-permute-start | bytes 663560 | tf_op jit(solution)/shard_map/ppermute | solution.py:336
  23.5 10.3 %collective-permute-start.5 = (bf16[3,3,3,16,256]{4,3,2,1,0:T(8,128)(2,1)S(1)}, bf16[3,3,3,16,256]{4,3,2,1,0:T(8,128)(2,1)S(1)}, u32[]{:S(2)}, u32[]{:S(2)}) collective-permute-start(bf16[3,3,3,16,256]{4,3,2,1,0:T(8,128)(2,1)S(1)} %copy-done), channel_id=1, source_target_pairs={{0,12},{4,0},{8,4},{12,8},{1,13},{5,1},{9,5},{13,9},{2,14},{6,2},{... | collective-permute-start | bytes 663560 | tf_op jit(solution)/shard_map/ppermute | solution.py:336
  28.3 2.4 %copy-start.2 = (f32[8,256]{1,0:T(8,128)S(1)}, f32[8,256]{1,0:T(8,128)}, u32[]{:S(2)}) copy-start(f32[8,256]{1,0:T(8,128)} %get-tuple-element.23.vec_ref) | copy-start | bytes 24580
  47.2 19.6 %collective-permute-start.6 = (bf16[13,4,4,256]{3,2,1,0:T(4,128)(2,1)S(1)}, bf16[13,4,4,256]{3,2,1,0:T(4,128)(2,1)S(1)}, u32[]{:S(2)}, u32[]{:S(2)}) collective-permute-start(bf16[13,4,4,256]{3,2,1,0:T(4,128)(2,1)S(1)} %get-tuple-element.34), channel_id=1, source_target_pairs={{0,2},{2,0},{1,3},{3,1},{4,6},{6,4},{5,7},{7,5},{8,10},{10,8},{9,1... | collective-permute-start | bytes 319496 | tf_op jit(solution)/shard_map/ppermute | solution.py:376
  50.6 5.8 %collective-permute-start.7 = (bf16[4,4,4,256]{3,2,1,0:T(4,128)(2,1)S(1)}, bf16[4,4,4,256]{3,2,1,0:T(4,128)(2,1)S(1)}, u32[]{:S(2)}, u32[]{:S(2)}) collective-permute-start(bf16[4,4,4,256]{3,2,1,0:T(4,128)(2,1)S(1)} %get-tuple-element.35), channel_id=1, source_target_pairs={{0,2},{2,0},{1,3},{3,1},{4,6},{6,4},{5,7},{7,5},{8,10},{10,8},{9,1... | collective-permute-start | bytes 98312 | tf_op jit(solution)/shard_map/ppermute | solution.py:375
  56.4 10.4 %collective-permute-start.8 = (bf16[4,4,4,256]{3,2,1,0:T(4,128)(2,1)S(1)}, bf16[4,4,4,256]{3,2,1,0:T(4,128)(2,1)S(1)}, u32[]{:S(2)}, u32[]{:S(2)}) collective-permute-start(bf16[4,4,4,256]{3,2,1,0:T(4,128)(2,1)S(1)} %shard_map.96.tail_ref), channel_id=1, source_target_pairs={{0,16},{16,32},{32,48},{48,64},{64,80},{80,96},{96,112},{112,128},... | collective-permute-start | bytes 98312 | tf_op jit(solution)/shard_map/ppermute | solution.py:379

commit v7 on v6

--- a/solution.py
+++ b/solution.py
@@ -61,10 +61,10 @@
     return value
 
 
-def group_stats(total, squares):
+def moments(total, squares):
     members = T * H * W * (C // GROUPS)
-    mean = group_sum(total) / members
-    spread = jnp.maximum(group_sum(squares) / members - mean * mean, 0.0)
+    mean = total / members
+    spread = jnp.maximum(squares / members - mean * mean, 0.0)
     return mean, lax.rsqrt(spread + epsilon)
 
 
@@ -100,14 +100,19 @@
         powers.append(squares)
     total = (totals[0] + totals[1]) + (totals[2] + totals[3])
     squares = (powers[0] + powers[1]) + (powers[2] + powers[3])
-    pieces = []
-    for value in (total, squares):
-        for piece in split3(jnp.sum(value, axis=0, keepdims=True)):
-            piece = piece.astype(F32)
-            pieces += [piece[:, 0:128], piece[:, 128:256]]
-    sums = jnp.concatenate(pieces + [jnp.zeros((4, 128), F32)], axis=0).astype(BF16)
-    for d in range(16):
-        out_ref[d, 14] = sums
+    line_sum = jnp.broadcast_to(jnp.sum(total, axis=0, keepdims=True), (8, C))
+    line_square = jnp.broadcast_to(jnp.sum(squares, axis=0, keepdims=True), (8, C))
+    spot = lanes((8, C)) & 7
+    sums = jnp.zeros((8, C), F32)
+    for start, value in ((0, group_sum(line_sum)), (3, group_sum(line_square))):
+        for i, piece in enumerate(split3(value)):
+            sums = jnp.where(spot == start + i, piece.astype(F32), sums)
+    halves = [sums[0:1, 0:128], sums[0:1, 128:256]]
+    extra = jnp.concatenate(
+        [pltpu.roll(sums[:, 0:128], 64, 1)[0:1], halves[0], pltpu.roll(sums[:, 128:256], 64, 1)[0:1], halves[1],
+         jnp.zeros((12, 128), F32)],
+        axis=0,
+    )
     row, col = rows((C, C)), lanes((C, C))
     source = 64 * ((col // 16) % 4) + 16 * (col // 64) + col % 16
     swapped = col ^ 64
@@ -129,14 +134,17 @@
                 a, b = block(first, m, 0, j), block(second, m, 1, j)
             else:
                 a = block(first, m - 9, 2, j)
-                b = block(second, m - 4, 2, j) if m < 13 else jnp.zeros((16, 128), F32)
+                b = block(second, m - 4, 2, j) if m < 13 else extra
             tile = jnp.where(left, a, b).astype(BF16)
             for x in range(4):
                 out_ref[4 * x + j, m] = tile
 
 
-def join_kernel(n_ref, latent_ref, other_ref, near_ref, far_ref, out_ref, shared_ref):
-    shared_ref[...] = jnp.full((1, C), n_ref[0], jnp.int32).astype(F32)
+def count_kernel(n_ref, out_ref):
+    out_ref[...] = jnp.full((1, C), n_ref[0], jnp.int32).astype(F32)
+
+
+def join_kernel(latent_ref, other_ref, near_ref, far_ref, out_ref):
     out_ref[0] = latent_ref[...]
     out_ref[1] = other_ref[...]
     straight = lax.axis_index("yl") == lax.axis_index("core")
@@ -162,14 +170,17 @@
             else:
                 last = jnp.where(left, nothing, w_ref[p, 4 + k])
             wm[k, 16 * p : 16 * p + 16, 128:256] = last
-    sums = sum(w_ref[p, 14].astype(F32) for p in range(16))
-    joined = lambda i: jnp.concatenate(
-        [sums[i + k : i + k + 1] + sums[i + k + 2 : i + k + 3] + sums[i + k + 4 : i + k + 5] for k in range(2)],
-        axis=1,
-    )
-    total = jnp.broadcast_to(joined(0), (8, C))
-    squares = jnp.broadcast_to(joined(6), (8, C))
-    mean, inv = group_stats(total, squares)
+    sums = sum(w_ref[p, 13].astype(F32) for p in range(16))[0:8]
+    turned = pltpu.roll(sums, 64, 1)
+    first = lanes((1, 128)) < 64
+    line = jnp.concatenate(
+        [jnp.where(first, turned[2 * i : 2 * i + 1], sums[2 * i + 1 : 2 * i + 2]) for i in range(2)], axis=1
+    )
+    line = jnp.broadcast_to(line, (8, C))
+    spot = lanes((8, C)) & 7
+    mean, inv = moments(
+        group_sum(jnp.where(spot < 3, line, 0.0)), group_sum(jnp.where((spot > 2) & (spot < 6), line, 0.0))
+    )
     scale = inv * vec_ref[0:1]
     mean, scale = mean[0:1], scale[0:1]
     shift = vec_ref[1:2]
@@ -227,8 +238,8 @@
     for k in range(9):
         wm[k, 192:256] = jnp.zeros((64, C), BF16)
     stats = st_ref[0] + st_ref[1] + st_ref[2] + st_ref[3]
-    mean, inv = group_stats(
-        jnp.broadcast_to(stats[0:1], (8, 128)), jnp.broadcast_to(stats[1:2], (8, 128))
+    mean, inv = moments(
+        group_sum(jnp.broadcast_to(stats[0:1], (8, 128))), group_sum(jnp.broadcast_to(stats[1:2], (8, 128)))
     )
     row, lane = rows((C, 128)), lanes((C, 128))
     mine = (row == 64 * ((lane // 16) % 4) + 16 * j + lane % 16).astype(F32)
@@ -318,7 +329,7 @@
     vectors = tuple(flat(v) for v in (gain_one, shift_one, gain_two, shift_two, bias))
     packed, vec = pl.pallas_call(
         pack_kernel,
-        out_shape=(sds((16, 15, 16, 128), BF16), sds((8, C), F32)),
+        out_shape=(sds((16, 14, 16, 128), BF16), sds((8, C), F32)),
         in_specs=[pl.BlockSpec(memory_space=pl.ANY)] * 7,
         out_specs=(whole(), whole()),
         scratch_shapes=[
@@ -331,23 +342,16 @@
         cost_estimate=cost(1),
     )(weight_one, source, *vectors)
     kernel_one = exchange(packed, COL)
-    kernel_two = [weight_two]
-    for step in range(1, 4):
-        kernel_two.append(lax.ppermute(weight_two, "x", [(x, (x + step) % 4) for x in range(4)]))
     other = lax.ppermute(source, "yl", [(0, 1), (1, 0)])
     near = [p for x in range(3) for p in ((4 * x + 3, 4 * x + 4), (4 * x + 4, 4 * x + 3))]
     far = [p for x in range(3) for p in ((4 * x + 3, 4 * x + 6), (4 * x + 4, 4 * x + 1))]
     near = lax.ppermute(source, COL, near)
     far = lax.ppermute(source, COL, far)
-    joined, shared = pl.pallas_call(
-        join_kernel,
-        out_shape=(sds((3, T, 4, 4, C), BF16), sds((1, C), F32)),
-        in_specs=[pl.BlockSpec(memory_space=pltpu.SMEM)] + [whole()] * 4,
-        out_specs=(whole(), whole()),
-        compiler_params=PARAMS,
-        cost_estimate=cost(1),
-    )(intersections, source, other, near, far)
+    joined = call(join_kernel, (source, other, near, far), sds((3, T, 4, 4, C), BF16), cost=cost(1))
     wide = lax.all_gather(joined, "core", axis=0, tiled=False)
+    kernel_two = [weight_two]
+    for step in range(1, 4):
+        kernel_two.append(lax.ppermute(weight_two, "x", [(x, (x + step) % 4) for x in range(4)]))
     hidden, stats = call(
         conv_one_kernel,
         (wide, kernel_one, vec),
@@ -355,8 +359,14 @@
         (pltpu.VMEM((4, T + 2, ROW, C), BF16), pltpu.VMEM((9, C, C), BF16)),
         cost=cost(4),
     )
-    stats, *kernel_two = lax.optimization_barrier((stats, *kernel_two))
+    intersections, stats = lax.optimization_barrier((intersections, stats))
     stats = exchange(stats, "x")
+    shared = pl.pallas_call(
+        count_kernel,
+        out_shape=sds((1, C), F32),
+        in_specs=[pl.BlockSpec(memory_space=pltpu.SMEM)],
+        out_specs=whole(),
+    )(intersections)
     home, away = call(
         conv_two_kernel,
         (hidden, stats, *kernel_two, vec),

time: 68.1 us -> 68.6 us (level)
  blocking collectives: 13.4 us -> 4.61 us
  waiting for transfers between devices: 11.4 us -> 15.3 us
  starting transfers between devices: 33.3 us -> 36.6 us
  Pallas kernels: 8.61 us -> 9.92 us
    all_to_all x1 -> x0, blocking collectives: 8.83 us -> none  [exchange(): return lax.all_to_all(array, axis, split_axis=0, concat_axis=0, tiled=True)]
    all_to_all x1 -> x2, waiting for transfers between devices: 0.01 us -> 5.3 us  [exchange(): return lax.all_to_all(array, axis, split_axis=0, concat_axis=0, tiled=True)]
    all_to_all x1 -> x2, starting transfers between devices: 5.92 us -> 9.18 us  [exchange(): return lax.all_to_all(array, axis, split_axis=0, concat_axis=0, tiled=True)]
    ppermute x1, waiting for transfers between devices: 5.87 us -> 4.66 us  [block(): received = lax.ppermute(tail, TILE, [(i, i + 1) for i in range(tiles - 1)])]
    pallas_call x5 -> x6, Pallas kernels: 6.24 us -> 6.94 us  [call(): pl.pallas_call(kernel, out_shape=out_shape, in_specs=[whole()] * len(inpu...]
  transfers between devices with their start and end apart: 10 -> 11, of which waited for: 3 -> 4; matrix products, arithmetic and copies ran while one was open for 0% -> 0% of each run, Pallas kernels for 5% -> 7%
where the time goes in v7:
time: 68.6 us; the launch traced here: 68 us
  starting transfers between devices  36.6 us (53%)
  waiting for transfers between devices  15.3 us (22%)
  Pallas kernels  9.92 us (14%)
  blocking collectives  4.61 us (7%)
  between operations  0.84 us (1%)
  local copies, waits for them, and re-layouts  0.7 us (1%)
    ppermute x3, starting transfers between devices, block(): lax.ppermute(weight_two, 'x', [(x, (x + step) % 4) for x in range(4)])  13.8 us
    all_to_all x2, starting transfers between devices, exchange(): return lax.all_to_all(array, axis, split_axis=0, concat_axis=0, tiled=True)  9.18 us
    pallas_call x6, Pallas kernels, call(): pl.pallas_call(kernel, out_shape=out_shape, in_specs=[whole()] * len(inpu...  6.94 us
    all_to_all x2, waiting for transfers between devices, exchange(): return lax.all_to_all(array, axis, split_axis=0, concat_axis=0, tiled=True)  5.3 us
    ppermute x1, waiting for transfers between devices, block(): received = lax.ppermute(tail, TILE, [(i, i + 1) for i in range(tiles - 1)])  4.66 us
    ppermute x1, starting transfers between devices, block(): received = lax.ppermute(tail, TILE, [(i, i + 1) for i in range(tiles - 1)])  4.49 us
    ppermute x1, starting transfers between devices, block(): rest = lax.ppermute(rest, 'yl', swap)  3.37 us
    ppermute x1, waiting for transfers between devices, block(): rest_tail = lax.ppermute(rest_tail, 'yl', swap)  3.33 us
  transfers between devices with their start and end apart: 11, of which 4 were waited for; matrix products, arithmetic and copies ran while one was open for 0% of the time, Pallas kernels for 7%

profile of v7, /device:TPU:264, one launch (start us, length us, event | category | flops | bytes accessed | tf_op | source)
XLA Modules:
  0.0 68.0 jit_solution(9166240796049876478)
XLA Ops:
  0.0 2.4 %shard_map.92 = (bf16[16,14,16,128]{3,2,1,0:T(8,128)(2,1)}, f32[8,256]{1,0:T(8,128)}) custom-call(bf16[3,3,3,16,256]{4,3,2,1,0:T(8,128)(2,1)} %w_hbm.1, bf16[17,4,4,256]{3,2,1,0:T(4,128)(2,1)} %bitcast.11, f32[1,256]{1,0:T(1,128)} %bitcast.18, f32[1,256]{1,0:T(1,128)} %bitcast.19, f32[1,256]{1,0:T(1,128)} %bitcast.20, f32[1,256]{1,0:T(1,128)} %bitcast.21, ...), custom_call_target="tpu_custom_call" | custom-call | flops 400000000 | bytes 1048576 | tf_op jit(solution)/shard_map/pallas_call | solution.py:330
  2.5 5.9 %all-to-all-start = ((bf16[16,14,16,128]{3,2,1,0:T(8,128)(2,1)}), bf16[16,14,16,128]{3,2,1,0:T(8,128)(2,1)S(1)}, u32[]{:S(2)}, u32[]{:S(2)}) async-start(bf16[16,14,16,128]{3,2,1,0:T(8,128)(2,1)} %get-tuple-element.16), calls=%async_computation | async-start | bytes 1835008 | tf_op jit(solution)/shard_map/all_to_all | solution.py:322
  8.4 2.0 %collective-permute-start = (bf16[17,4,4,256]{3,2,1,0:T(4,128)(2,1)S(1)}, bf16[17,4,4,256]{3,2,1,0:T(4,128)(2,1)S(1)}, u32[]{:S(2)}, u32[]{:S(2)}) collective-permute-start(bf16[17,4,4,256]{3,2,1,0:T(4,128)(2,1)S(1)} %bitcast.12), channel_id=1, source_target_pairs={{0,2},{2,0},{1,3},{3,1},{4,6},{6,4},{5,7},{7,5},{8,10},{10,8},{9,1... | collective-permute-start | bytes 417800 | tf_op jit(solution)/shard_map/ppermute | solution.py:345
  10.4 0.7 collective-permute-start.1
  11.1 0.7 collective-permute-start.2
  11.8 4.5 %collective-permute-start.3 = (bf16[3,3,3,16,256]{4,3,2,1,0:T(8,128)(2,1)S(1)}, bf16[3,3,3,16,256]{4,3,2,1,0:T(8,128)(2,1)S(1)}, u32[]{:S(2)}, u32[]{:S(2)}) collective-permute-start(bf16[3,3,3,16,256]{4,3,2,1,0:T(8,128)(2,1)S(1)} %copy-done), channel_id=1, source_target_pairs={{0,4},{4,8},{8,12},{12,0},{1,5},{5,9},{9,13},{13,1},{2,6},{6,10},{... | collective-permute-start | bytes 663560 | tf_op jit(solution)/shard_map/ppermute | solution.py:354
  16.2 4.6 %collective-permute-start.4 = (bf16[3,3,3,16,256]{4,3,2,1,0:T(8,128)(2,1)S(1)}, bf16[3,3,3,16,256]{4,3,2,1,0:T(8,128)(2,1)S(1)}, u32[]{:S(2)}, u32[]{:S(2)}) collective-permute-start(bf16[3,3,3,16,256]{4,3,2,1,0:T(8,128)(2,1)S(1)} %copy-done), channel_id=1, source_target_pairs={{0,8},{4,12},{8,0},{12,4},{1,9},{5,13},{9,1},{13,5},{2,10},{6,14},... | collective-permute-start | bytes 663560 | tf_op jit(solution)/shard_map/ppermute | solution.py:354
  20.8 2.0 %collective-permute-done.other_ref = bf16[17,4,4,256]{3,2,1,0:T(4,128)(2,1)S(1)} collective-permute-done((bf16[17,4,4,256]{3,2,1,0:T(4,128)(2,1)S(1)}, bf16[17,4,4,256]{3,2,1,0:T(4,128)(2,1)S(1)}, u32[]{:S(2)}, u32[]{:S(2)}) %collective-permute-start) | collective-permute-done | bytes 139296 | tf_op jit(solution)/shard_map/ppermute | solution.py:345
  22.8 4.7 %collective-permute-start.5 = (bf16[3,3,3,16,256]{4,3,2,1,0:T(8,128)(2,1)S(1)}, bf16[3,3,3,16,256]{4,3,2,1,0:T(8,128)(2,1)S(1)}, u32[]{:S(2)}, u32[]{:S(2)}) collective-permute-start(bf16[3,3,3,16,256]{4,3,2,1,0:T(8,128)(2,1)S(1)} %copy-done), channel_id=1, source_target_pairs={{0,12},{4,0},{8,4},{12,8},{1,13},{5,1},{9,5},{13,9},{2,14},{6,2},{... | collective-permute-start | bytes 663560 | tf_op jit(solution)/shard_map/ppermute | solution.py:354
  27.7 2.4 %all-gather = bf16[6,17,4,4,256]{4,3,2,1,0:T(4,128)(2,1)S(1)} all-gather(bf16[3,17,4,4,256]{4,3,2,1,0:T(4,128)(2,1)S(1)} %shard_map.91), channel_id=2, replica_groups=mesh['z'=8,'yh'=4,'x'=4,'yl'=2,'core'=2] {'core'}, dimensions={0}, use_global_device_ids=true | all-gather | bytes 1253376 | tf_op jit(solution)/shard_map/all_gather | solution.py:351
  30.1 3.8 %shard_map.93 = (bf16[4,17,24,128]{3,2,1,0:T(8,128)(2,1)S(1)}, f32[4,8,128]{2,1,0:T(8,128)}) custom-call(bf16[2,3,17,4,4,256]{5,4,3,2,1,0:T(4,128)(2,1)S(1)} %bitcast.9, bf16[16,14,16,128]{3,2,1,0:T(8,128)(2,1)S(1)} %all-to-all-done.w_ref, f32[8,256]{1,0:T(8,128)S(1)} %copy-done.3), custom_call_target="tpu_custom_call" | custom-call | flops 1600000000 | bytes 1048576 | tf_op jit(solution)/shard_map/pallas_call | solution.py:26
  33.9 3.3 %all-to-all-start.1 = ((f32[4,8,128]{2,1,0:T(8,128)}), f32[4,8,128]{2,1,0:T(8,128)S(1)}, u32[]{:S(2)}, u32[]{:S(2)}) async-start(f32[4,8,128]{2,1,0:T(8,128)} %get-tuple-element.20), calls=%async_computation.1 | async-start | bytes 32768 | tf_op jit(solution)/shard_map/all_to_all | solution.py:322
  37.2 5.3 %all-to-all-done.1.st_ref = f32[4,8,128]{2,1,0:T(8,128)S(1)} async-done(((f32[4,8,128]{2,1,0:T(8,128)}), f32[4,8,128]{2,1,0:T(8,128)S(1)}, u32[]{:S(2)}, u32[]{:S(2)}) %all-to-all-start.1) | async-done | bytes 16416 | tf_op jit(solution)/shard_map/all_to_all | solution.py:322
  42.5 2.3 %shard_map.94 = (f32[2,17,4,4,256]{4,3,2,1,0:T(4,128)S(1)}, bf16[2,17,4,4,256]{4,3,2,1,0:T(4,128)(2,1)S(1)}) custom-call(bf16[4,17,24,128]{3,2,1,0:T(8,128)(2,1)S(1)} %get-tuple-element.18.hid_ref, f32[4,8,128]{2,1,0:T(8,128)S(1)} %all-to-all-done.1.st_ref, bf16[3,3,3,16,256]{4,3,2,1,0:T(8,128)(2,1)S(1)} %copy-done, ...), custom_call_target="tpu_custom_call" | custom-call | flops 1600000000 | bytes 1048576 | tf_op jit(solution)/shard_map/pallas_call | solution.py:26
  44.7 2.2 %all-gather.1 = bf16[4,17,4,4,256]{4,3,2,1,0:T(4,128)(2,1)S(1)} all-gather(bf16[2,17,4,4,256]{4,3,2,1,0:T(4,128)(2,1)S(1)} %get-tuple-element.22), channel_id=3, replica_groups=mesh['z'=8,'yh'=4,'x'=4,'yl'=2,'core'=2] {'core'}, dimensions={0}, use_global_device_ids=true | all-gather | bytes 835584 | tf_op jit(solution)/shard_map/all_gather | solution.py:377
  46.9 0.1 shard_map.95
  47.0 3.4 %collective-permute-start.6 = (bf16[13,4,4,256]{3,2,1,0:T(4,128)(2,1)S(1)}, bf16[13,4,4,256]{3,2,1,0:T(4,128)(2,1)S(1)}, u32[]{:S(2)}, u32[]{:S(2)}) collective-permute-start(bf16[13,4,4,256]{3,2,1,0:T(4,128)(2,1)S(1)} %get-tuple-element.24), channel_id=1, source_target_pairs={{0,2},{2,0},{1,3},{3,1},{4,6},{6,4},{5,7},{7,5},{8,10},{10,8},{9,1... | collective-permute-start | bytes 319496 | tf_op jit(solution)/shard_map/ppermute | solution.py:386
  50.4 2.5 %collective-permute-start.7 = (bf16[4,4,4,256]{3,2,1,0:T(4,128)(2,1)S(1)}, bf16[4,4,4,256]{3,2,1,0:T(4,128)(2,1)S(1)}, u32[]{:S(2)}, u32[]{:S(2)}) collective-permute-start(bf16[4,4,4,256]{3,2,1,0:T(4,128)(2,1)S(1)} %get-tuple-element.25), channel_id=1, source_target_pairs={{0,2},{2,0},{1,3},{3,1},{4,6},{6,4},{5,7},{7,5},{8,10},{10,8},{9,1... | collective-permute-start | bytes 98312 | tf_op jit(solution)/shard_map/ppermute | solution.py:385
  52.9 3.3 %collective-permute-done.7.other_ref = bf16[4,4,4,256]{3,2,1,0:T(4,128)(2,1)S(1)} collective-permute-done((bf16[4,4,4,256]{3,2,1,0:T(4,128)(2,1)S(1)}, bf16[4,4,4,256]{3,2,1,0:T(4,128)(2,1)S(1)}, u32[]{:S(2)}, u32[]{:S(2)}) %collective-permute-start.7) | collective-permute-done | bytes 32800 | tf_op jit(solution)/shard_map/ppermute | solution.py:385
  56.2 4.5 %collective-permute-start.8 = (bf16[4,4,4,256]{3,2,1,0:T(4,128)(2,1)S(1)}, bf16[4,4,4,256]{3,2,1,0:T(4,128)(2,1)S(1)}, u32[]{:S(2)}, u32[]{:S(2)}) collective-permute-start(bf16[4,4,4,256]{3,2,1,0:T(4,128)(2,1)S(1)} %shard_map.96.tail_ref), channel_id=1, source_target_pairs={{0,16},{16,32},{32,48},{48,64},{64,80},{80,96},{96,112},{112,128},... | collective-permute-start | bytes 98312 | tf_op jit(solution)/shard_map/ppermute | solution.py:389
  61.4 0.6 shard_map.97.shared_ref
  61.9 4.7 %collective-permute-done.8.received_ref = bf16[4,4,4,256]{3,2,1,0:T(4,128)(2,1)S(1)} collective-permute-done((bf16[4,4,4,256]{3,2,1,0:T(4,128)(2,1)S(1)}, bf16[4,4,4,256]{3,2,1,0:T(4,128)(2,1)S(1)}, u32[]{:S(2)}, u32[]{:S(2)}) %collective-permute-start.8) | collective-permute-done | bytes 32800 | tf_op jit(solution)/shard_map/ppermute | solution.py:389
  66.6 0.7 copy-done.2
  67.3 0.8 %shard_map.98 = bf16[17,4,4,256]{3,2,1,0:T(4,128)(2,1)} custom-call(f32[17,4,4,256]{3,2,1,0:T(4,128)S(1)} %get-tuple-element.23.own_ref, bf16[13,4,4,256]{3,2,1,0:T(4,128)(2,1)S(1)} %collective-permute-done.6.other_ref, bf16[4,4,4,256]{3,2,1,0:T(4,128)(2,1)S(1)} %shard_map.96.tail_ref, bf16[17,4,4,256]{3,2,1,0:T(4,128)(2,1)S(1)} %bitcast.17, ...), custom_call_target="tpu_custom_call" | custom-call | flops 400000000 | bytes 1048576 | tf_op jit(solution)/shard_map/pallas_call | solution.py:26
  (16 shorter events, 0.1 us)
Async XLA Ops:
  2.4 5.9 %copy-start.1 = (bf16[1,17,4,4,256]{4,3,2,1,0:T(4,128)(2,1)S(1)}, bf16[1,17,4,4,256]{4,3,2,1,0:T(4,128)(2,1)}, u32[]{:S(2)}) copy-start(bf16[1,17,4,4,256]{4,3,2,1,0:T(4,128)(2,1)} %param.9) | copy-start | bytes 417796
  2.4 9.3 %copy-start = (bf16[3,3,3,16,256]{4,3,2,1,0:T(8,128)(2,1)S(1)}, bf16[3,3,3,16,256]{4,3,2,1,0:T(8,128)(2,1)}, u32[]{:S(2)}) copy-start(bf16[3,3,3,16,256]{4,3,2,1,0:T(8,128)(2,1)} %w0_ref.1) | copy-start | bytes 663556
  2.5 27.6 %all-to-all-start = ((bf16[16,14,16,128]{3,2,1,0:T(8,128)(2,1)}), bf16[16,14,16,128]{3,2,1,0:T(8,128)(2,1)S(1)}, u32[]{:S(2)}, u32[]{:S(2)}) async-start(bf16[16,14,16,128]{3,2,1,0:T(8,128)(2,1)} %get-tuple-element.16), calls=%async_computation | async-start | bytes 1835008 | tf_op jit(solution)/shard_map/all_to_all | solution.py:322
  8.4 14.5 %collective-permute-start = (bf16[17,4,4,256]{3,2,1,0:T(4,128)(2,1)S(1)}, bf16[17,4,4,256]{3,2,1,0:T(4,128)(2,1)S(1)}, u32[]{:S(2)}, u32[]{:S(2)}) collective-permute-start(bf16[17,4,4,256]{3,2,1,0:T(4,128)(2,1)S(1)} %bitcast.12), channel_id=1, source_target_pairs={{0,2},{2,0},{1,3},{3,1},{4,6},{6,4},{5,7},{7,5},{8,10},{10,8},{9,1... | collective-permute-start | bytes 417800 | tf_op jit(solution)/shard_map/ppermute | solution.py:345
  10.4 17.2 %collective-permute-start.1 = (bf16[17,4,4,256]{3,2,1,0:T(4,128)(2,1)S(1)}, bf16[17,4,4,256]{3,2,1,0:T(4,128)(2,1)S(1)}, u32[]{:S(2)}, u32[]{:S(2)}) collective-permute-start(bf16[17,4,4,256]{3,2,1,0:T(4,128)(2,1)S(1)} %bitcast.13), channel_id=1, source_target_pairs={{3,4},{4,3},{7,8},{8,7},{11,12},{12,11},{19,20},{20,19},{23,24},{2... | collective-permute-start | bytes 417800 | tf_op jit(solution)/shard_map/ppermute | solution.py:348
  11.1 16.5 %collective-permute-start.2 = (bf16[17,4,4,256]{3,2,1,0:T(4,128)(2,1)S(1)}, bf16[17,4,4,256]{3,2,1,0:T(4,128)(2,1)S(1)}, u32[]{:S(2)}, u32[]{:S(2)}) collective-permute-start(bf16[17,4,4,256]{3,2,1,0:T(4,128)(2,1)S(1)} %bitcast.14), channel_id=1, source_target_pairs={{3,6},{4,1},{7,10},{8,5},{11,14},{12,9},{19,22},{20,17},{23,26},{2... | collective-permute-start | bytes 417800 | tf_op jit(solution)/shard_map/ppermute | solution.py:349
  11.8 25.4 %collective-permute-start.3 = (bf16[3,3,3,16,256]{4,3,2,1,0:T(8,128)(2,1)S(1)}, bf16[3,3,3,16,256]{4,3,2,1,0:T(8,128)(2,1)S(1)}, u32[]{:S(2)}, u32[]{:S(2)}) collective-permute-start(bf16[3,3,3,16,256]{4,3,2,1,0:T(8,128)(2,1)S(1)} %copy-done), channel_id=1, source_target_pairs={{0,4},{4,8},{8,12},{12,0},{1,5},{5,9},{9,13},{13,1},{2,6},{6,10},{... | collective-permute-start | bytes 663560 | tf_op jit(solution)/shard_map/ppermute | solution.py:354
  16.2 20.9 %collective-permute-start.4 = (bf16[3,3,3,16,256]{4,3,2,1,0:T(8,128)(2,1)S(1)}, bf16[3,3,3,16,256]{4,3,2,1,0:T(8,128)(2,1)S(1)}, u32[]{:S(2)}, u32[]{:S(2)}) collective-permute-start(bf16[3,3,3,16,256]{4,3,2,1,0:T(8,128)(2,1)S(1)} %copy-done), channel_id=1, source_target_pairs={{0,8},{4,12},{8,0},{12,4},{1,9},{5,13},{9,1},{13,5},{2,10},{6,14},... | collective-permute-start | bytes 663560 | tf_op jit(solution)/shard_map/ppermute | solution.py:354
  22.8 14.3 %collective-permute-start.5 = (bf16[3,3,3,16,256]{4,3,2,1,0:T(8,128)(2,1)S(1)}, bf16[3,3,3,16,256]{4,3,2,1,0:T(8,128)(2,1)S(1)}, u32[]{:S(2)}, u32[]{:S(2)}) collective-permute-start(bf16[3,3,3,16,256]{4,3,2,1,0:T(8,128)(2,1)S(1)} %copy-done), channel_id=1, source_target_pairs={{0,12},{4,0},{8,4},{12,8},{1,13},{5,1},{9,5},{13,9},{2,14},{6,2},{... | collective-permute-start | bytes 663560 | tf_op jit(solution)/shard_map/ppermute | solution.py:354
  27.7 2.4 %copy-start.3 = (f32[8,256]{1,0:T(8,128)S(1)}, f32[8,256]{1,0:T(8,128)}, u32[]{:S(2)}) copy-start(f32[8,256]{1,0:T(8,128)} %get-tuple-element.17.vec_ref) | copy-start | bytes 24580
  33.9 8.6 %all-to-all-start.1 = ((f32[4,8,128]{2,1,0:T(8,128)}), f32[4,8,128]{2,1,0:T(8,128)S(1)}, u32[]{:S(2)}, u32[]{:S(2)}) async-start(f32[4,8,128]{2,1,0:T(8,128)} %get-tuple-element.20), calls=%async_computation.1 | async-start | bytes 32768 | tf_op jit(solution)/shard_map/all_to_all | solution.py:322
  47.0 19.6 %collective-permute-start.6 = (bf16[13,4,4,256]{3,2,1,0:T(4,128)(2,1)S(1)}, bf16[13,4,4,256]{3,2,1,0:T(4,128)(2,1)S(1)}, u32[]{:S(2)}, u32[]{:S(2)}) collective-permute-start(bf16[13,4,4,256]{3,2,1,0:T(4,128)(2,1)S(1)} %get-tuple-element.24), channel_id=1, source_target_pairs={{0,2},{2,0},{1,3},{3,1},{4,6},{6,4},{5,7},{7,5},{8,10},{10,8},{9,1... | collective-permute-start | bytes 319496 | tf_op jit(solution)/shard_map/ppermute | solution.py:386
  50.4 5.8 %collective-permute-start.7 = (bf16[4,4,4,256]{3,2,1,0:T(4,128)(2,1)S(1)}, bf16[4,4,4,256]{3,2,1,0:T(4,128)(2,1)S(1)}, u32[]{:S(2)}, u32[]{:S(2)}) collective-permute-start(bf16[4,4,4,256]{3,2,1,0:T(4,128)(2,1)S(1)} %get-tuple-element.25), channel_id=1, source_target_pairs={{0,2},{2,0},{1,3},{3,1},{4,6},{6,4},{5,7},{7,5},{8,10},{10,8},{9,1... | collective-permute-start | bytes 98312 | tf_op jit(solution)/shard_map/ppermute | solution.py:385
  56.2 10.4 %collective-permute-start.8 = (bf16[4,4,4,256]{3,2,1,0:T(4,128)(2,1)S(1)}, bf16[4,4,4,256]{3,2,1,0:T(4,128)(2,1)S(1)}, u32[]{:S(2)}, u32[]{:S(2)}) collective-permute-start(bf16[4,4,4,256]{3,2,1,0:T(4,128)(2,1)S(1)} %shard_map.96.tail_ref), channel_id=1, source_target_pairs={{0,16},{16,32},{32,48},{48,64},{64,80},{80,96},{96,112},{112,128},... | collective-permute-start | bytes 98312 | tf_op jit(solution)/shard_map/ppermute | solution.py:389
  66.6 0.7 %copy-start.2 = (f32[1,256]{1,0:T(1,128)S(1)}, f32[1,256]{1,0:T(1,128)}, u32[]{:S(2)}) copy-start(f32[1,256]{1,0:T(1,128)} %shard_map.97.shared_ref) | copy-start | bytes 3076

commit v8 on v7

--- a/solution.py
+++ b/solution.py
@@ -279,38 +279,30 @@
             target[d // 2, :, h] = y[:, 4 * d : 4 * d + 4].astype(target.dtype)
 
 
-def pair_kernel(home_ref, got_ref, own_ref, tail_ref, main_ref):
+def pair_kernel(home_ref, got_ref, latent_ref, vec_ref, own_ref, send_ref, straight_ref, across_ref):
     other = 1 - lax.axis_index("core")
     for t in range(T):
-        own_ref[t] = home_ref[0, t] + got_ref[other, 0, t].astype(F32)
+        own = home_ref[0, t] + got_ref[other, 0, t].astype(F32)
         send = (home_ref[1, t] + got_ref[other, 1, t].astype(F32)).astype(BF16)
-        if t < T - OVMAX:
-            main_ref[t] = send
-        else:
-            tail_ref[t - T + OVMAX] = send
-
-
-def decode(own, other, latent, bias):
-    return (latent.astype(F32) + (own + other.astype(F32) + bias)).astype(BF16)
-
-
-def tail_kernel(own_ref, other_ref, latent_ref, vec_ref, tail_ref):
-    for i in range(OVMAX):
-        t = T - OVMAX + i
-        tail_ref[i] = decode(own_ref[t], other_ref[i], latent_ref[t], vec_ref[4:5])
-
-
-def blend_kernel(own_ref, other_ref, tail_ref, latent_ref, vec_ref, shared_ref, received_ref, out_ref):
-    bias, shared = vec_ref[4:5], shared_ref[...]
+        own = latent_ref[t].astype(F32) + (own + vec_ref[4:5])
+        own_ref[t] = own
+        send_ref[t] = send
+        if t >= T - OVMAX:
+            straight_ref[t - T + OVMAX] = own.astype(BF16)
+            across_ref[t - T + OVMAX] = send
+
+
+def blend_kernel(own_ref, other_ref, shared_ref, straight_ref, across_ref, out_ref):
+    shared = shared_ref[...]
+    before = [
+        (straight_ref[i].astype(F32) + across_ref[i].astype(F32)).astype(BF16).astype(F32) for i in range(OVMAX)
+    ]
     for t in range(T):
-        if t >= T - OVMAX:
-            out_ref[t] = tail_ref[t - T + OVMAX]
-            continue
-        own = decode(own_ref[t], other_ref[t], latent_ref[t], bias)
+        own = (own_ref[t] + other_ref[t].astype(F32)).astype(BF16)
         if t < OVMAX:
-            other = received_ref[OVMAX - 1].astype(F32)
+            other = before[OVMAX - 1]
             for n in range(t + 2, OVMAX + 1):
-                other = jnp.where((shared == n)[None], received_ref[OVMAX - n + t].astype(F32), other)
+                other = jnp.where((shared == n)[None], before[OVMAX - n + t], other)
             share = jnp.full((1, C), t + 1, F32) / (shared + 1.0)
             head = own.astype(F32)
             mixed = share * head + (1.0 - share) * other
@@ -375,19 +367,18 @@
         cost=cost(4),
     )
     got = lax.all_gather(away, "core", axis=0, tiled=False)
-    own, rest_tail, rest = call(
+    own, send, straight, across = call(
         pair_kernel,
-        (home, got),
-        (sds((T, 4, 4, C), F32), sds((OVMAX, 4, 4, C), BF16), sds((T - OVMAX, 4, 4, C), BF16)),
+        (home, got, source, vec),
+        (sds((T, 4, 4, C), F32), sds((T, 4, 4, C), BF16), sds((OVMAX, 4, 4, C), BF16), sds((OVMAX, 4, 4, C), BF16)),
         cost=cost(1),
     )
-    swap = [(0, 1), (1, 0)]
-    rest_tail = lax.ppermute(rest_tail, "yl", swap)
-    rest = lax.ppermute(rest, "yl", swap)
-    tail = call(tail_kernel, (own, rest_tail, source, vec), sds((OVMAX, 4, 4, C), BF16), cost=cost(1))
     tiles = lax.axis_size(TILE)
-    received = lax.ppermute(tail, TILE, [(i, i + 1) for i in range(tiles - 1)])
-    out = call(blend_kernel, (own, rest, tail, source, vec, shared, received), sds((T, 4, 4, C), BF16), cost=cost(1))
+    rest = lax.ppermute(send, "yl", [(0, 1), (1, 0)])
+    straight = lax.ppermute(straight, TILE, [(i, i + 1) for i in range(tiles - 1)])
+    route = [(2 * i + yl, 2 * i + 3 - yl) for i in range(tiles - 1) for yl in range(2)]
+    across = lax.ppermute(across, ("z", "yh", "yl"), route)
+    out = call(blend_kernel, (own, rest, shared, straight, across), sds((T, 4, 4, C), BF16), cost=cost(1))
     return out[None]
 
 

time: 68.6 us -> 67.4 us (0.983)
  waiting for transfers between devices: 15.3 us -> 13.4 us
  starting transfers between devices: 36.6 us -> 38.1 us
    ppermute x3, waiting for transfers between devices: 8 us -> 6.03 us  [the longest x1 5.18 us: block(): across = lax.ppermute(across, ('z', 'yh', 'yl'), route)]
    ppermute x3, starting transfers between devices: 10.3 us -> 11.8 us  [the longest x1 4.49 us: block(): lax.ppermute(straight, TILE, [(i, i + 1) for i in range(tiles - 1)])]
    pallas_call x6 -> x5, Pallas kernels: 6.94 us -> 6.95 us  [call(): pl.pallas_call(kernel, out_shape=out_shape, in_specs=[whole()] * len(inpu...]
where the time goes in v8:
time: 67.4 us; the launch traced here: 66.8 us
  starting transfers between devices  38.1 us (57%)
  waiting for transfers between devices  13.4 us (20%)
  Pallas kernels  9.94 us (15%)
  blocking collectives  4.61 us (7%)
  between operations  0.84 us (1%)
    ppermute x3, starting transfers between devices, block(): lax.ppermute(weight_two, 'x', [(x, (x + step) % 4) for x in range(4)])  13.8 us
    all_to_all x2, starting transfers between devices, exchange(): return lax.all_to_all(array, axis, split_axis=0, concat_axis=0, tiled=True)  9.18 us
    pallas_call x5, Pallas kernels, call(): pl.pallas_call(kernel, out_shape=out_shape, in_specs=[whole()] * len(inpu...  6.95 us
    all_to_all x2, waiting for transfers between devices, exchange(): return lax.all_to_all(array, axis, split_axis=0, concat_axis=0, tiled=True)  5.3 us
    ppermute x1, waiting for transfers between devices, block(): across = lax.ppermute(across, ('z', 'yh', 'yl'), route)  5.18 us
    ppermute x1, starting transfers between devices, block(): lax.ppermute(straight, TILE, [(i, i + 1) for i in range(tiles - 1)])  4.49 us
    ppermute x1, starting transfers between devices, block(): across = lax.ppermute(across, ('z', 'yh', 'yl'), route)  3.91 us
    ppermute x1, starting transfers between devices, block(): rest = lax.ppermute(send, 'yl', [(0, 1), (1, 0)])  3.37 us
  transfers between devices with their start and end apart: 11, of which 4 were waited for; matrix products, arithmetic and copies ran while one was open for 0% of the time, Pallas kernels for 7%

profile of v8, /device:TPU:264, one launch (start us, length us, event | category | flops | bytes accessed | tf_op | source)
XLA Modules:
  0.0 66.8 jit_solution(3780892968582768979)
XLA Ops:
  0.0 2.4 %shard_map.92 = (bf16[16,14,16,128]{3,2,1,0:T(8,128)(2,1)}, f32[8,256]{1,0:T(8,128)}) custom-call(bf16[3,3,3,16,256]{4,3,2,1,0:T(8,128)(2,1)} %w_hbm.1, bf16[17,4,4,256]{3,2,1,0:T(4,128)(2,1)} %bitcast.11, f32[1,256]{1,0:T(1,128)} %bitcast.17, f32[1,256]{1,0:T(1,128)} %bitcast.18, f32[1,256]{1,0:T(1,128)} %bitcast.19, f32[1,256]{1,0:T(1,128)} %bitcast.20, ...), custom_call_target="tpu_custom_call" | custom-call | flops 400000000 | bytes 1048576 | tf_op jit(solution)/shard_map/pallas_call | solution.py:322
  2.4 0.0 copy-start
  2.5 5.9 %all-to-all-start = ((bf16[16,14,16,128]{3,2,1,0:T(8,128)(2,1)}), bf16[16,14,16,128]{3,2,1,0:T(8,128)(2,1)S(1)}, u32[]{:S(2)}, u32[]{:S(2)}) async-start(bf16[16,14,16,128]{3,2,1,0:T(8,128)(2,1)} %get-tuple-element.17), calls=%async_computation | async-start | bytes 1835008 | tf_op jit(solution)/shard_map/all_to_all | solution.py:314
  8.4 2.0 %collective-permute-start = (bf16[17,4,4,256]{3,2,1,0:T(4,128)(2,1)S(1)}, bf16[17,4,4,256]{3,2,1,0:T(4,128)(2,1)S(1)}, u32[]{:S(2)}, u32[]{:S(2)}) collective-permute-start(bf16[17,4,4,256]{3,2,1,0:T(4,128)(2,1)S(1)} %bitcast.12), channel_id=1, source_target_pairs={{0,2},{2,0},{1,3},{3,1},{4,6},{6,4},{5,7},{7,5},{8,10},{10,8},{9,1... | collective-permute-start | bytes 417800 | tf_op jit(solution)/shard_map/ppermute | solution.py:337
  10.4 0.7 %collective-permute-start.1 = (bf16[17,4,4,256]{3,2,1,0:T(4,128)(2,1)S(1)}, bf16[17,4,4,256]{3,2,1,0:T(4,128)(2,1)S(1)}, u32[]{:S(2)}, u32[]{:S(2)}) collective-permute-start(bf16[17,4,4,256]{3,2,1,0:T(4,128)(2,1)S(1)} %bitcast.13), channel_id=1, source_target_pairs={{3,4},{4,3},{7,8},{8,7},{11,12},{12,11},{19,20},{20,19},{23,24},{2... | collective-permute-start | bytes 417800 | tf_op jit(solution)/shard_map/ppermute | solution.py:340
  11.1 0.7 %collective-permute-start.2 = (bf16[17,4,4,256]{3,2,1,0:T(4,128)(2,1)S(1)}, bf16[17,4,4,256]{3,2,1,0:T(4,128)(2,1)S(1)}, u32[]{:S(2)}, u32[]{:S(2)}) collective-permute-start(bf16[17,4,4,256]{3,2,1,0:T(4,128)(2,1)S(1)} %bitcast.14), channel_id=1, source_target_pairs={{3,6},{4,1},{7,10},{8,5},{11,14},{12,9},{19,22},{20,17},{23,26},{2... | collective-permute-start | bytes 417800 | tf_op jit(solution)/shard_map/ppermute | solution.py:341
  11.8 4.5 %collective-permute-start.3 = (bf16[3,3,3,16,256]{4,3,2,1,0:T(8,128)(2,1)S(1)}, bf16[3,3,3,16,256]{4,3,2,1,0:T(8,128)(2,1)S(1)}, u32[]{:S(2)}, u32[]{:S(2)}) collective-permute-start(bf16[3,3,3,16,256]{4,3,2,1,0:T(8,128)(2,1)S(1)} %copy-done), channel_id=1, source_target_pairs={{0,4},{4,8},{8,12},{12,0},{1,5},{5,9},{9,13},{13,1},{2,6},{6,10},{... | collective-permute-start | bytes 663560 | tf_op jit(solution)/shard_map/ppermute | solution.py:346
  16.2 4.6 %collective-permute-start.4 = (bf16[3,3,3,16,256]{4,3,2,1,0:T(8,128)(2,1)S(1)}, bf16[3,3,3,16,256]{4,3,2,1,0:T(8,128)(2,1)S(1)}, u32[]{:S(2)}, u32[]{:S(2)}) collective-permute-start(bf16[3,3,3,16,256]{4,3,2,1,0:T(8,128)(2,1)S(1)} %copy-done), channel_id=1, source_target_pairs={{0,8},{4,12},{8,0},{12,4},{1,9},{5,13},{9,1},{13,5},{2,10},{6,14},... | collective-permute-start | bytes 663560 | tf_op jit(solution)/shard_map/ppermute | solution.py:346
  20.8 2.0 %collective-permute-done.other_ref = bf16[17,4,4,256]{3,2,1,0:T(4,128)(2,1)S(1)} collective-permute-done((bf16[17,4,4,256]{3,2,1,0:T(4,128)(2,1)S(1)}, bf16[17,4,4,256]{3,2,1,0:T(4,128)(2,1)S(1)}, u32[]{:S(2)}, u32[]{:S(2)}) %collective-permute-start) | collective-permute-done | bytes 139296 | tf_op jit(solution)/shard_map/ppermute | solution.py:337
  22.8 4.7 %collective-permute-start.5 = (bf16[3,3,3,16,256]{4,3,2,1,0:T(8,128)(2,1)S(1)}, bf16[3,3,3,16,256]{4,3,2,1,0:T(8,128)(2,1)S(1)}, u32[]{:S(2)}, u32[]{:S(2)}) collective-permute-start(bf16[3,3,3,16,256]{4,3,2,1,0:T(8,128)(2,1)S(1)} %copy-done), channel_id=1, source_target_pairs={{0,12},{4,0},{8,4},{12,8},{1,13},{5,1},{9,5},{13,9},{2,14},{6,2},{... | collective-permute-start | bytes 663560 | tf_op jit(solution)/shard_map/ppermute | solution.py:346
  27.7 2.4 %all-gather = bf16[6,17,4,4,256]{4,3,2,1,0:T(4,128)(2,1)S(1)} all-gather(bf16[3,17,4,4,256]{4,3,2,1,0:T(4,128)(2,1)S(1)} %shard_map.91), channel_id=2, replica_groups=mesh['z'=8,'yh'=4,'x'=4,'yl'=2,'core'=2] {'core'}, dimensions={0}, use_global_device_ids=true | all-gather | bytes 1253376 | tf_op jit(solution)/shard_map/all_gather | solution.py:343
  30.1 3.8 %shard_map.93 = (bf16[4,17,24,128]{3,2,1,0:T(8,128)(2,1)S(1)}, f32[4,8,128]{2,1,0:T(8,128)}) custom-call(bf16[2,3,17,4,4,256]{5,4,3,2,1,0:T(4,128)(2,1)S(1)} %bitcast.9, bf16[16,14,16,128]{3,2,1,0:T(8,128)(2,1)S(1)} %all-to-all-done.w_ref, f32[8,256]{1,0:T(8,128)S(1)} %copy-done.3), custom_call_target="tpu_custom_call" | custom-call | flops 1600000000 | bytes 1048576 | tf_op jit(solution)/shard_map/pallas_call | solution.py:26
  33.9 3.3 %all-to-all-start.1 = ((f32[4,8,128]{2,1,0:T(8,128)}), f32[4,8,128]{2,1,0:T(8,128)S(1)}, u32[]{:S(2)}, u32[]{:S(2)}) async-start(f32[4,8,128]{2,1,0:T(8,128)} %get-tuple-element.21), calls=%async_computation.1 | async-start | bytes 32768 | tf_op jit(solution)/shard_map/all_to_all | solution.py:314
  37.2 5.3 %all-to-all-done.1.st_ref = f32[4,8,128]{2,1,0:T(8,128)S(1)} async-done(((f32[4,8,128]{2,1,0:T(8,128)}), f32[4,8,128]{2,1,0:T(8,128)S(1)}, u32[]{:S(2)}, u32[]{:S(2)}) %all-to-all-start.1) | async-done | bytes 16416 | tf_op jit(solution)/shard_map/all_to_all | solution.py:314
  42.5 2.3 %shard_map.94 = (f32[2,17,4,4,256]{4,3,2,1,0:T(4,128)S(1)}, bf16[2,17,4,4,256]{4,3,2,1,0:T(4,128)(2,1)S(1)}) custom-call(bf16[4,17,24,128]{3,2,1,0:T(8,128)(2,1)S(1)} %get-tuple-element.19.hid_ref, f32[4,8,128]{2,1,0:T(8,128)S(1)} %all-to-all-done.1.st_ref, bf16[3,3,3,16,256]{4,3,2,1,0:T(8,128)(2,1)S(1)} %copy-done, ...), custom_call_target="tpu_custom_call" | custom-call | flops 1600000000 | bytes 1048576 | tf_op jit(solution)/shard_map/pallas_call | solution.py:26
  44.7 2.2 %all-gather.1 = bf16[4,17,4,4,256]{4,3,2,1,0:T(4,128)(2,1)S(1)} all-gather(bf16[2,17,4,4,256]{4,3,2,1,0:T(4,128)(2,1)S(1)} %get-tuple-element.23), channel_id=3, replica_groups=mesh['z'=8,'yh'=4,'x'=4,'yl'=2,'core'=2] {'core'}, dimensions={0}, use_global_device_ids=true | all-gather | bytes 835584 | tf_op jit(solution)/shard_map/all_gather | solution.py:369
  46.9 0.1 shard_map.95
  47.0 3.4 %collective-permute-start.6 = (bf16[17,4,4,256]{3,2,1,0:T(4,128)(2,1)S(1)}, bf16[17,4,4,256]{3,2,1,0:T(4,128)(2,1)S(1)}, u32[]{:S(2)}, u32[]{:S(2)}) collective-permute-start(bf16[17,4,4,256]{3,2,1,0:T(4,128)(2,1)S(1)} %get-tuple-element.25), channel_id=1, source_target_pairs={{0,2},{2,0},{1,3},{3,1},{4,6},{6,4},{5,7},{7,5},{8,10},{10,8},{9,1... | collective-permute-start | bytes 417800 | tf_op jit(solution)/shard_map/ppermute | solution.py:377
  50.4 4.5 %collective-permute-start.7 = (bf16[4,4,4,256]{3,2,1,0:T(4,128)(2,1)S(1)}, bf16[4,4,4,256]{3,2,1,0:T(4,128)(2,1)S(1)}, u32[]{:S(2)}, u32[]{:S(2)}) collective-permute-start(bf16[4,4,4,256]{3,2,1,0:T(4,128)(2,1)S(1)} %get-tuple-element.27), channel_id=1, source_target_pairs={{0,16},{16,32},{32,48},{48,64},{64,80},{80,96},{96,112},{112,128},... | collective-permute-start | bytes 98312 | tf_op jit(solution)/shard_map/ppermute | solution.py:378
  54.9 3.9 %collective-permute-start.8 = (bf16[4,4,4,256]{3,2,1,0:T(4,128)(2,1)S(1)}, bf16[4,4,4,256]{3,2,1,0:T(4,128)(2,1)S(1)}, u32[]{:S(2)}, u32[]{:S(2)}) collective-permute-start(bf16[4,4,4,256]{3,2,1,0:T(4,128)(2,1)S(1)} %get-tuple-element.28), channel_id=1, source_target_pairs={{0,18},{2,16},{16,34},{18,32},{32,50},{34,48},{48,66},{50,64},{64,... | collective-permute-start | bytes 98312 | tf_op jit(solution)/shard_map/ppermute | solution.py:380
  59.5 0.6 shard_map.96.shared_ref
  60.1 0.8 %collective-permute-done.7.straight_ref = bf16[4,4,4,256]{3,2,1,0:T(4,128)(2,1)S(1)} collective-permute-done((bf16[4,4,4,256]{3,2,1,0:T(4,128)(2,1)S(1)}, bf16[4,4,4,256]{3,2,1,0:T(4,128)(2,1)S(1)}, u32[]{:S(2)}, u32[]{:S(2)}) %collective-permute-start.7) | collective-permute-done | bytes 32800 | tf_op jit(solution)/shard_map/ppermute | solution.py:378
  60.9 5.2 %collective-permute-done.8.across_ref = bf16[4,4,4,256]{3,2,1,0:T(4,128)(2,1)S(1)} collective-permute-done((bf16[4,4,4,256]{3,2,1,0:T(4,128)(2,1)S(1)}, bf16[4,4,4,256]{3,2,1,0:T(4,128)(2,1)S(1)}, u32[]{:S(2)}, u32[]{:S(2)}) %collective-permute-start.8) | collective-permute-done | bytes 32800 | tf_op jit(solution)/shard_map/ppermute | solution.py:380
  66.1 0.8 %shard_map.97 = bf16[17,4,4,256]{3,2,1,0:T(4,128)(2,1)} custom-call(f32[17,4,4,256]{3,2,1,0:T(4,128)S(1)} %get-tuple-element.24.own_ref, bf16[17,4,4,256]{3,2,1,0:T(4,128)(2,1)S(1)} %collective-permute-done.6.other_ref, f32[1,256]{1,0:T(1,128)S(1)} %copy-done.2, bf16[4,4,4,256]{3,2,1,0:T(4,128)(2,1)S(1)} %collective-permute-done.7.straight_ref, ...), custom_call_target="tpu_custom_call" | custom-call | flops 400000000 | bytes 1048576 | tf_op jit(solution)/shard_map/pallas_call | solution.py:26
  (15 shorter events, 0.1 us)
Async XLA Ops:
  2.4 5.9 %copy-start.1 = (bf16[1,17,4,4,256]{4,3,2,1,0:T(4,128)(2,1)S(1)}, bf16[1,17,4,4,256]{4,3,2,1,0:T(4,128)(2,1)}, u32[]{:S(2)}) copy-start(bf16[1,17,4,4,256]{4,3,2,1,0:T(4,128)(2,1)} %param.9) | copy-start | bytes 417796
  2.4 9.3 %copy-start = (bf16[3,3,3,16,256]{4,3,2,1,0:T(8,128)(2,1)S(1)}, bf16[3,3,3,16,256]{4,3,2,1,0:T(8,128)(2,1)}, u32[]{:S(2)}) copy-start(bf16[3,3,3,16,256]{4,3,2,1,0:T(8,128)(2,1)} %w0_ref.1) | copy-start | bytes 663556
  2.5 27.6 %all-to-all-start = ((bf16[16,14,16,128]{3,2,1,0:T(8,128)(2,1)}), bf16[16,14,16,128]{3,2,1,0:T(8,128)(2,1)S(1)}, u32[]{:S(2)}, u32[]{:S(2)}) async-start(bf16[16,14,16,128]{3,2,1,0:T(8,128)(2,1)} %get-tuple-element.17), calls=%async_computation | async-start | bytes 1835008 | tf_op jit(solution)/shard_map/all_to_all | solution.py:314
  8.4 14.5 %collective-permute-start = (bf16[17,4,4,256]{3,2,1,0:T(4,128)(2,1)S(1)}, bf16[17,4,4,256]{3,2,1,0:T(4,128)(2,1)S(1)}, u32[]{:S(2)}, u32[]{:S(2)}) collective-permute-start(bf16[17,4,4,256]{3,2,1,0:T(4,128)(2,1)S(1)} %bitcast.12), channel_id=1, source_target_pairs={{0,2},{2,0},{1,3},{3,1},{4,6},{6,4},{5,7},{7,5},{8,10},{10,8},{9,1... | collective-permute-start | bytes 417800 | tf_op jit(solution)/shard_map/ppermute | solution.py:337
  10.4 17.2 %collective-permute-start.1 = (bf16[17,4,4,256]{3,2,1,0:T(4,128)(2,1)S(1)}, bf16[17,4,4,256]{3,2,1,0:T(4,128)(2,1)S(1)}, u32[]{:S(2)}, u32[]{:S(2)}) collective-permute-start(bf16[17,4,4,256]{3,2,1,0:T(4,128)(2,1)S(1)} %bitcast.13), channel_id=1, source_target_pairs={{3,4},{4,3},{7,8},{8,7},{11,12},{12,11},{19,20},{20,19},{23,24},{2... | collective-permute-start | bytes 417800 | tf_op jit(solution)/shard_map/ppermute | solution.py:340
  11.1 16.5 %collective-permute-start.2 = (bf16[17,4,4,256]{3,2,1,0:T(4,128)(2,1)S(1)}, bf16[17,4,4,256]{3,2,1,0:T(4,128)(2,1)S(1)}, u32[]{:S(2)}, u32[]{:S(2)}) collective-permute-start(bf16[17,4,4,256]{3,2,1,0:T(4,128)(2,1)S(1)} %bitcast.14), channel_id=1, source_target_pairs={{3,6},{4,1},{7,10},{8,5},{11,14},{12,9},{19,22},{20,17},{23,26},{2... | collective-permute-start | bytes 417800 | tf_op jit(solution)/shard_map/ppermute | solution.py:341
  11.8 25.4 %collective-permute-start.3 = (bf16[3,3,3,16,256]{4,3,2,1,0:T(8,128)(2,1)S(1)}, bf16[3,3,3,16,256]{4,3,2,1,0:T(8,128)(2,1)S(1)}, u32[]{:S(2)}, u32[]{:S(2)}) collective-permute-start(bf16[3,3,3,16,256]{4,3,2,1,0:T(8,128)(2,1)S(1)} %copy-done), channel_id=1, source_target_pairs={{0,4},{4,8},{8,12},{12,0},{1,5},{5,9},{9,13},{13,1},{2,6},{6,10},{... | collective-permute-start | bytes 663560 | tf_op jit(solution)/shard_map/ppermute | solution.py:346
  16.2 20.9 %collective-permute-start.4 = (bf16[3,3,3,16,256]{4,3,2,1,0:T(8,128)(2,1)S(1)}, bf16[3,3,3,16,256]{4,3,2,1,0:T(8,128)(2,1)S(1)}, u32[]{:S(2)}, u32[]{:S(2)}) collective-permute-start(bf16[3,3,3,16,256]{4,3,2,1,0:T(8,128)(2,1)S(1)} %copy-done), channel_id=1, source_target_pairs={{0,8},{4,12},{8,0},{12,4},{1,9},{5,13},{9,1},{13,5},{2,10},{6,14},... | collective-permute-start | bytes 663560 | tf_op jit(solution)/shard_map/ppermute | solution.py:346
  22.8 14.3 %collective-permute-start.5 = (bf16[3,3,3,16,256]{4,3,2,1,0:T(8,128)(2,1)S(1)}, bf16[3,3,3,16,256]{4,3,2,1,0:T(8,128)(2,1)S(1)}, u32[]{:S(2)}, u32[]{:S(2)}) collective-permute-start(bf16[3,3,3,16,256]{4,3,2,1,0:T(8,128)(2,1)S(1)} %copy-done), channel_id=1, source_target_pairs={{0,12},{4,0},{8,4},{12,8},{1,13},{5,1},{9,5},{13,9},{2,14},{6,2},{... | collective-permute-start | bytes 663560 | tf_op jit(solution)/shard_map/ppermute | solution.py:346
  27.7 2.4 %copy-start.3 = (f32[8,256]{1,0:T(8,128)S(1)}, f32[8,256]{1,0:T(8,128)}, u32[]{:S(2)}) copy-start(f32[8,256]{1,0:T(8,128)} %get-tuple-element.18.vec_ref) | copy-start | bytes 24580
  33.9 8.6 %all-to-all-start.1 = ((f32[4,8,128]{2,1,0:T(8,128)}), f32[4,8,128]{2,1,0:T(8,128)S(1)}, u32[]{:S(2)}, u32[]{:S(2)}) async-start(f32[4,8,128]{2,1,0:T(8,128)} %get-tuple-element.21), calls=%async_computation.1 | async-start | bytes 32768 | tf_op jit(solution)/shard_map/all_to_all | solution.py:314
  47.0 19.0 %collective-permute-start.6 = (bf16[17,4,4,256]{3,2,1,0:T(4,128)(2,1)S(1)}, bf16[17,4,4,256]{3,2,1,0:T(4,128)(2,1)S(1)}, u32[]{:S(2)}, u32[]{:S(2)}) collective-permute-start(bf16[17,4,4,256]{3,2,1,0:T(4,128)(2,1)S(1)} %get-tuple-element.25), channel_id=1, source_target_pairs={{0,2},{2,0},{1,3},{3,1},{4,6},{6,4},{5,7},{7,5},{8,10},{10,8},{9,1... | collective-permute-start | bytes 417800 | tf_op jit(solution)/shard_map/ppermute | solution.py:377
  50.4 10.5 %collective-permute-start.7 = (bf16[4,4,4,256]{3,2,1,0:T(4,128)(2,1)S(1)}, bf16[4,4,4,256]{3,2,1,0:T(4,128)(2,1)S(1)}, u32[]{:S(2)}, u32[]{:S(2)}) collective-permute-start(bf16[4,4,4,256]{3,2,1,0:T(4,128)(2,1)S(1)} %get-tuple-element.27), channel_id=1, source_target_pairs={{0,16},{16,32},{32,48},{48,64},{64,80},{80,96},{96,112},{112,128},... | collective-permute-start | bytes 98312 | tf_op jit(solution)/shard_map/ppermute | solution.py:378
  54.9 11.2 %collective-permute-start.8 = (bf16[4,4,4,256]{3,2,1,0:T(4,128)(2,1)S(1)}, bf16[4,4,4,256]{3,2,1,0:T(4,128)(2,1)S(1)}, u32[]{:S(2)}, u32[]{:S(2)}) collective-permute-start(bf16[4,4,4,256]{3,2,1,0:T(4,128)(2,1)S(1)} %get-tuple-element.28), channel_id=1, source_target_pairs={{0,18},{2,16},{16,34},{18,32},{32,50},{34,48},{48,66},{50,64},{64,... | collective-permute-start | bytes 98312 | tf_op jit(solution)/shard_map/ppermute | solution.py:380
  60.1 6.0 %copy-start.2 = (f32[1,256]{1,0:T(1,128)S(1)}, f32[1,256]{1,0:T(1,128)}, u32[]{:S(2)}) copy-start(f32[1,256]{1,0:T(1,128)} %shard_map.96.shared_ref) | copy-start | bytes 3076

commit v9 on v7

--- a/solution.py
+++ b/solution.py
@@ -190,7 +190,7 @@
     inside = (row >= jnp.where(me == 0, 4, 0)) & (row < jnp.where(me == 3, 20, ROW))
     act[:, 0:2] = jnp.zeros((4, 2, ROW, C), BF16)
 
-    def frame(t, _):
+    def frame(t):
         for h in range(4):
             lo = l_ref[0, 2, t, h].astype(F32)
             hi = l_ref[1, 2, t, h].astype(F32)
@@ -200,7 +200,8 @@
             act[h, t + 2] = jnp.where(inside, y, 0.0).astype(BF16)
         return 0
 
-    lax.fori_loop(0, T, frame, 0)
+    for t in range(T):
+        frame(t)
 
     size = T * ROW
     lane = lanes((size, 128))
@@ -253,7 +254,7 @@
     odd, upper = (place & 1) != 0, (place & 2) != 0
     act[:, 0:2] = jnp.zeros((4, 2, 16, C), BF16)
 
-    def frame(t, _):
+    def frame(t):
         for h in range(4):
             v = hid_ref[h, t].astype(F32)
             y = silu((v - mean) * scale + shift)
@@ -266,7 +267,8 @@
                 act[h, t + 2, :, at : at + 128] = jnp.concatenate([low, high], axis=0).astype(BF16)
         return 0
 
-    lax.fori_loop(0, T, frame, 0)
+    for t in range(T):
+        frame(t)
     for h in range(4):
         taps = [dh for dh in range(3) if 0 <= h + dh - 1 < 4]
         lhs = jnp.concatenate(

time: 68.6 us -> 67.1 us (0.978)
  Pallas kernels: 9.92 us -> 8.46 us
    pallas_call x6, Pallas kernels: 6.94 us -> 5.47 us  [call(): pl.pallas_call(kernel, out_shape=out_shape, in_specs=[whole()] * len(inpu...]
  transfers between devices with their start and end apart: 11 -> 11, of which waited for: 4 -> 4; matrix products, arithmetic and copies ran while one was open for 0% -> 0% of each run, Pallas kernels for 7% -> 5%
where the time goes in v9:
time: 67.1 us; the launch traced here: 66.6 us
  starting transfers between devices  36.6 us (55%)
  waiting for transfers between devices  15.3 us (23%)
  Pallas kernels  8.46 us (13%)
  blocking collectives  4.61 us (7%)
  between operations  0.84 us (1%)
  local copies, waits for them, and re-layouts  0.7 us (1%)
    ppermute x3, starting transfers between devices, block(): lax.ppermute(weight_two, 'x', [(x, (x + step) % 4) for x in range(4)])  13.8 us
    all_to_all x2, starting transfers between devices, exchange(): return lax.all_to_all(array, axis, split_axis=0, concat_axis=0, tiled=True)  9.18 us
    pallas_call x6, Pallas kernels, call(): pl.pallas_call(kernel, out_shape=out_shape, in_specs=[whole()] * len(inpu...  5.47 us
    all_to_all x2, waiting for transfers between devices, exchange(): return lax.all_to_all(array, axis, split_axis=0, concat_axis=0, tiled=True)  5.3 us
    ppermute x1, waiting for transfers between devices, block(): received = lax.ppermute(tail, TILE, [(i, i + 1) for i in range(tiles - 1)])  4.66 us
    ppermute x1, starting transfers between devices, block(): received = lax.ppermute(tail, TILE, [(i, i + 1) for i in range(tiles - 1)])  4.49 us
    ppermute x1, starting transfers between devices, block(): rest = lax.ppermute(rest, 'yl', swap)  3.38 us
    ppermute x1, waiting for transfers between devices, block(): rest_tail = lax.ppermute(rest_tail, 'yl', swap)  3.33 us
  transfers between devices with their start and end apart: 11, of which 4 were waited for; matrix products, arithmetic and copies ran while one was open for 0% of the time, Pallas kernels for 5%

profile of v9, /device:TPU:264, one launch (start us, length us, event | category | flops | bytes accessed | tf_op | source)
XLA Modules:
  0.0 66.6 jit_solution(7274194665661337880)
XLA Ops:
  0.0 2.4 %shard_map.92 = (bf16[16,14,16,128]{3,2,1,0:T(8,128)(2,1)}, f32[8,256]{1,0:T(8,128)}) custom-call(bf16[3,3,3,16,256]{4,3,2,1,0:T(8,128)(2,1)} %w_hbm.1, bf16[17,4,4,256]{3,2,1,0:T(4,128)(2,1)} %bitcast.11, f32[1,256]{1,0:T(1,128)} %bitcast.18, f32[1,256]{1,0:T(1,128)} %bitcast.19, f32[1,256]{1,0:T(1,128)} %bitcast.20, f32[1,256]{1,0:T(1,128)} %bitcast.21, ...), custom_call_target="tpu_custom_call" | custom-call | flops 400000000 | bytes 1048576 | tf_op jit(solution)/shard_map/pallas_call | solution.py:332
  2.5 5.9 %all-to-all-start = ((bf16[16,14,16,128]{3,2,1,0:T(8,128)(2,1)}), bf16[16,14,16,128]{3,2,1,0:T(8,128)(2,1)S(1)}, u32[]{:S(2)}, u32[]{:S(2)}) async-start(bf16[16,14,16,128]{3,2,1,0:T(8,128)(2,1)} %get-tuple-element.16), calls=%async_computation | async-start | bytes 1835008 | tf_op jit(solution)/shard_map/all_to_all | solution.py:324
  8.4 2.0 %collective-permute-start = (bf16[17,4,4,256]{3,2,1,0:T(4,128)(2,1)S(1)}, bf16[17,4,4,256]{3,2,1,0:T(4,128)(2,1)S(1)}, u32[]{:S(2)}, u32[]{:S(2)}) collective-permute-start(bf16[17,4,4,256]{3,2,1,0:T(4,128)(2,1)S(1)} %bitcast.12), channel_id=1, source_target_pairs={{0,2},{2,0},{1,3},{3,1},{4,6},{6,4},{5,7},{7,5},{8,10},{10,8},{9,1... | collective-permute-start | bytes 417800 | tf_op jit(solution)/shard_map/ppermute | solution.py:347
  10.4 0.7 %collective-permute-start.1 = (bf16[17,4,4,256]{3,2,1,0:T(4,128)(2,1)S(1)}, bf16[17,4,4,256]{3,2,1,0:T(4,128)(2,1)S(1)}, u32[]{:S(2)}, u32[]{:S(2)}) collective-permute-start(bf16[17,4,4,256]{3,2,1,0:T(4,128)(2,1)S(1)} %bitcast.13), channel_id=1, source_target_pairs={{3,4},{4,3},{7,8},{8,7},{11,12},{12,11},{19,20},{20,19},{23,24},{2... | collective-permute-start | bytes 417800 | tf_op jit(solution)/shard_map/ppermute | solution.py:350
  11.1 0.7 %collective-permute-start.2 = (bf16[17,4,4,256]{3,2,1,0:T(4,128)(2,1)S(1)}, bf16[17,4,4,256]{3,2,1,0:T(4,128)(2,1)S(1)}, u32[]{:S(2)}, u32[]{:S(2)}) collective-permute-start(bf16[17,4,4,256]{3,2,1,0:T(4,128)(2,1)S(1)} %bitcast.14), channel_id=1, source_target_pairs={{3,6},{4,1},{7,10},{8,5},{11,14},{12,9},{19,22},{20,17},{23,26},{2... | collective-permute-start | bytes 417800 | tf_op jit(solution)/shard_map/ppermute | solution.py:351
  11.8 4.5 %collective-permute-start.3 = (bf16[3,3,3,16,256]{4,3,2,1,0:T(8,128)(2,1)S(1)}, bf16[3,3,3,16,256]{4,3,2,1,0:T(8,128)(2,1)S(1)}, u32[]{:S(2)}, u32[]{:S(2)}) collective-permute-start(bf16[3,3,3,16,256]{4,3,2,1,0:T(8,128)(2,1)S(1)} %copy-done), channel_id=1, source_target_pairs={{0,4},{4,8},{8,12},{12,0},{1,5},{5,9},{9,13},{13,1},{2,6},{6,10},{... | collective-permute-start | bytes 663560 | tf_op jit(solution)/shard_map/ppermute | solution.py:356
  16.2 4.6 %collective-permute-start.4 = (bf16[3,3,3,16,256]{4,3,2,1,0:T(8,128)(2,1)S(1)}, bf16[3,3,3,16,256]{4,3,2,1,0:T(8,128)(2,1)S(1)}, u32[]{:S(2)}, u32[]{:S(2)}) collective-permute-start(bf16[3,3,3,16,256]{4,3,2,1,0:T(8,128)(2,1)S(1)} %copy-done), channel_id=1, source_target_pairs={{0,8},{4,12},{8,0},{12,4},{1,9},{5,13},{9,1},{13,5},{2,10},{6,14},... | collective-permute-start | bytes 663560 | tf_op jit(solution)/shard_map/ppermute | solution.py:356
  20.8 2.0 %collective-permute-done.other_ref = bf16[17,4,4,256]{3,2,1,0:T(4,128)(2,1)S(1)} collective-permute-done((bf16[17,4,4,256]{3,2,1,0:T(4,128)(2,1)S(1)}, bf16[17,4,4,256]{3,2,1,0:T(4,128)(2,1)S(1)}, u32[]{:S(2)}, u32[]{:S(2)}) %collective-permute-start) | collective-permute-done | bytes 139296 | tf_op jit(solution)/shard_map/ppermute | solution.py:347
  22.8 4.7 %collective-permute-start.5 = (bf16[3,3,3,16,256]{4,3,2,1,0:T(8,128)(2,1)S(1)}, bf16[3,3,3,16,256]{4,3,2,1,0:T(8,128)(2,1)S(1)}, u32[]{:S(2)}, u32[]{:S(2)}) collective-permute-start(bf16[3,3,3,16,256]{4,3,2,1,0:T(8,128)(2,1)S(1)} %copy-done), channel_id=1, source_target_pairs={{0,12},{4,0},{8,4},{12,8},{1,13},{5,1},{9,5},{13,9},{2,14},{6,2},{... | collective-permute-start | bytes 663560 | tf_op jit(solution)/shard_map/ppermute | solution.py:356
  27.7 2.4 %all-gather = bf16[6,17,4,4,256]{4,3,2,1,0:T(4,128)(2,1)S(1)} all-gather(bf16[3,17,4,4,256]{4,3,2,1,0:T(4,128)(2,1)S(1)} %shard_map.91), channel_id=2, replica_groups=mesh['z'=8,'yh'=4,'x'=4,'yl'=2,'core'=2] {'core'}, dimensions={0}, use_global_device_ids=true | all-gather | bytes 1253376 | tf_op jit(solution)/shard_map/all_gather | solution.py:353
  30.1 3.0 %shard_map.93 = (bf16[4,17,24,128]{3,2,1,0:T(8,128)(2,1)S(1)}, f32[4,8,128]{2,1,0:T(8,128)}) custom-call(bf16[2,3,17,4,4,256]{5,4,3,2,1,0:T(4,128)(2,1)S(1)} %bitcast.9, bf16[16,14,16,128]{3,2,1,0:T(8,128)(2,1)S(1)} %all-to-all-done.w_ref, f32[8,256]{1,0:T(8,128)S(1)} %copy-done.3), custom_call_target="tpu_custom_call" | custom-call | flops 1600000000 | bytes 1048576 | tf_op jit(solution)/shard_map/pallas_call | solution.py:26
  33.1 3.3 %all-to-all-start.1 = ((f32[4,8,128]{2,1,0:T(8,128)}), f32[4,8,128]{2,1,0:T(8,128)S(1)}, u32[]{:S(2)}, u32[]{:S(2)}) async-start(f32[4,8,128]{2,1,0:T(8,128)} %get-tuple-element.20), calls=%async_computation.1 | async-start | bytes 32768 | tf_op jit(solution)/shard_map/all_to_all | solution.py:324
  36.4 5.3 %all-to-all-done.1.st_ref = f32[4,8,128]{2,1,0:T(8,128)S(1)} async-done(((f32[4,8,128]{2,1,0:T(8,128)}), f32[4,8,128]{2,1,0:T(8,128)S(1)}, u32[]{:S(2)}, u32[]{:S(2)}) %all-to-all-start.1) | async-done | bytes 16416 | tf_op jit(solution)/shard_map/all_to_all | solution.py:324
  41.7 1.6 %shard_map.94 = (f32[2,17,4,4,256]{4,3,2,1,0:T(4,128)S(1)}, bf16[2,17,4,4,256]{4,3,2,1,0:T(4,128)(2,1)S(1)}) custom-call(bf16[4,17,24,128]{3,2,1,0:T(8,128)(2,1)S(1)} %get-tuple-element.18.hid_ref, f32[4,8,128]{2,1,0:T(8,128)S(1)} %all-to-all-done.1.st_ref, bf16[3,3,3,16,256]{4,3,2,1,0:T(8,128)(2,1)S(1)} %copy-done, ...), custom_call_target="tpu_custom_call" | custom-call | flops 1600000000 | bytes 1048576 | tf_op jit(solution)/shard_map/pallas_call | solution.py:26
  43.3 2.2 %all-gather.1 = bf16[4,17,4,4,256]{4,3,2,1,0:T(4,128)(2,1)S(1)} all-gather(bf16[2,17,4,4,256]{4,3,2,1,0:T(4,128)(2,1)S(1)} %get-tuple-element.22), channel_id=3, replica_groups=mesh['z'=8,'yh'=4,'x'=4,'yl'=2,'core'=2] {'core'}, dimensions={0}, use_global_device_ids=true | all-gather | bytes 835584 | tf_op jit(solution)/shard_map/all_gather | solution.py:379
  45.5 0.1 shard_map.95
  45.5 3.4 %collective-permute-start.6 = (bf16[13,4,4,256]{3,2,1,0:T(4,128)(2,1)S(1)}, bf16[13,4,4,256]{3,2,1,0:T(4,128)(2,1)S(1)}, u32[]{:S(2)}, u32[]{:S(2)}) collective-permute-start(bf16[13,4,4,256]{3,2,1,0:T(4,128)(2,1)S(1)} %get-tuple-element.24), channel_id=1, source_target_pairs={{0,2},{2,0},{1,3},{3,1},{4,6},{6,4},{5,7},{7,5},{8,10},{10,8},{9,1... | collective-permute-start | bytes 319496 | tf_op jit(solution)/shard_map/ppermute | solution.py:388
  48.9 2.5 %collective-permute-start.7 = (bf16[4,4,4,256]{3,2,1,0:T(4,128)(2,1)S(1)}, bf16[4,4,4,256]{3,2,1,0:T(4,128)(2,1)S(1)}, u32[]{:S(2)}, u32[]{:S(2)}) collective-permute-start(bf16[4,4,4,256]{3,2,1,0:T(4,128)(2,1)S(1)} %get-tuple-element.25), channel_id=1, source_target_pairs={{0,2},{2,0},{1,3},{3,1},{4,6},{6,4},{5,7},{7,5},{8,10},{10,8},{9,1... | collective-permute-start | bytes 98312 | tf_op jit(solution)/shard_map/ppermute | solution.py:387
  51.4 3.3 %collective-permute-done.7.other_ref = bf16[4,4,4,256]{3,2,1,0:T(4,128)(2,1)S(1)} collective-permute-done((bf16[4,4,4,256]{3,2,1,0:T(4,128)(2,1)S(1)}, bf16[4,4,4,256]{3,2,1,0:T(4,128)(2,1)S(1)}, u32[]{:S(2)}, u32[]{:S(2)}) %collective-permute-start.7) | collective-permute-done | bytes 32800 | tf_op jit(solution)/shard_map/ppermute | solution.py:387
  54.8 4.5 %collective-permute-start.8 = (bf16[4,4,4,256]{3,2,1,0:T(4,128)(2,1)S(1)}, bf16[4,4,4,256]{3,2,1,0:T(4,128)(2,1)S(1)}, u32[]{:S(2)}, u32[]{:S(2)}) collective-permute-start(bf16[4,4,4,256]{3,2,1,0:T(4,128)(2,1)S(1)} %shard_map.96.tail_ref), channel_id=1, source_target_pairs={{0,16},{16,32},{32,48},{48,64},{64,80},{80,96},{96,112},{112,128},... | collective-permute-start | bytes 98312 | tf_op jit(solution)/shard_map/ppermute | solution.py:391
  59.9 0.6 shard_map.97.shared_ref
  60.5 4.7 %collective-permute-done.8.received_ref = bf16[4,4,4,256]{3,2,1,0:T(4,128)(2,1)S(1)} collective-permute-done((bf16[4,4,4,256]{3,2,1,0:T(4,128)(2,1)S(1)}, bf16[4,4,4,256]{3,2,1,0:T(4,128)(2,1)S(1)}, u32[]{:S(2)}, u32[]{:S(2)}) %collective-permute-start.8) | collective-permute-done | bytes 32800 | tf_op jit(solution)/shard_map/ppermute | solution.py:391
  65.1 0.7 %copy-done.2 = f32[1,256]{1,0:T(1,128)S(1)} copy-done((f32[1,256]{1,0:T(1,128)S(1)}, f32[1,256]{1,0:T(1,128)}, u32[]{:S(2)}) %copy-start.2) | copy-done | bytes 1048
  65.8 0.8 %shard_map.98 = bf16[17,4,4,256]{3,2,1,0:T(4,128)(2,1)} custom-call(f32[17,4,4,256]{3,2,1,0:T(4,128)S(1)} %get-tuple-element.23.own_ref, bf16[13,4,4,256]{3,2,1,0:T(4,128)(2,1)S(1)} %collective-permute-done.6.other_ref, bf16[4,4,4,256]{3,2,1,0:T(4,128)(2,1)S(1)} %shard_map.96.tail_ref, bf16[17,4,4,256]{3,2,1,0:T(4,128)(2,1)S(1)} %bitcast.17, ...), custom_call_target="tpu_custom_call" | custom-call | flops 400000000 | bytes 1048576 | tf_op jit(solution)/shard_map/pallas_call | solution.py:26
  (16 shorter events, 0.1 us)
Async XLA Ops:
  2.4 5.9 %copy-start.1 = (bf16[1,17,4,4,256]{4,3,2,1,0:T(4,128)(2,1)S(1)}, bf16[1,17,4,4,256]{4,3,2,1,0:T(4,128)(2,1)}, u32[]{:S(2)}) copy-start(bf16[1,17,4,4,256]{4,3,2,1,0:T(4,128)(2,1)} %param.9) | copy-start | bytes 417796
  2.4 9.3 %copy-start = (bf16[3,3,3,16,256]{4,3,2,1,0:T(8,128)(2,1)S(1)}, bf16[3,3,3,16,256]{4,3,2,1,0:T(8,128)(2,1)}, u32[]{:S(2)}) copy-start(bf16[3,3,3,16,256]{4,3,2,1,0:T(8,128)(2,1)} %w0_ref.1) | copy-start | bytes 663556
  2.5 27.6 %all-to-all-start = ((bf16[16,14,16,128]{3,2,1,0:T(8,128)(2,1)}), bf16[16,14,16,128]{3,2,1,0:T(8,128)(2,1)S(1)}, u32[]{:S(2)}, u32[]{:S(2)}) async-start(bf16[16,14,16,128]{3,2,1,0:T(8,128)(2,1)} %get-tuple-element.16), calls=%async_computation | async-start | bytes 1835008 | tf_op jit(solution)/shard_map/all_to_all | solution.py:324
  8.4 14.5 %collective-permute-start = (bf16[17,4,4,256]{3,2,1,0:T(4,128)(2,1)S(1)}, bf16[17,4,4,256]{3,2,1,0:T(4,128)(2,1)S(1)}, u32[]{:S(2)}, u32[]{:S(2)}) collective-permute-start(bf16[17,4,4,256]{3,2,1,0:T(4,128)(2,1)S(1)} %bitcast.12), channel_id=1, source_target_pairs={{0,2},{2,0},{1,3},{3,1},{4,6},{6,4},{5,7},{7,5},{8,10},{10,8},{9,1... | collective-permute-start | bytes 417800 | tf_op jit(solution)/shard_map/ppermute | solution.py:347
  10.4 17.2 %collective-permute-start.1 = (bf16[17,4,4,256]{3,2,1,0:T(4,128)(2,1)S(1)}, bf16[17,4,4,256]{3,2,1,0:T(4,128)(2,1)S(1)}, u32[]{:S(2)}, u32[]{:S(2)}) collective-permute-start(bf16[17,4,4,256]{3,2,1,0:T(4,128)(2,1)S(1)} %bitcast.13), channel_id=1, source_target_pairs={{3,4},{4,3},{7,8},{8,7},{11,12},{12,11},{19,20},{20,19},{23,24},{2... | collective-permute-start | bytes 417800 | tf_op jit(solution)/shard_map/ppermute | solution.py:350
  11.1 16.5 %collective-permute-start.2 = (bf16[17,4,4,256]{3,2,1,0:T(4,128)(2,1)S(1)}, bf16[17,4,4,256]{3,2,1,0:T(4,128)(2,1)S(1)}, u32[]{:S(2)}, u32[]{:S(2)}) collective-permute-start(bf16[17,4,4,256]{3,2,1,0:T(4,128)(2,1)S(1)} %bitcast.14), channel_id=1, source_target_pairs={{3,6},{4,1},{7,10},{8,5},{11,14},{12,9},{19,22},{20,17},{23,26},{2... | collective-permute-start | bytes 417800 | tf_op jit(solution)/shard_map/ppermute | solution.py:351
  11.8 24.6 %collective-permute-start.3 = (bf16[3,3,3,16,256]{4,3,2,1,0:T(8,128)(2,1)S(1)}, bf16[3,3,3,16,256]{4,3,2,1,0:T(8,128)(2,1)S(1)}, u32[]{:S(2)}, u32[]{:S(2)}) collective-permute-start(bf16[3,3,3,16,256]{4,3,2,1,0:T(8,128)(2,1)S(1)} %copy-done), channel_id=1, source_target_pairs={{0,4},{4,8},{8,12},{12,0},{1,5},{5,9},{9,13},{13,1},{2,6},{6,10},{... | collective-permute-start | bytes 663560 | tf_op jit(solution)/shard_map/ppermute | solution.py:356
  16.2 20.2 %collective-permute-start.4 = (bf16[3,3,3,16,256]{4,3,2,1,0:T(8,128)(2,1)S(1)}, bf16[3,3,3,16,256]{4,3,2,1,0:T(8,128)(2,1)S(1)}, u32[]{:S(2)}, u32[]{:S(2)}) collective-permute-start(bf16[3,3,3,16,256]{4,3,2,1,0:T(8,128)(2,1)S(1)} %copy-done), channel_id=1, source_target_pairs={{0,8},{4,12},{8,0},{12,4},{1,9},{5,13},{9,1},{13,5},{2,10},{6,14},... | collective-permute-start | bytes 663560 | tf_op jit(solution)/shard_map/ppermute | solution.py:356
  22.8 13.6 %collective-permute-start.5 = (bf16[3,3,3,16,256]{4,3,2,1,0:T(8,128)(2,1)S(1)}, bf16[3,3,3,16,256]{4,3,2,1,0:T(8,128)(2,1)S(1)}, u32[]{:S(2)}, u32[]{:S(2)}) collective-permute-start(bf16[3,3,3,16,256]{4,3,2,1,0:T(8,128)(2,1)S(1)} %copy-done), channel_id=1, source_target_pairs={{0,12},{4,0},{8,4},{12,8},{1,13},{5,1},{9,5},{13,9},{2,14},{6,2},{... | collective-permute-start | bytes 663560 | tf_op jit(solution)/shard_map/ppermute | solution.py:356
  27.7 2.4 %copy-start.3 = (f32[8,256]{1,0:T(8,128)S(1)}, f32[8,256]{1,0:T(8,128)}, u32[]{:S(2)}) copy-start(f32[8,256]{1,0:T(8,128)} %get-tuple-element.17.vec_ref) | copy-start | bytes 24580
  33.1 8.6 %all-to-all-start.1 = ((f32[4,8,128]{2,1,0:T(8,128)}), f32[4,8,128]{2,1,0:T(8,128)S(1)}, u32[]{:S(2)}, u32[]{:S(2)}) async-start(f32[4,8,128]{2,1,0:T(8,128)} %get-tuple-element.20), calls=%async_computation.1 | async-start | bytes 32768 | tf_op jit(solution)/shard_map/all_to_all | solution.py:324
  45.5 19.6 %collective-permute-start.6 = (bf16[13,4,4,256]{3,2,1,0:T(4,128)(2,1)S(1)}, bf16[13,4,4,256]{3,2,1,0:T(4,128)(2,1)S(1)}, u32[]{:S(2)}, u32[]{:S(2)}) collective-permute-start(bf16[13,4,4,256]{3,2,1,0:T(4,128)(2,1)S(1)} %get-tuple-element.24), channel_id=1, source_target_pairs={{0,2},{2,0},{1,3},{3,1},{4,6},{6,4},{5,7},{7,5},{8,10},{10,8},{9,1... | collective-permute-start | bytes 319496 | tf_op jit(solution)/shard_map/ppermute | solution.py:388
  48.9 5.8 %collective-permute-start.7 = (bf16[4,4,4,256]{3,2,1,0:T(4,128)(2,1)S(1)}, bf16[4,4,4,256]{3,2,1,0:T(4,128)(2,1)S(1)}, u32[]{:S(2)}, u32[]{:S(2)}) collective-permute-start(bf16[4,4,4,256]{3,2,1,0:T(4,128)(2,1)S(1)} %get-tuple-element.25), channel_id=1, source_target_pairs={{0,2},{2,0},{1,3},{3,1},{4,6},{6,4},{5,7},{7,5},{8,10},{10,8},{9,1... | collective-permute-start | bytes 98312 | tf_op jit(solution)/shard_map/ppermute | solution.py:387
  54.8 10.4 %collective-permute-start.8 = (bf16[4,4,4,256]{3,2,1,0:T(4,128)(2,1)S(1)}, bf16[4,4,4,256]{3,2,1,0:T(4,128)(2,1)S(1)}, u32[]{:S(2)}, u32[]{:S(2)}) collective-permute-start(bf16[4,4,4,256]{3,2,1,0:T(4,128)(2,1)S(1)} %shard_map.96.tail_ref), channel_id=1, source_target_pairs={{0,16},{16,32},{32,48},{48,64},{64,80},{80,96},{96,112},{112,128},... | collective-permute-start | bytes 98312 | tf_op jit(solution)/shard_map/ppermute | solution.py:391
  65.1 0.7 %copy-start.2 = (f32[1,256]{1,0:T(1,128)S(1)}, f32[1,256]{1,0:T(1,128)}, u32[]{:S(2)}) copy-start(f32[1,256]{1,0:T(1,128)} %shard_map.97.shared_ref) | copy-start | bytes 3076
